TPU v7x, 256 devices: a whole 4x4x8 slice. The times are simulated.
256 devices in a mesh: shot: 64 (over y, z, core), grp: 4 (over x).
Axes of the slice: x: 4, y: 4, z: 8, core: 2. Of those that a mesh axis runs over, the one named last changes fastest.
Arguments:
- offsets: bfloat16 [49152, 32, 512], P(('shot', 'grp')), may hold values from -500 to 500
- slant_weights: bfloat16 [64, 32], replicated, may hold values from -1 to 1
- live: int32 [49152, 64], P(('shot', 'grp')), may hold values from 0 to 1, as said below
- block_tile: int32 [24576, 1], P(('shot', 'grp')), may hold values from 0 to 63; in each aligned block of 96 rows (0 to 95, 96 to 191, ...) at most 2 rows name the same one
- image_slot: int32 [24576], P(('shot', 'grp')), may hold values from 0 to 15
Outputs:
- image: bfloat16 [1024, 128, 512], P(('shot', 'grp'))
Inputs may be any that keep to these rules, and one draw needn't show every extreme that they name: Each position's live angles are 0 up to a cutoff minus 1, the cutoff at least 16; the first position of every 192 positions keeps all 64 angles. `block_tile`: among the 96 blocks of one device no tile is named more than 2 times.
All inputs are finite; a program needn't handle non-finite values.
Results may differ from a plain program's by a relative error of at most 0.0049.
Values may be sent and summed in bfloat16 or wider, within the bound.
No kernel may reach another device: no remote copies, remote signals or barrier semaphores. Data moves between devices by JAX's collectives and lax.ppermute only.
A program may use at most 192 MiB of HBM per device.

v0:
```python
import jax
import jax.numpy as jnp
from jax import lax
from jax.sharding import Mesh
from jax.sharding import PartitionSpec as P

IMG_DEV = 4
SHOT_GRP = ("shot_0", "shot_1", "shot_2", "grp")
SHOT = ("shot_0", "shot_1", "shot_2")


def over_axes(array, axes):
    for axis in axes:
        array = lax.psum(array, axis)
    return array


def in_blocks(array, dim, count):
    before, after = (array.shape[:dim], array.shape[dim + 1 :])
    return jnp.moveaxis(array.reshape(*before, count, -1, *after), dim, 0)


def sent_and_summed(array, axis, dim):
    parts = in_blocks(array, dim, lax.axis_size(axis))
    arrived = lax.all_to_all(parts, axis, split_axis=0, concat_axis=0, tiled=True)
    return arrived.sum(axis=0)


def slant_stack(gathers, weights, live_mask):
    slanted = jnp.einsum("ah,phz->paz", weights, gathers, preferred_element_type=jnp.float32)
    return (slanted * live_mask[:, :, None]).astype(jnp.bfloat16)


def angle_moments(angles, live_mask):
    widened = angles.astype(jnp.float32)
    return (jnp.sum(widened * widened, axis=(0, 2)), jnp.sum(live_mask, axis=0))


def global_gain(square_sum, live_count, depth_len):
    totals = (over_axes(square_sum, SHOT_GRP), over_axes(live_count, SHOT_GRP))
    return lax.rsqrt(totals[0] / (depth_len * totals[1]) + 1e-06)


def local(offsets, slant_weights, live, block_tile, image_slot):
    peer_count = lax.axis_size(SHOT)
    block_count = block_tile.shape[0]
    capacity = block_count // peer_count + 1
    slot_count = peer_count * capacity
    depth_len = offsets.shape[2]
    angle_count = slant_weights.shape[0]
    traces = 2 * angle_count
    tile_ids = block_tile[:, 0]
    block_index = jnp.arange(block_count)
    earlier = (tile_ids[:, None] == tile_ids[None, :]) & (
        block_index[None, :] < block_index[:, None]
    )
    slot_rank = jnp.sum(earlier.astype(jnp.int32), axis=1)
    targets = tile_ids * capacity + slot_rank
    labels = (
        jnp.full((slot_count,), -1.0, jnp.float32).at[targets].set(image_slot.astype(jnp.float32))
    )
    labels = labels.astype(jnp.bfloat16).reshape(peer_count, capacity)
    inner = offsets.shape[1:]
    raw_sent = (
        jnp.zeros((slot_count, 2) + inner, jnp.bfloat16)
        .at[targets]
        .set(offsets.reshape((block_count, 2) + inner))
    )
    live_sent = (
        jnp.zeros((slot_count, traces), jnp.bfloat16)
        .at[targets]
        .set(live.reshape(block_count, traces).astype(jnp.bfloat16))
    )
    raw_in, live_in, labels_in = (
        lax.all_to_all(
            raw_sent.reshape((peer_count, capacity, 2) + inner),
            SHOT,
            split_axis=0,
            concat_axis=0,
            tiled=True,
        ),
        lax.all_to_all(
            live_sent.reshape(peer_count, capacity, traces),
            SHOT,
            split_axis=0,
            concat_axis=0,
            tiled=True,
        ),
        lax.all_to_all(labels, SHOT, split_axis=0, concat_axis=0, tiled=True),
    )
    mask_in = live_in.reshape(slot_count * 2, angle_count).astype(jnp.float32)
    angles = slant_stack(raw_in.reshape((slot_count * 2,) + inner), slant_weights, mask_in)
    square_sum, live_count = angle_moments(angles, mask_in)
    received = angles.reshape(slot_count, traces * depth_len)
    angle_gain = global_gain(square_sum, live_count, depth_len)
    tile_rows = IMG_DEV * lax.axis_size("grp")
    slot_codes = labels_in.reshape(slot_count).astype(jnp.float32)
    holder = (slot_codes[None, :] == jnp.arange(tile_rows, dtype=jnp.float32)[:, None]).astype(
        jnp.bfloat16
    )
    stacked = sent_and_summed(
        jnp.dot(holder, received, preferred_element_type=jnp.float32), "grp", 0
    )
    trace_gain = jnp.tile(angle_gain, 2)
    return (stacked.reshape(IMG_DEV, traces, depth_len) * trace_gain[None, :, None]).astype(
        jnp.bfloat16
    )


def solution(mesh):
    torus = Mesh(
        mesh.devices.reshape(4, 8, 2, mesh.shape["grp"]), ("shot_0", "shot_1", "shot_2", "grp")
    )
    return jax.shard_map(
        local,
        mesh=torus,
        in_specs=(P(SHOT_GRP, None, None), P(), P(SHOT_GRP, None), P(SHOT_GRP, None), P(SHOT_GRP)),
        out_specs=P(SHOT_GRP, None, None),
        check_vma=False,
    )
```

profile of v0, /device:TPU:1, one launch (start us, length us, event | category | flops | bytes accessed | tf_op | source)
XLA Modules:
  0.0 352.8 jit_solution(17804898050667033546)
XLA Ops:
  0.0 0.9 convert_reduce_fusion
  0.9 0.7 fusion.10
  1.6 0.7 convert_element_type.49
  2.2 0.9 scatter_custom_fusion
  3.1 0.8 all_to_all.20
  3.9 13.1 %all-to-all-start = ((bf16[64,1,2]{2,1,0:T(2,128)(2,1)}), bf16[64,1,2]{2,1,0:T(2,128)(2,1)S(1)}, u32[]{:S(2)}, u32[]{:S(2)}) async-start(bf16[64,1,2]{2,1,0:T(2,128)(2,1)} %all_to_all.20), calls=%async_computation | async-start | bytes 65536 | tf_op jit(solution)/shard_map/all_to_all | solution.py:89
  17.1 0.8 convert_element_type.53
  17.9 0.1 copy.10
  18.0 0.1 reshape.92
  18.1 1.4 scatter_custom_fusion.2
  19.5 6.9 %all-to-all-done = bf16[64,1,2]{2,1,0:T(2,128)(2,1)S(1)} async-done(((bf16[64,1,2]{2,1,0:T(2,128)(2,1)}), bf16[64,1,2]{2,1,0:T(2,128)(2,1)S(1)}, u32[]{:S(2)}, u32[]{:S(2)}) %all-to-all-start) | async-done | bytes 288 | tf_op jit(solution)/shard_map/all_to_all | solution.py:89
  26.4 4.7 %all-to-all-start.2 = ((bf16[64,2,128]{2,1,0:T(2,128)(2,1)}), bf16[64,2,128]{2,1,0:T(2,128)(2,1)S(1)}, u32[]{:S(2)}, u32[]{:S(2)}) async-start(bf16[64,2,128]{2,1,0:T(2,128)(2,1)} %bitcast.7), calls=%async_computation.2 | async-start | bytes 65536 | tf_op jit(solution)/shard_map/all_to_all | solution.py:82
  31.1 4.3 %broadcast_in_dim.7 = bf16[128,2,32,512]{3,2,1,0:T(8,128)(2,1)} broadcast(bf16[]{:T(256)} %constant.5.clone.1), dimensions={} | broadcast | bytes 8388610 | tf_op jit(solution)/shard_map/broadcast_in_dim | solution.py:65
  35.4 17.8 %scatter_fusion = bf16[128,2,32,512]{3,2,1,0:T(8,128)(2,1)} fusion(bf16[128,2,32,512]{3,2,1,0:T(8,128)(2,1)} %broadcast_in_dim.7, s32[96]{0:T(128)S(1)} %fusion.10, bf16[96,2,32,512]{3,2,1,0:T(8,128)(2,1)} %bitcast.26), kind=kCustom, calls=%fused_computation.1 | custom fusion | bytes 18874752 | tf_op jit(solution)/shard_map/scatter | solution.py:67
  53.1 0.0 all-to-all-done.2
  53.1 10.8 %all-to-all-start.1 = ((bf16[64,2,2,32,512]{4,3,2,1,0:T(8,128)(2,1)}), bf16[64,2,2,32,512]{4,3,2,1,0:T(8,128)(2,1)}, u32[]{:S(2)}, u32[]{:S(2)}) async-start(bf16[64,2,2,32,512]{4,3,2,1,0:T(8,128)(2,1)} %bitcast.25), calls=%async_computation.1 | async-start | bytes 16777216 | tf_op jit(solution)/shard_map/all_to_all | solution.py:75
  63.9 0.1 convert_reduce_fusion.1
  64.0 0.1 reshape.70
  64.1 0.1 reshape.71
  64.2 185.4 %all-to-all-done.1 = bf16[64,2,2,32,512]{4,3,2,1,0:T(8,128)(2,1)} async-done(((bf16[64,2,2,32,512]{4,3,2,1,0:T(8,128)(2,1)}), bf16[64,2,2,32,512]{4,3,2,1,0:T(8,128)(2,1)}, u32[]{:S(2)}, u32[]{:S(2)}) %all-to-all-start.1) | async-done | bytes 8388640 | tf_op jit(solution)/shard_map/all_to_all | solution.py:75
  249.6 12.6 %multiply_reduce_fusion = (f32[64]{0:T(128)S(1)}, bf16[256,64,512]{2,1,0:T(8,128)(2,1)}) fusion(f32[256,64]{1,0:T(8,128)S(1)} %reshape.71, bf16[256,32,512]{2,1,0:T(8,128)(2,1)} %bitcast.5, bf16[64,32]{0,1:T(8,128)(2,1)S(1)} %copy-done), kind=kOutput, calls=%fused_computation.3 | convolution fusion | flops 578813888 | bytes 25235712 | tf_op jit(solution)/shard_map/ah,phz->paz/dot_general | solution.py:30
  262.3 20.4 %reshape.97 = bf16[128,65536,1]{1,0,2:T(8,128)(2,1)} reshape(bf16[256,64,512]{2,1,0:T(8,128)(2,1)} %get-tuple-element.14) | data formatting | bytes 33554432 | tf_op jit(solution)/shard_map/reshape | solution.py:94
  282.7 10.0 %fusion.6 = f32[4,4,65536]{2,1,0:T(4,128)} fusion(bf16[128,65536,1]{1,0,2:T(8,128)(2,1)} %reshape.97, f32[4,4]{1,0:T(4,128)S(1)} %multiply_add_fusion, f32[128]{0:T(128)S(1)} %reshape.70), kind=kOutput, calls=%fused_computation.15 | convolution fusion | flops 268437504 | bytes 20972096 | tf_op jit(solution)/shard_map/dot_general | solution.py:102
  292.8 4.8 %all-to-all-start.3 = ((f32[4,4,65536]{2,1,0:T(4,128)}), f32[4,4,65536]{2,1,0:T(4,128)}, u32[]{:S(2)}, u32[]{:S(2)}) async-start(f32[4,4,65536]{2,1,0:T(4,128)} %fusion.6), calls=%async_computation.3 | async-start | bytes 8388608 | tf_op jit(solution)/shard_map/all_to_all | solution.py:25
  297.6 0.1 reduce_sum.42
  297.7 9.4 %all-reduce.2 = (f32[64]{0:T(128)S(1)}, f32[64]{0:T(128)S(1)}) all-reduce(f32[64]{0:T(128)S(1)} %get-tuple-element.13, f32[64]{0:T(128)S(1)} %reduce_sum.42), channel_id=1, replica_groups=mesh['shot_0'=4,'shot_1'=8,'shot_2'=2,'grp'=4] {'shot_0'}, use_global_device_ids=true, to_apply=%region_6.0 | all-reduce | flops 128 | bytes 1024 | tf_op jit(solution)/shard_map/psum | solution.py:14
  307.1 12.6 %all-reduce = (f32[64]{0:T(128)S(1)}, f32[64]{0:T(128)S(1)}) all-reduce(f32[64]{0:T(128)S(1)} %get-tuple-element.9, f32[64]{0:T(128)S(1)} %get-tuple-element.10), channel_id=1, replica_groups=mesh['shot_0'=4,'shot_1'=8,'shot_2'=2,'grp'=4] {'shot_1'}, use_global_device_ids=true, to_apply=%region_7.0 | all-reduce | flops 128 | bytes 1024 | tf_op jit(solution)/shard_map/psum | solution.py:14
  319.6 5.3 %all-reduce.3 = (f32[64]{0:T(128)S(1)}, f32[64]{0:T(128)S(1)}) all-reduce(f32[64]{0:T(128)S(1)} %get-tuple-element.5, f32[64]{0:T(128)S(1)} %get-tuple-element.6), channel_id=1, replica_groups=mesh['shot_0'=4,'shot_1'=8,'shot_2'=2,'grp'=4] {'shot_2'}, use_global_device_ids=true, to_apply=%region_8.0 | all-reduce | flops 128 | bytes 1024 | tf_op jit(solution)/shard_map/psum | solution.py:14
  324.9 23.5 %all-reduce.1 = (f32[64]{0:T(128)S(1)}, f32[64]{0:T(128)S(1)}) all-reduce(f32[64]{0:T(128)S(1)} %get-tuple-element.11, f32[64]{0:T(128)S(1)} %get-tuple-element.12), channel_id=1, replica_groups=mesh['shot_0'=4,'shot_1'=8,'shot_2'=2,'grp'=4] {'grp'}, use_global_device_ids=true, to_apply=%region_9.0 | all-reduce | flops 128 | bytes 1024 | tf_op jit(solution)/shard_map/psum | solution.py:14
  348.4 0.1 mul.42
  348.5 3.2 reduce_sum.40
  351.7 1.1 fusion.1
  (9 shorter events, 0.0 us)
Async XLA Ops:
  0.0 249.6 %copy-start = (bf16[64,32]{0,1:T(8,128)(2,1)S(1)}, bf16[64,32]{0,1:T(8,128)(2,1)}, u32[]{:S(2)}) copy-start(bf16[64,32]{0,1:T(8,128)(2,1)} %param.6) | copy-start | bytes 12292
  3.9 22.5 %all-to-all-start = ((bf16[64,1,2]{2,1,0:T(2,128)(2,1)}), bf16[64,1,2]{2,1,0:T(2,128)(2,1)S(1)}, u32[]{:S(2)}, u32[]{:S(2)}) async-start(bf16[64,1,2]{2,1,0:T(2,128)(2,1)} %all_to_all.20), calls=%async_computation | async-start | bytes 65536 | tf_op jit(solution)/shard_map/all_to_all | solution.py:89
  26.4 26.7 %all-to-all-start.2 = ((bf16[64,2,128]{2,1,0:T(2,128)(2,1)}), bf16[64,2,128]{2,1,0:T(2,128)(2,1)S(1)}, u32[]{:S(2)}, u32[]{:S(2)}) async-start(bf16[64,2,128]{2,1,0:T(2,128)(2,1)} %bitcast.7), calls=%async_computation.2 | async-start | bytes 65536 | tf_op jit(solution)/shard_map/all_to_all | solution.py:82
  53.1 196.5 %all-to-all-start.1 = ((bf16[64,2,2,32,512]{4,3,2,1,0:T(8,128)(2,1)}), bf16[64,2,2,32,512]{4,3,2,1,0:T(8,128)(2,1)}, u32[]{:S(2)}, u32[]{:S(2)}) async-start(bf16[64,2,2,32,512]{4,3,2,1,0:T(8,128)(2,1)} %bitcast.25), calls=%async_computation.1 | async-start | bytes 16777216 | tf_op jit(solution)/shard_map/all_to_all | solution.py:75
  282.7 70.1 %copy-start.1 = (bf16[64,32]{0,1:T(8,128)(2,1)S(1)}, bf16[64,32]{0,1:T(8,128)(2,1)}, u32[]{:S(2)}) copy-start(bf16[64,32]{0,1:T(8,128)(2,1)} %param.6) | copy-start | bytes 12292
  292.8 55.8 %all-to-all-start.3 = ((f32[4,4,65536]{2,1,0:T(4,128)}), f32[4,4,65536]{2,1,0:T(4,128)}, u32[]{:S(2)}, u32[]{:S(2)}) async-start(f32[4,4,65536]{2,1,0:T(4,128)} %fusion.6), calls=%async_computation.3 | async-start | bytes 8388608 | tf_op jit(solution)/shard_map/all_to_all | solution.py:25
where the time goes:
time: 354 us; the launch traced here: 353 us
  waiting for transfers between devices  192 us (54%)
  blocking collectives  50.8 us (14%)
  local copies, waits for them, and re-layouts  46 us (13%)
  starting transfers between devices  33.4 us (9%)
  matrix products  22.7 us (6%)
  other arithmetic  7.56 us (2%)
    all_to_all x1, waiting for transfers between devices, local(): lax.all_to_all(raw_sent.reshape((peer_count, capacity, 2) + inner), SHOT,...  185 us
    psum x4, blocking collectives, over_axes(): array = lax.psum(array, axis)  50.8 us
    reshape x1, local copies, waits for them, and re-layouts, local(): received = angles.reshape(slot_count, traces * depth_len)  20.4 us
    scatter x1, local copies, waits for them, and re-layouts, local(): raw_sent = jnp.zeros((slot_count, 2) + inner, jnp.bfloat16).at[targets].s...  17.8 us
    all_to_all x1, starting transfers between devices, local(): lax.all_to_all(labels, SHOT, split_axis=0, concat_axis=0, tiled=True)  13.1 us
    dot_general x1, matrix products, slant_stack(): jnp.einsum('ah,phz->paz', weights, gathers, preferred_element_type=jnp.fl...  12.6 us
    all_to_all x1, starting transfers between devices, local(): lax.all_to_all(raw_sent.reshape((peer_count, capacity, 2) + inner), SHOT,...  10.8 us
    dot_general x1, matrix products, local(): jnp.dot(holder, received, preferred_element_type=jnp.float32)  10 us
  transfers between devices with their start and end apart: 4, of which 2 were waited for; matrix products, arithmetic and copies ran while one was open for 7% of the time, Pallas kernels for 0%

commit v1 on v0

v1 whole, which is shorter than its diff:
```python
import functools

import jax
import jax.numpy as jnp
from jax import lax
from jax.experimental import pallas as pl
from jax.experimental.pallas import tpu as pltpu
from jax.sharding import Mesh
from jax.sharding import PartitionSpec as P

SHOT_GRP = ("shot_0", "shot_1", "shot_2", "grp")
PLANE = ("shot_0", "shot_2", "grp")
LANES = 128
CAP = 2
GROUP = 8


def pack_kernel(
    parity, tile_ref, slot_ref, live_ref, off_ref, out_ref,
    data, zeros, meta, meta_low, count, in_sems, out_sem, meta_sem,
):
    blocks = off_ref.shape[0]
    hh = off_ref.shape[2]
    quarters = data.shape[0]
    tiles = count.shape[0]
    rows = meta.shape[1]
    parts = in_sems.shape[0]
    step = blocks // parts
    angles = live_ref.shape[1]

    def load(g, q):
        return pltpu.make_async_copy(
            off_ref.at[pl.ds(g * step, step), parity, :, pl.ds(q * LANES, LANES)],
            data.at[q, pl.ds(g * step, step)],
            in_sems.at[g],
        )

    for g in range(parts):
        for q in range(quarters):
            load(g, q).start()
    zeros[...] = jnp.zeros_like(zeros)
    meta[...] = jnp.zeros_like(meta)

    def clear(t, _):
        count[t] = 0
        return 0

    lax.fori_loop(0, tiles, clear, 0)

    def place(tile, rank):
        column = (tile // 16) * 2 + tile % 2
        return column, ((tile // 2) % 8) * CAP + rank

    def target(column, row):
        return out_ref.at[column, :, pl.ds(pl.multiple_of(row * hh, hh), hh), :]

    def send(b, _):
        tile = tile_ref[b]
        rank = count[tile]
        count[tile] = rank + 1
        column, row = place(tile, rank)
        pltpu.make_async_copy(data.at[:, b], target(column, row), out_sem).start()
        flags = live_ref[pl.ds(b * 2 + parity, 1), :].astype(jnp.float32)
        meta[column, pl.ds(row, 1), :angles] = flags * (slot_ref[b] + 1).astype(jnp.float32)
        return 0

    for g in range(parts):
        for q in range(quarters):
            load(g, q).wait()
        lax.fori_loop(g * step, (g + 1) * step, send, 0)

    def fill(tile, _):
        used = count[tile]
        for rank in range(CAP):
            column, row = place(tile, rank)

            @pl.when(used <= rank)
            def _():
                pltpu.make_async_copy(zeros, target(column, row), out_sem).start()
        return 0

    lax.fori_loop(0, tiles, fill, 0)
    meta_low[...] = meta[...].astype(jnp.bfloat16)

    def meta_copy(q):
        return pltpu.make_async_copy(
            meta_low, out_ref.at[:, q, pl.ds(rows * hh, rows), :], meta_sem
        )

    for q in range(quarters):
        meta_copy(q).start()
    whole = out_ref.at[:, :, pl.ds(0, rows * hh), :]
    pltpu.make_async_copy(whole, whole, out_sem).wait()
    for q in range(quarters):
        meta_copy(q).wait()


def pack(parity, tiles, slots, live, blocks, columns, quarters, tile_count):
    count, _, hh, depth = blocks.shape
    rows = tile_count // columns * CAP
    parts = 8
    any_space = pl.BlockSpec(memory_space=pl.ANY)
    smem = pl.BlockSpec(memory_space=pltpu.SMEM)
    return pl.pallas_call(
        functools.partial(pack_kernel, parity),
        out_shape=jax.ShapeDtypeStruct(
            (columns, quarters, rows * hh + rows, LANES), jnp.bfloat16
        ),
        in_specs=[smem, smem, pl.BlockSpec(memory_space=pltpu.VMEM), any_space],
        out_specs=any_space,
        scratch_shapes=[
            pltpu.VMEM((quarters, count, hh, LANES), jnp.bfloat16),
            pltpu.VMEM((quarters, hh, LANES), jnp.bfloat16),
            pltpu.VMEM((columns, rows, LANES), jnp.float32),
            pltpu.VMEM((columns, rows, LANES), jnp.bfloat16),
            pltpu.SMEM((tile_count,), jnp.int32),
            pltpu.SemaphoreType.DMA((parts,)),
            pltpu.SemaphoreType.DMA,
            pltpu.SemaphoreType.DMA,
        ],
        compiler_params=pltpu.CompilerParams(vmem_limit_bytes=16 * 2**20),
        cost_estimate=pl.CostEstimate(
            flops=8_000_000_000, bytes_accessed=7 * 2**20, transcendentals=0
        ),
        name=f"pack{parity}",
    )(tiles, slots, live, blocks)


def stack_kernel(code_ref, w_ref, in_ref, out_ref, acc):
    step = pl.program_id(0)
    angles, lanes = acc.shape[2:]
    tile_rows = out_ref.shape[1]
    depth = w_ref.shape[1]
    slots = (in_ref.shape[1] * GROUP) // (depth + GROUP)

    @pl.when(step == 0)
    def _():
        acc[...] = jnp.zeros_like(acc)

    row = lax.broadcasted_iota(jnp.int32, (angles, lanes), 0)
    for u in range(in_ref.shape[0]):
        for part in range(slots // GROUP):
            product = jnp.dot(
                w_ref[...],
                in_ref[u, part * depth : (part + 1) * depth, :],
                preferred_element_type=jnp.float32,
            )
            for j in range(GROUP):
                slot = part * GROUP + j
                code = code_ref[(step * in_ref.shape[0] + u) * slots + slot]
                label = code // 128
                cut = code % 128
                angle = jnp.where(row < cut, product[j * angles : (j + 1) * angles], 0.0)
                acc[slot // CAP, label] += angle.astype(jnp.bfloat16).astype(jnp.float32)

    @pl.when(step == pl.num_programs(0) - 1)
    def _():
        out_ref[...] = acc[:, :tile_rows].astype(out_ref.dtype)


def stack(arrived, weights, tile_rows, hh):
    sources, length, lanes = arrived.shape
    slots = length // (hh + 1)
    angles = weights.shape[0] // GROUP
    flags = arrived[:, slots * hh :, :angles]
    label = jnp.max(flags, axis=2).astype(jnp.int32)
    cut = jnp.sum((flags > 0).astype(jnp.int32), axis=2)
    code = (jnp.where(label == 0, tile_rows, label - 1) * 128 + cut).reshape(-1)
    per = 4
    tiles = slots // CAP
    return pl.pallas_call(
        stack_kernel,
        grid=(sources // per,),
        out_shape=jax.ShapeDtypeStruct((tiles, tile_rows, angles, lanes), jnp.bfloat16),
        in_specs=[
            pl.BlockSpec(memory_space=pltpu.SMEM),
            pl.BlockSpec(weights.shape, lambda i: (0, 0)),
            pl.BlockSpec((per, length, lanes), lambda i: (i, 0, 0)),
        ],
        out_specs=pl.BlockSpec((tiles, tile_rows, angles, lanes), lambda i: (0, 0, 0, 0)),
        scratch_shapes=[pltpu.VMEM((tiles, tile_rows + 1, angles, lanes), jnp.float32)],
        compiler_params=pltpu.CompilerParams(vmem_limit_bytes=24 * 2**20),
        cost_estimate=pl.CostEstimate(
            flops=12_000_000_000, bytes_accessed=7 * 2**20, transcendentals=0
        ),
        name="stack",
    )(code, weights, arrived)


def moments_kernel(cut_ref, w_ref, in_ref, out_ref):
    step = pl.program_id(0)
    angles, lanes = out_ref.shape
    count, hh, depth = in_ref.shape

    @pl.when(step == 0)
    def _():
        out_ref[...] = jnp.zeros_like(out_ref)

    row = lax.broadcasted_iota(jnp.int32, (angles, lanes), 0)
    total = out_ref[...]
    for part in range(count // GROUP):
        gathers = in_ref[part * GROUP : (part + 1) * GROUP].reshape(GROUP * hh, depth)
        square = None
        for q in range(depth // lanes):
            product = jnp.dot(
                w_ref[...],
                gathers[:, q * lanes : (q + 1) * lanes],
                preferred_element_type=jnp.float32,
            )
            product = product.astype(jnp.bfloat16).astype(jnp.float32)
            square = product * product if square is None else square + product * product
        for j in range(GROUP):
            cut = cut_ref[step * count + part * GROUP + j]
            total += jnp.where(row < cut, square[j * angles : (j + 1) * angles], 0.0)
    out_ref[...] = total


def moments(offsets, weights, live):
    positions, hh, depth = offsets.shape
    angles = live.shape[1]
    per = 16
    squares = pl.pallas_call(
        moments_kernel,
        grid=(positions // per,),
        out_shape=jax.ShapeDtypeStruct((angles, LANES), jnp.float32),
        in_specs=[
            pl.BlockSpec(memory_space=pltpu.SMEM),
            pl.BlockSpec(weights.shape, lambda i: (0, 0)),
            pl.BlockSpec((per, hh, depth), lambda i: (i, 0, 0)),
        ],
        out_specs=pl.BlockSpec((angles, LANES), lambda i: (0, 0)),
        compiler_params=pltpu.CompilerParams(vmem_limit_bytes=24 * 2**20),
        cost_estimate=pl.CostEstimate(
            flops=12_000_000_000, bytes_accessed=6 * 2**20, transcendentals=0
        ),
        name="moments",
    )(jnp.sum(live, axis=1), weights, offsets)
    return jnp.sum(squares, axis=1), jnp.sum(live, axis=0).astype(jnp.float32)


def finish_kernel(gain_ref, first_ref, second_ref, out_ref):
    quarters, images, angles, lanes = first_ref.shape
    gain = gain_ref[...]
    for half, ref in enumerate((first_ref, second_ref)):
        for q in range(quarters):
            for k in range(images):
                value = ref[q, k].astype(jnp.float32) * gain
                out_ref[
                    k, half * angles : (half + 1) * angles, q * lanes : (q + 1) * lanes
                ] = value.astype(out_ref.dtype)


def finish(gain, first, second):
    quarters, images, angles, lanes = first.shape
    vmem = pl.BlockSpec(memory_space=pltpu.VMEM)
    return pl.pallas_call(
        finish_kernel,
        out_shape=jax.ShapeDtypeStruct((images, 2 * angles, quarters * lanes), jnp.bfloat16),
        in_specs=[vmem, vmem, vmem],
        out_specs=vmem,
        name="finish",
    )(jnp.broadcast_to(gain[:, None], (angles, lanes)), first, second)


def local(offsets, slant_weights, live, block_tile, image_slot):
    block_count = block_tile.shape[0]
    _, hh, depth = offsets.shape
    angles = slant_weights.shape[0]
    tile_count = lax.axis_size(("shot_0", "shot_1", "shot_2"))
    columns = lax.axis_size(("shot_0", "shot_2"))
    quarters = lax.axis_size("grp")
    tile_rows = 4 * quarters
    blocks = offsets.reshape(block_count, 2, hh, depth)
    tiles = block_tile[:, 0]
    weights = jnp.kron(jnp.eye(GROUP, dtype=jnp.bfloat16), slant_weights)

    ends = []
    for parity in range(2):
        sent = pack(
            parity, tiles, image_slot, live, blocks, columns, quarters, tile_count
        )
        sent = sent.reshape((columns * quarters,) + sent.shape[2:])
        arrived = lax.all_to_all(sent, PLANE, 0, 0, tiled=True)
        dense = stack(arrived, weights, tile_rows, hh)
        dense = dense.reshape((-1, angles, LANES))
        summed = lax.psum_scatter(dense, "shot_1", scatter_dimension=0, tiled=True)
        swapped = summed.reshape(quarters, 4, angles, LANES)
        ends.append(lax.all_to_all(swapped, "grp", 0, 0, tiled=True))

    squares, counts = moments(offsets, weights, live)
    totals = lax.psum(jnp.concatenate([squares, counts]), SHOT_GRP)
    gain = lax.rsqrt(totals[:angles] / (depth * totals[angles:]) + 1e-06)
    return finish(gain, ends[0], ends[1])


def solution(mesh):
    torus = Mesh(
        mesh.devices.reshape(4, 8, 2, mesh.shape["grp"]), ("shot_0", "shot_1", "shot_2", "grp")
    )
    return jax.shard_map(
        local,
        mesh=torus,
        in_specs=(P(SHOT_GRP, None, None), P(), P(SHOT_GRP, None), P(SHOT_GRP, None), P(SHOT_GRP)),
        out_specs=P(SHOT_GRP, None, None),
        check_vma=False,
    )
```

time: 354 us -> 268 us (0.76)
  waiting for transfers between devices: 192 us -> 81.8 us
  Pallas kernels: 0 us -> 45.4 us
  local copies, waits for them, and re-layouts: 46 us -> 15.9 us
  blocking collectives: 50.8 us -> 79.3 us
  matrix products: 22.7 us -> 0 us
  between operations: 0.1 us -> 13.6 us
  starting transfers between devices: 33.4 us -> 24.9 us
    all_to_all x4, waiting for transfers between devices: 192 us -> 81.8 us  [the longest x2 76.3 us: local(): arrived = lax.all_to_all(sent, PLANE, 0, 0, tiled=True)]
    pallas_call x0 -> x6, Pallas kernels: none -> 45.4 us  [the longest x2 20.1 us: stack(): pl.pallas_call(stack_kernel, grid=(sources // per,), out_shape=jax.ShapeD...]
    psum x4 -> x1, blocking collectives: 50.8 us -> 79.3 us  [local(): totals = lax.psum(jnp.concatenate([squares, counts]), SHOT_GRP)]
    dot_general x2 -> x0, matrix products: 22.7 us -> none  [the longest x1 12.6 us: slant_stack(): jnp.einsum('ah,phz->paz', weights, gathers, preferred_element_type=jnp.fl...]
    reshape x1 -> x0, local copies, waits for them, and re-layouts: 20.4 us -> none  [local(): received = angles.reshape(slot_count, traces * depth_len)]
    scatter x3 -> x0, local copies, waits for them, and re-layouts: 20 us -> none  [the longest x1 17.8 us: local(): raw_sent = jnp.zeros((slot_count, 2) + inner, jnp.bfloat16).at[targets].s...]
    unnamed x4 -> x27, local copies, waits for them, and re-layouts: 0.01 us -> 14.6 us
    all_to_all x4, starting transfers between devices: 33.4 us -> 24.8 us  [the longest x2 15.5 us: local(): arrived = lax.all_to_all(sent, PLANE, 0, 0, tiled=True)]
  transfers between devices with their start and end apart: 4 -> 6, of which waited for: 2 -> 3; matrix products, arithmetic and copies ran while one was open for 7% -> 2% of each run, Pallas kernels for 0% -> 14%
where the time goes in v1:
time: 268 us; the launch traced here: 267 us
  waiting for transfers between devices  81.8 us (31%)
  blocking collectives  79.3 us (30%)
  Pallas kernels  45.4 us (17%)
  starting transfers between devices  24.9 us (9%)
  local copies, waits for them, and re-layouts  15.9 us (6%)
  between operations  13.6 us (5%)
  other arithmetic  5.68 us (2%)
    psum x1, blocking collectives, local(): totals = lax.psum(jnp.concatenate([squares, counts]), SHOT_GRP)  79.3 us
    all_to_all x2, waiting for transfers between devices, local(): arrived = lax.all_to_all(sent, PLANE, 0, 0, tiled=True)  76.3 us
    pallas_call x2, Pallas kernels, stack(): pl.pallas_call(stack_kernel, grid=(sources // per,), out_shape=jax.ShapeD...  20.1 us
    all_to_all x2, starting transfers between devices, local(): arrived = lax.all_to_all(sent, PLANE, 0, 0, tiled=True)  15.5 us
    unnamed x27, local copies, waits for them, and re-layouts  14.6 us
    pallas_call x2, Pallas kernels, pack(): pl.pallas_call(functools.partial(pack_kernel, parity), out_shape=jax.Shap...  13.9 us
    pallas_call x1, Pallas kernels, moments(): pl.pallas_call(moments_kernel, grid=(positions // per,), out_shape=jax.Sh...  9.37 us
    all_to_all x2, starting transfers between devices, local(): ends.append(lax.all_to_all(swapped, 'grp', 0, 0, tiled=True))  9.29 us
  transfers between devices with their start and end apart: 6, of which 3 were waited for; matrix products, arithmetic and copies ran while one was open for 2% of the time, Pallas kernels for 14%

profile of v1, /device:TPU:1, one launch (start us, length us, event | category | flops | bytes accessed | tf_op | source)
XLA Modules:
  0.0 266.6 jit_solution(6019543273853485647)
XLA Ops:
  6.5 0.9 copy.10.live_ref
  7.5 2.8 %copy-done.2 = bf16[192,32,512]{2,1,0:T(8,128)(2,1)S(1)} copy-done((bf16[192,32,512]{2,1,0:T(8,128)(2,1)S(1)}, bf16[192,32,512]{2,1,0:T(8,128)(2,1)}, u32[]{:S(2)}) %copy-start.2) | copy-done | bytes 6291480
  10.3 0.7 copy-done.5
  10.9 0.7 copy-done.7
  11.6 7.0 %pack1.1 = bf16[8,4,528,128]{3,2,1,0:T(8,128)(2,1)S(1)} custom-call(s32[96]{0:T(128)S(1)} %bitcast.16, s32[96]{0:T(128)S(1)} %copy-done.7, s32[192,64]{1,0:T(8,128)S(1)} %copy.10.live_ref, bf16[96,2,32,512]{3,2,1,0:T(8,128)(2,1)S(1)} %bitcast.14), custom_call_target="tpu_custom_call" | custom-call | flops 8000000000 | bytes 7340032 | tf_op jit(solution)/shard_map/pack1/pallas_call | solution.py:104
  18.6 2.0 copy-done.1
  20.5 8.8 %all-to-all-start.2 = ((bf16[32,528,128]{2,1,0:T(8,128)(2,1)}), bf16[32,528,128]{2,1,0:T(8,128)(2,1)}, u32[]{:S(2)}, u32[]{:S(2)}) async-start(bf16[32,528,128]{2,1,0:T(8,128)(2,1)} %bitcast.13), calls=%async_computation.3 | async-start | bytes 8650752 | tf_op jit(solution)/shard_map/all_to_all | solution.py:283
  29.3 0.1 broadcast_multiply_fusion
  29.4 0.3 mul.47
  29.8 0.1 copy.9.w_ref
  29.9 2.8 %copy-done.3 = bf16[192,32,512]{2,1,0:T(8,128)(2,1)S(1)} copy-done((bf16[192,32,512]{2,1,0:T(8,128)(2,1)S(1)}, bf16[192,32,512]{2,1,0:T(8,128)(2,1)}, u32[]{:S(2)}) %copy-start.3) | copy-done | bytes 6291480
  32.7 7.0 %pack0.1 = bf16[8,4,528,128]{3,2,1,0:T(8,128)(2,1)S(1)} custom-call(s32[96]{0:T(128)S(1)} %bitcast.17, s32[96]{0:T(128)S(1)} %copy-done.8, s32[192,64]{1,0:T(8,128)S(1)} %copy.10.live_ref, bf16[96,2,32,512]{3,2,1,0:T(8,128)(2,1)S(1)} %bitcast.15), custom_call_target="tpu_custom_call" | custom-call | flops 8000000000 | bytes 7340032 | tf_op jit(solution)/shard_map/pack0/pallas_call | solution.py:104
  39.7 2.0 copy-done
  41.7 38.4 %all-to-all-done.2.in_ref = bf16[32,528,128]{2,1,0:T(8,128)(2,1)} async-done(((bf16[32,528,128]{2,1,0:T(8,128)(2,1)}), bf16[32,528,128]{2,1,0:T(8,128)(2,1)}, u32[]{:S(2)}, u32[]{:S(2)}) %all-to-all-start.2) | async-done | bytes 4325408 | tf_op jit(solution)/shard_map/all_to_all | solution.py:283
  80.1 6.8 %all-to-all-start = ((bf16[32,528,128]{2,1,0:T(8,128)(2,1)}), bf16[32,528,128]{2,1,0:T(8,128)(2,1)}, u32[]{:S(2)}, u32[]{:S(2)}) async-start(bf16[32,528,128]{2,1,0:T(8,128)(2,1)} %bitcast.12), calls=%async_computation | async-start | bytes 8650752 | tf_op jit(solution)/shard_map/all_to_all | solution.py:283
  86.9 1.1 slice_reduce_fusion
  88.0 1.5 convert_reduce_fusion
  89.6 10.0 %stack.3 = bf16[8,16,64,128]{3,2,1,0:T(8,128)(2,1)} custom-call(s32[512]{0:T(512)S(1)} %reshape.68.code_ref, bf16[512,256]{1,0:T(8,128)(2,1)S(1)} %copy.9.w_ref, bf16[32,528,128]{2,1,0:T(8,128)(2,1)} %all-to-all-done.2.in_ref), custom_call_target="tpu_custom_call" | custom-call | flops 12000000000 | bytes 7340032 | tf_op jit(solution)/shard_map/stack/pallas_call | solution.py:171
  99.7 37.9 %all-to-all-done.in_ref = bf16[32,528,128]{2,1,0:T(8,128)(2,1)} async-done(((bf16[32,528,128]{2,1,0:T(8,128)(2,1)}), bf16[32,528,128]{2,1,0:T(8,128)(2,1)}, u32[]{:S(2)}, u32[]{:S(2)}) %all-to-all-start) | async-done | bytes 4325408 | tf_op jit(solution)/shard_map/all_to_all | solution.py:283
  137.7 1.1 slice_reduce_fusion.1
  138.7 1.5 convert_reduce_fusion.1
  140.4 10.1 %stack.2 = bf16[8,16,64,128]{3,2,1,0:T(8,128)(2,1)} custom-call(s32[512]{0:T(512)S(1)} %reshape.67.code_ref, bf16[512,256]{1,0:T(8,128)(2,1)S(1)} %copy.9.w_ref, bf16[32,528,128]{2,1,0:T(8,128)(2,1)} %all-to-all-done.in_ref), custom_call_target="tpu_custom_call" | custom-call | flops 12000000000 | bytes 7340032 | tf_op jit(solution)/shard_map/stack/pallas_call | solution.py:171
  150.5 0.1 fusion.7
  150.6 5.8 %all-to-all-start.3 = ((bf16[4,4,64,128]{3,2,1,0:T(8,128)(2,1)}), bf16[4,4,64,128]{3,2,1,0:T(8,128)(2,1)S(1)}, u32[]{:S(2)}, u32[]{:S(2)}) async-start(bf16[4,4,64,128]{3,2,1,0:T(8,128)(2,1)} %bitcast.18), calls=%async_computation.5 | async-start | bytes 524288 | tf_op jit(solution)/shard_map/all_to_all | solution.py:288
  156.5 2.8 %copy-done.4 = bf16[192,32,512]{2,1,0:T(8,128)(2,1)S(1)} copy-done((bf16[192,32,512]{2,1,0:T(8,128)(2,1)S(1)}, bf16[192,32,512]{2,1,0:T(8,128)(2,1)}, u32[]{:S(2)}) %copy-start.4) | copy-done | bytes 6291480
  159.2 9.4 %moments.1 = f32[64,128]{1,0:T(8,128)S(1)} custom-call(s32[192]{0:T(256)S(1)} %get-tuple-element.5.cut_ref, bf16[512,256]{1,0:T(8,128)(2,1)S(1)} %copy.9.w_ref, bf16[192,32,512]{2,1,0:T(8,128)(2,1)S(1)} %copy-done.4), custom_call_target="tpu_custom_call" | custom-call | flops 12000000000 | bytes 6291456 | tf_op jit(solution)/shard_map/moments/pallas_call | solution.py:222
  168.6 0.1 reduce_sum.50
  168.8 79.3 %psum.7 = f32[128]{0:T(128)S(1)} all-reduce(f32[128]{0:T(128)S(1)} %pad_maximum_fusion), channel_id=1, replica_groups=mesh['shot_0'=4,'shot_1'=8,'shot_2'=2,'grp'=4] {'shot_0','shot_1','shot_..., use_global_device_ids=true, to_apply=%region_3.4 | all-reduce | flops 128 | bytes 1024 | tf_op jit(solution)/shard_map/psum | solution.py:291
  248.1 3.5 %all-to-all-start.1 = ((bf16[4,4,64,128]{3,2,1,0:T(8,128)(2,1)}), bf16[4,4,64,128]{3,2,1,0:T(8,128)(2,1)S(1)}, u32[]{:S(2)}, u32[]{:S(2)}) async-start(bf16[4,4,64,128]{3,2,1,0:T(8,128)(2,1)} %bitcast.19), calls=%async_computation.2 | async-start | bytes 524288 | tf_op jit(solution)/shard_map/all_to_all | solution.py:288
  251.6 5.5 %all-to-all-done.1.first_ref = bf16[4,4,64,128]{3,2,1,0:T(8,128)(2,1)S(1)} async-done(((bf16[4,4,64,128]{3,2,1,0:T(8,128)(2,1)}), bf16[4,4,64,128]{3,2,1,0:T(8,128)(2,1)S(1)}, u32[]{:S(2)}, u32[]{:S(2)}) %all-to-all-start.1) | async-done | bytes 262176 | tf_op jit(solution)/shard_map/all_to_all | solution.py:288
  257.1 0.7 broadcast_in_dim.15.gain_ref
  257.8 1.9 finish.1
  (34 shorter events, 0.5 us)
Async XLA Ops:
  7.5 2.8 %copy-start.2 = (bf16[192,32,512]{2,1,0:T(8,128)(2,1)S(1)}, bf16[192,32,512]{2,1,0:T(8,128)(2,1)}, u32[]{:S(2)}) copy-start(bf16[192,32,512]{2,1,0:T(8,128)(2,1)} %in_ref.1) | copy-start | bytes 18874372
  10.3 0.7 copy-start.5
  10.9 0.7 copy-start.7
  18.6 2.0 copy-start.1
  20.5 8.8 %copy-start.12 = (bf16[64,32]{0,1:T(8,128)(2,1)S(1)}, bf16[64,32]{0,1:T(8,128)(2,1)}, u32[]{:S(2)}) copy-start(bf16[64,32]{0,1:T(8,128)(2,1)} %param.6) | copy-start | bytes 12292
  20.5 9.4 %copy-start.6 = (s32[96,1]{0,1:T(1,128)S(1)}, s32[96,1]{0,1:T(1,128)}, u32[]{:S(2)}) copy-start(s32[96,1]{0,1:T(1,128)} %param.8) | copy-start | bytes 1156
  20.5 9.4 %copy-start.8 = (s32[96]{0:T(128)S(1)}, s32[96]{0:T(128)}, u32[]{:S(2)}) copy-start(s32[96]{0:T(128)} %slot_ref.3) | copy-start | bytes 1156
  20.5 59.5 %all-to-all-start.2 = ((bf16[32,528,128]{2,1,0:T(8,128)(2,1)}), bf16[32,528,128]{2,1,0:T(8,128)(2,1)}, u32[]{:S(2)}, u32[]{:S(2)}) async-start(bf16[32,528,128]{2,1,0:T(8,128)(2,1)} %bitcast.13), calls=%async_computation.3 | async-start | bytes 8650752 | tf_op jit(solution)/shard_map/all_to_all | solution.py:283
  29.9 2.8 %copy-start.3 = (bf16[192,32,512]{2,1,0:T(8,128)(2,1)S(1)}, bf16[192,32,512]{2,1,0:T(8,128)(2,1)}, u32[]{:S(2)}) copy-start(bf16[192,32,512]{2,1,0:T(8,128)(2,1)} %in_ref.1) | copy-start | bytes 18874372
  39.7 2.0 copy-start
  80.1 57.6 %all-to-all-start = ((bf16[32,528,128]{2,1,0:T(8,128)(2,1)}), bf16[32,528,128]{2,1,0:T(8,128)(2,1)}, u32[]{:S(2)}, u32[]{:S(2)}) async-start(bf16[32,528,128]{2,1,0:T(8,128)(2,1)} %bitcast.12), calls=%async_computation | async-start | bytes 8650752 | tf_op jit(solution)/shard_map/all_to_all | solution.py:283
  86.9 63.7 %reduce-scatter.5.cloned.1.call-start = ((), (), s32[]{:S(2)}) async-start(), calls=%async_computation.7 | async-start | bytes 2359296 | tf_op jit(solution)/shard_map/reduce_scatter | solution.py:286
  99.7 148.4 %reduce-scatter.3.cloned.1.call-start = ((), (), s32[]{:S(2)}) async-start(), calls=%async_computation.6 | async-start | bytes 2359296 | tf_op jit(solution)/shard_map/reduce_scatter | solution.py:286
  140.4 10.1 %copy-start.11 = (s32[192,64]{0,1:T(8,128)S(1)}, s32[192,64]{0,1:T(8,128)}, u32[]{:S(2)}) copy-start(s32[192,64]{0,1:T(8,128)} %param.7) | copy-start | bytes 147460
  150.6 97.5 %all-to-all-start.3 = ((bf16[4,4,64,128]{3,2,1,0:T(8,128)(2,1)}), bf16[4,4,64,128]{3,2,1,0:T(8,128)(2,1)S(1)}, u32[]{:S(2)}, u32[]{:S(2)}) async-start(bf16[4,4,64,128]{3,2,1,0:T(8,128)(2,1)} %bitcast.18), calls=%async_computation.5 | async-start | bytes 524288 | tf_op jit(solution)/shard_map/all_to_all | solution.py:288
  156.5 2.8 %copy-start.4 = (bf16[192,32,512]{2,1,0:T(8,128)(2,1)S(1)}, bf16[192,32,512]{2,1,0:T(8,128)(2,1)}, u32[]{:S(2)}) copy-start(bf16[192,32,512]{2,1,0:T(8,128)(2,1)} %in_ref.1) | copy-start | bytes 18874372
  248.1 9.7 %copy-start.9 = (bf16[4,4,64,128]{3,2,1,0:T(8,128)(2,1)}, bf16[4,4,64,128]{3,2,1,0:T(8,128)(2,1)S(1)}, u32[]{:S(2)}) copy-start(bf16[4,4,64,128]{3,2,1,0:T(8,128)(2,1)S(1)} %all-to-all-done.3.second_ref) | copy-start | bytes 786436
  248.1 9.0 %all-to-all-start.1 = ((bf16[4,4,64,128]{3,2,1,0:T(8,128)(2,1)}), bf16[4,4,64,128]{3,2,1,0:T(8,128)(2,1)S(1)}, u32[]{:S(2)}, u32[]{:S(2)}) async-start(bf16[4,4,64,128]{3,2,1,0:T(8,128)(2,1)} %bitcast.19), calls=%async_computation.2 | async-start | bytes 524288 | tf_op jit(solution)/shard_map/all_to_all | solution.py:288
  257.1 0.7 copy-start.10
Sparse Core Ops, SparseCore 0:
  99.8 41.0 reduce-scatter.4
  150.6 40.2 reduce-scatter.2

commit v2 on v1

v2 whole, which is shorter than its diff:
```python
import functools

import jax
import jax.numpy as jnp
from jax import lax
from jax.experimental import pallas as pl
from jax.experimental.pallas import tpu as pltpu
from jax.sharding import Mesh
from jax.sharding import PartitionSpec as P


SHOT_GRP = ("shot_0", "shot_1", "shot_2", "grp")
PLANE = ("shot_0", "shot_2", "grp")
RING = 8
LANES = 128
CAP = 2
PIECES = ((0, 5), (5, 8))


def pack_kernel(
    first, last, home_ref, tile_ref, slot_ref, live_ref, off_ref, *refs
):
    *total_ref, out_ref, data, zeros, flags, meta, meta_low, count = refs[:-3]
    in_sems, out_sem, meta_sem = refs[-3:]
    blocks, size, _ = off_ref.shape
    positions = flags.shape[0]
    quarters = data.shape[0]
    tiles = count.shape[0]
    slots = (last - first) * CAP
    parts = in_sems.shape[0]
    step = blocks // parts
    home = home_ref[0]

    def load(g, q):
        return pltpu.make_async_copy(
            off_ref.at[pl.ds(g * step, step), :, pl.ds(q * LANES, LANES)],
            data.at[q, pl.ds(g * step, step)],
            in_sems.at[g],
        )

    for g in range(parts):
        for q in range(quarters):
            load(g, q).start()
    zeros[...] = jnp.zeros_like(zeros)
    meta[...] = jnp.zeros_like(meta)

    def clear(t, _):
        count[t] = 0
        return 0

    lax.fori_loop(0, tiles, clear, 0)
    live = live_ref[...].astype(jnp.float32)
    twice = jnp.concatenate([live, live], axis=0)
    for low in range(0, positions, LANES):
        high = min(low + LANES, positions)
        turned = twice[:, low:high].T
        odd = lax.broadcasted_iota(jnp.int32, turned.shape, 0) % 2 == 1
        upper = lax.broadcasted_iota(jnp.int32, turned.shape, 1) >= LANES // 2
        flags[low:high, :] = jnp.where(odd == upper, turned, 0.0)

    def place(tile):
        ahead = ((tile // 2) % RING - home + RING) % RING
        near = jnp.minimum(ahead, RING - ahead)
        order = jnp.maximum(7 - 2 * near + (ahead > RING // 2).astype(jnp.int32), 0)
        column = (tile // (2 * RING)) * 2 + tile % 2
        mine = (order >= first) & (order < last)
        return column, (order - first) * CAP, mine

    def target(column, slot):
        return out_ref.at[column, :, pl.ds(pl.multiple_of(slot * size, size), size), :]

    def send(b, _):
        tile = tile_ref[b]
        rank = count[tile]
        count[tile] = rank + 1
        column, slot, mine = place(tile)

        @pl.when(mine)
        def _():
            pltpu.make_async_copy(data.at[:, b], target(column, slot + rank), out_sem).start()
            mark = (slot_ref[b] + 1).astype(jnp.float32)
            row = flags[pl.ds(2 * b, 1), :] + flags[pl.ds(2 * b + 1, 1), :]
            meta[column, pl.ds(slot + rank, 1), :] = row * mark

        return 0

    for g in range(parts):
        for q in range(quarters):
            load(g, q).wait()
        lax.fori_loop(g * step, (g + 1) * step, send, 0)

    def fill(tile, _):
        used = count[tile]
        column, slot, mine = place(tile)
        for rank in range(CAP):

            @pl.when(mine & (used <= rank))
            def _():
                pltpu.make_async_copy(zeros, target(column, slot + rank), out_sem).start()

        return 0

    lax.fori_loop(0, tiles, fill, 0)
    if total_ref:
        rest = total_ref[0][...]
        for term in range(3):
            part = rest.astype(jnp.bfloat16).astype(jnp.float32)
            rest = rest - part
            for column in range(meta.shape[0]):
                meta[column, slots + term : slots + term + 1, :] = part
    meta_low[...] = meta[...].astype(jnp.bfloat16)

    def meta_copy(q):
        return pltpu.make_async_copy(
            meta_low, out_ref.at[:, q, pl.ds(slots * size, meta.shape[1]), :], meta_sem
        )

    for q in range(quarters):
        meta_copy(q).start()
    whole = out_ref.at[:, :, pl.ds(0, slots * size), :]
    pltpu.make_async_copy(whole, whole, out_sem).wait()
    for q in range(quarters):
        meta_copy(q).wait()


def pack(piece, home, tiles, slots, live, blocks, carried, columns, quarters, tile_count):
    first, last = piece
    count, size, _ = blocks.shape
    rows = (last - first) * CAP
    meta_rows = -(-(rows + 3 * len(carried)) // 16) * 16
    vmem = pl.BlockSpec(memory_space=pltpu.VMEM)
    parts = 8
    hbm = pl.BlockSpec(memory_space=pltpu.HBM)
    smem = pl.BlockSpec(memory_space=pltpu.SMEM)
    return pl.pallas_call(
        functools.partial(pack_kernel, first, last),
        out_shape=jax.ShapeDtypeStruct(
            (columns, quarters, rows * size + meta_rows, LANES), jnp.bfloat16
        ),
        in_specs=[smem, smem, smem, vmem, hbm] + [vmem] * len(carried),
        out_specs=hbm,
        scratch_shapes=[
            pltpu.VMEM((quarters, count, size, LANES), jnp.bfloat16),
            pltpu.VMEM((quarters, size, LANES), jnp.bfloat16),
            pltpu.VMEM((2 * count, LANES), jnp.float32),
            pltpu.VMEM((columns, meta_rows, LANES), jnp.float32),
            pltpu.VMEM((columns, meta_rows, LANES), jnp.bfloat16),
            pltpu.SMEM((tile_count,), jnp.int32),
            pltpu.SemaphoreType.DMA((parts,)),
            pltpu.SemaphoreType.DMA,
            pltpu.SemaphoreType.DMA,
        ],
        compiler_params=pltpu.CompilerParams(vmem_limit_bytes=60 * 2**20),
        cost_estimate=pl.CostEstimate(
            flops=8_000_000_000, bytes_accessed=10 * 2**20, transcendentals=0
        ),
    )(home, tiles, slots, live, blocks, *carried)


def stack_kernel(slots, shift, code_ref, w_ref, in_ref, out_ref, acc):
    place, step = pl.program_id(0), pl.program_id(1)
    per, _, _ = in_ref.shape
    traces, lanes = acc.shape[1:]
    angles = traces // 2

    @pl.when(step == 0)
    def _():
        acc[...] = jnp.zeros_like(acc)

    row = lax.broadcasted_iota(jnp.int32, (angles, lanes), 0)
    for u in range(per):
        product = jnp.dot(w_ref[...], in_ref[u], preferred_element_type=jnp.float32)
        for j in range(CAP):
            code = code_ref[(step * per + u) * slots + (shift + place) * CAP + j]
            label = code >> 14
            for half, cut in enumerate(((code >> 7) & 127, code & 127)):
                low = half * angles
                angle = product[j * traces + low : j * traces + low + angles]
                angle = jnp.where(row < cut, angle, 0.0).astype(jnp.bfloat16)
                acc[label, low : low + angles, :] += angle.astype(jnp.float32)

    @pl.when(step == pl.num_programs(1) - 1)
    def _():
        out_ref[0] = acc[: out_ref.shape[1]].astype(out_ref.dtype)


def codes(arrived, slots, size, tile_rows):
    flags = arrived[:, slots * size : slots * size + slots, :].astype(jnp.int32)
    lane = lax.broadcasted_iota(jnp.int32, flags.shape, 2)
    live = (flags > 0).astype(jnp.int32) * jnp.where(lane < LANES // 2, 128, 1)
    label = jnp.where(flags > 0, flags - 1, tile_rows) * 16384
    return jnp.sum(live + jnp.where(lane == 0, label, 0), axis=2).reshape(-1)


def stack(code, weights, arrived, slots, shift, count, tile_rows, traces, dtype):
    sources, _, lanes = arrived.shape
    depth = weights.shape[1]
    per = 16
    return pl.pallas_call(
        functools.partial(stack_kernel, slots, shift),
        grid=(count, sources // per),
        out_shape=jax.ShapeDtypeStruct((count, tile_rows, traces, lanes), dtype),
        in_specs=[
            pl.BlockSpec(memory_space=pltpu.SMEM),
            pl.BlockSpec(weights.shape, lambda d, i: (0, 0)),
            pl.BlockSpec((per, depth, lanes), lambda d, i: (i, shift + d, 0)),
        ],
        out_specs=pl.BlockSpec((1, tile_rows, traces, lanes), lambda d, i: (d, 0, 0, 0)),
        scratch_shapes=[pltpu.VMEM((tile_rows + 1, traces, lanes), jnp.float32)],
        compiler_params=pltpu.CompilerParams(vmem_limit_bytes=16 * 2**20),
        cost_estimate=pl.CostEstimate(
            flops=2_500_000_000 * count, bytes_accessed=2**21 * count, transcendentals=0
        ),
    )(code, weights, arrived)


def join_kernel(half, rising_ref, falling_ref, own_ref, up_ref, down_ref):
    def added(out, passed, own, low, high):
        value = passed.astype(jnp.float32) + own_ref[own, low:high].astype(jnp.float32)
        out[low:high] = value.astype(out.dtype)

    rows = up_ref.shape[0]
    if half:
        middle = rows // 2
        added(up_ref, rising_ref[...], 0, 0, middle)
        up_ref[middle:] = own_ref[0, middle:]
        down_ref[:middle] = own_ref[1, :middle]
        added(down_ref, falling_ref[...], 1, middle, rows)
    else:
        added(up_ref, rising_ref[...], 0, 0, rows)
        added(down_ref, falling_ref[...], 1, 0, rows)


def join(half, rising, falling, own, pair):
    vmem = pl.BlockSpec(memory_space=pltpu.VMEM)
    shape = jax.ShapeDtypeStruct(own.shape[1:], own.dtype)
    block = (2,) + own.shape[1:]
    return pl.pallas_call(
        functools.partial(join_kernel, half),
        grid=(1,),
        out_shape=(shape, shape),
        in_specs=[vmem, vmem, pl.BlockSpec(block, lambda i: (pair, 0, 0, 0))],
        out_specs=(vmem, vmem),
        compiler_params=pltpu.CompilerParams(vmem_limit_bytes=16 * 2**20),
        cost_estimate=pl.CostEstimate(
            flops=1_000_000_000, bytes_accessed=3 * 2**20, transcendentals=0
        ),
        name="join",
    )(rising, falling, own)


def moments_kernel(group, cut_ref, w_ref, in_ref, out_ref):
    step = pl.program_id(0)
    angles, lanes = out_ref.shape
    count, hh, depth = in_ref.shape

    @pl.when(step == 0)
    def _():
        out_ref[...] = jnp.zeros_like(out_ref)

    row = lax.broadcasted_iota(jnp.int32, (angles, lanes), 0)
    total = out_ref[...]
    for part in range(count // group):
        gathers = in_ref[part * group : (part + 1) * group].reshape(group * hh, depth)
        square = None
        for q in range(depth // lanes):
            product = jnp.dot(
                w_ref[...],
                gathers[:, q * lanes : (q + 1) * lanes],
                preferred_element_type=jnp.float32,
            )
            product = product.astype(jnp.bfloat16).astype(jnp.float32)
            square = product * product if square is None else square + product * product
        for j in range(group):
            cut = cut_ref[step * count + part * group + j]
            total += jnp.where(row < cut, square[j * angles : (j + 1) * angles], 0.0)
    out_ref[...] = total


def moments(offsets, weights, live):
    positions, hh, depth = offsets.shape
    angles = live.shape[1]
    per = 16
    squares = pl.pallas_call(
        functools.partial(moments_kernel, weights.shape[0] // angles),
        grid=(positions // per,),
        out_shape=jax.ShapeDtypeStruct((angles, LANES), jnp.float32),
        in_specs=[
            pl.BlockSpec(memory_space=pltpu.SMEM),
            pl.BlockSpec(weights.shape, lambda i: (0, 0)),
            pl.BlockSpec((per, hh, depth), lambda i: (i, 0, 0)),
        ],
        out_specs=pl.BlockSpec((angles, LANES), lambda i: (0, 0)),
        compiler_params=pltpu.CompilerParams(vmem_limit_bytes=60 * 2**20),
        cost_estimate=pl.CostEstimate(
            flops=10_000_000_000, bytes_accessed=6 * 2**20, transcendentals=0
        ),
        name="moments",
    )(jnp.sum(live, axis=1), weights, offsets)
    return jnp.sum(squares, axis=1), jnp.sum(live, axis=0).astype(jnp.float32)


def finish_kernel(in_ref, out_ref):
    quarters, images, _, lanes = in_ref.shape
    for q in range(quarters):
        for k in range(images):
            out_ref[k, :, q * lanes : (q + 1) * lanes] = in_ref[q, k]


def finish(swapped):
    quarters, images, traces, lanes = swapped.shape
    vmem = pl.BlockSpec(memory_space=pltpu.VMEM)
    return pl.pallas_call(
        finish_kernel,
        out_shape=jax.ShapeDtypeStruct((images, traces, quarters * lanes), swapped.dtype),
        in_specs=[vmem],
        out_specs=vmem,
        name="finish",
    )(swapped)


def work(offsets, slant_weights, live, block_tile, image_slot):
    block_count = block_tile.shape[0]
    _, hh, depth = offsets.shape
    angles = slant_weights.shape[0]
    traces = 2 * angles
    size = 2 * hh
    tile_count = lax.axis_size(("shot_0", "shot_1", "shot_2"))
    columns = lax.axis_size(("shot_0", "shot_2"))
    quarters = lax.axis_size("grp")
    tile_rows = 4 * quarters
    blocks = offsets.reshape(block_count, size, depth)
    tiles = block_tile[:, 0]
    home = lax.axis_index("shot_1").reshape(1)
    up = [(i, (i + 1) % RING) for i in range(RING)]
    down = [(i, (i - 1) % RING) for i in range(RING)]

    def diagonal(count):
        return jnp.kron(jnp.eye(count, dtype=jnp.bfloat16), slant_weights)

    squares, counts = moments(offsets, diagonal(8), live)
    totals = jnp.concatenate([squares, counts])
    totals = lax.psum(totals, "shot_1")[None, :]

    pair = diagonal(2 * CAP)
    arrived, code = [], []
    for n, piece in enumerate(PIECES):
        slots = (piece[1] - piece[0]) * CAP
        carried = [totals] if n else []
        sent = pack(
            piece, home, tiles, image_slot, live.T, blocks, carried,
            columns, quarters, tile_count,
        )
        sent = sent.reshape((columns * quarters,) + sent.shape[2:])
        arrived.append(lax.all_to_all(sent, PLANE, 0, 0, tiled=True))
        code.append(codes(arrived[-1], slots, size, tile_rows))
    low = slots * (size + 1)
    totals = jnp.sum(arrived[1][:, low : low + 3].astype(jnp.float32), axis=(0, 1))
    gain = lax.rsqrt(totals[:angles] / (depth * totals[angles:]) + 1e-06)

    def stacked(n, shift, count, dtype):
        slots = (PIECES[n][1] - PIECES[n][0]) * CAP
        return stack(
            code[n], pair, arrived[n], slots, shift, count, tile_rows, traces, dtype
        )

    far = stacked(0, 0, 1, jnp.bfloat16)[0]
    rising = lax.ppermute(far[: tile_rows // 2], "shot_1", up)
    falling = lax.ppermute(far[tile_rows // 2 :], "shot_1", down)
    middle = stacked(0, 1, 4, jnp.bfloat16)
    near = stacked(1, 0, 2, jnp.bfloat16)
    for n, (parts, at) in enumerate(((middle, 0), (middle, 1), (near, 0))):
        rising, falling = join(n == 0, rising, falling, parts, at)
        rising = lax.ppermute(rising, "shot_1", up)
        falling = lax.ppermute(falling, "shot_1", down)
    own = stacked(1, 2, 1, jnp.float32)[0]
    total = own + rising.astype(jnp.float32) + falling.astype(jnp.float32)
    image = (total * jnp.tile(gain, 2)[None, :, None]).astype(jnp.bfloat16)
    image = image.reshape(quarters, 4, traces, LANES)
    swapped = lax.all_to_all(image, "grp", 0, 0, tiled=True)
    return finish(swapped)


def solution(mesh):
    torus = Mesh(
        mesh.devices.reshape(4, RING, 2, mesh.shape["grp"]),
        ("shot_0", "shot_1", "shot_2", "grp"),
    )
    return jax.shard_map(
        work,
        mesh=torus,
        in_specs=(P(SHOT_GRP, None, None), P(), P(SHOT_GRP, None), P(SHOT_GRP, None), P(SHOT_GRP)),
        out_specs=P(SHOT_GRP, None, None),
        check_vma=False,
    )
```

time: 268 us -> 167 us (0.62)
  blocking collectives: 79.3 us -> 30.3 us
  waiting for transfers between devices: 81.8 us -> 48.2 us
  local copies, waits for them, and re-layouts: 15.9 us -> 1.77 us
  between operations: 13.6 us -> 0.21 us
  starting transfers between devices: 24.9 us -> 28.9 us
  Pallas kernels: 45.4 us -> 48.9 us
    psum x1, blocking collectives: 79.3 us -> 18.3 us  [work(): totals = lax.psum(totals, 'shot_1')[None, :]]
    all_to_all x4 -> x2, waiting for transfers between devices: 81.8 us -> 25.4 us  [work(): arrived.append(lax.all_to_all(sent, PLANE, 0, 0, tiled=True))]
    ppermute x0 -> x8, waiting for transfers between devices: none -> 22.8 us  [the longest x3 22.8 us: work(): rising = lax.ppermute(rising, 'shot_1', up)]
    unnamed x27 -> x4, local copies, waits for them, and re-layouts: 14.6 us -> 0.01 us
    ppermute x0 -> x8, starting transfers between devices: none -> 13.8 us  [the longest x3 6.94 us: work(): falling = lax.ppermute(falling, 'shot_1', down)]
    all_to_all x0 -> x1, blocking collectives: none -> 12 us  [work(): swapped = lax.all_to_all(image, 'grp', 0, 0, tiled=True)]
    all_to_all x4 -> x2, starting transfers between devices: 24.8 us -> 15.1 us  [work(): arrived.append(lax.all_to_all(sent, PLANE, 0, 0, tiled=True))]
    pallas_call x6 -> x11, Pallas kernels: 45.4 us -> 48.9 us  [the longest x2 16.1 us: pack(): pl.pallas_call(functools.partial(pack_kernel, first, last), out_shape=jax...]
  transfers between devices with their start and end apart: 6 -> 10, of which waited for: 3 -> 5; matrix products, arithmetic and copies ran while one was open for 2% -> 4% of each run, Pallas kernels for 14% -> 22%
where the time goes in v2:
time: 167 us; the launch traced here: 164 us
  Pallas kernels  48.9 us (29%)
  waiting for transfers between devices  48.2 us (29%)
  blocking collectives  30.3 us (18%)
  starting transfers between devices  28.9 us (17%)
  other arithmetic  5.51 us (3%)
  local copies, waits for them, and re-layouts  1.77 us (1%)
    all_to_all x2, waiting for transfers between devices, work(): arrived.append(lax.all_to_all(sent, PLANE, 0, 0, tiled=True))  25.4 us
    ppermute x3, waiting for transfers between devices, work(): rising = lax.ppermute(rising, 'shot_1', up)  22.8 us
    psum x1, blocking collectives, work(): totals = lax.psum(totals, 'shot_1')[None, :]  18.3 us
    pallas_call x2, Pallas kernels, pack(): pl.pallas_call(functools.partial(pack_kernel, first, last), out_shape=jax...  16.1 us
    all_to_all x2, starting transfers between devices, work(): arrived.append(lax.all_to_all(sent, PLANE, 0, 0, tiled=True))  15.1 us
    pallas_call x4, Pallas kernels, stack(): pl.pallas_call(functools.partial(stack_kernel, slots, shift), grid=(count...  15 us
    pallas_call x1, Pallas kernels, moments(): pl.pallas_call(functools.partial(moments_kernel, weights.shape[0] // angl...  12.3 us
    all_to_all x1, blocking collectives, work(): swapped = lax.all_to_all(image, 'grp', 0, 0, tiled=True)  12 us
  transfers between devices with their start and end apart: 10, of which 5 were waited for; matrix products, arithmetic and copies ran while one was open for 4% of the time, Pallas kernels for 22%

profile of v2, /device:TPU:1, one launch (start us, length us, event | category | flops | bytes accessed | tf_op | source)
XLA Modules:
  0.0 163.9 jit_solution(11567763091544595965)
XLA Ops:
  0.0 8.1 %shard_map.57 = bf16[8,4,656,128]{3,2,1,0:T(8,128)(2,1)} custom-call(s32[1]{0:T(128)} %bitcast.home_ref, s32[96]{0:T(128)} %bitcast.34, s32[96]{0:T(128)} %slot_ref.3, s32[64,192]{1,0:T(8,128)} %bitcast.30, bf16[96,64,512]{2,1,0:T(8,128)(2,1)} %bitcast.32), custom_call_target="tpu_custom_call" | custom-call | flops 8000000000 | bytes 10485760 | tf_op jit(solution)/shard_map/pallas_call | solution.py:135
  8.2 8.7 %all-to-all-start.1 = ((bf16[32,656,128]{2,1,0:T(8,128)(2,1)}), bf16[32,656,128]{2,1,0:T(8,128)(2,1)}, u32[]{:S(2)}, u32[]{:S(2)}) async-start(bf16[32,656,128]{2,1,0:T(8,128)(2,1)} %bitcast.27), calls=%async_computation.1 | async-start | bytes 10747904 | tf_op jit(solution)/shard_map/all_to_all | solution.py:355
  17.0 0.3 mul.85
  17.3 0.8 copy.8.w_ref
  18.2 0.6 fusion.15
  18.7 12.3 %moments.1 = f32[64,128]{1,0:T(8,128)} custom-call(s32[192]{0:T(256)} %get-tuple-element.17.cut_ref, bf16[512,256]{1,0:T(8,128)(2,1)} %copy.8.w_ref, bf16[192,32,512]{2,1,0:T(8,128)(2,1)} %in_ref.1), custom_call_target="tpu_custom_call" | custom-call | flops 10000000000 | bytes 6291456 | tf_op jit(solution)/shard_map/moments/pallas_call | solution.py:284
  31.0 0.9 reduce_sum.55
  31.9 18.3 %psum.7.refs_0_ = f32[1,128]{1,0:T(1,128)} all-reduce(f32[1,128]{1,0:T(1,128)S(1)} %maximum_bitcast_fusion), channel_id=1, replica_groups=mesh['shot_0'=4,'shot_1'=8,'shot_2'=2,'grp'=4] {'shot_1'}, use_global_device_ids=true, to_apply=%region_3.4 | all-reduce | flops 128 | bytes 1024 | tf_op jit(solution)/shard_map/psum | solution.py:343
  50.3 7.9 %shard_map.55 = bf16[8,4,400,128]{3,2,1,0:T(8,128)(2,1)} custom-call(s32[1]{0:T(128)} %bitcast.home_ref, s32[96]{0:T(128)} %bitcast.35, s32[96]{0:T(128)} %slot_ref.3, s32[64,192]{1,0:T(8,128)} %bitcast.31, bf16[96,64,512]{2,1,0:T(8,128)(2,1)} %bitcast.33, f32[1,128]{1,0:T(1,128)} %psum.7.refs_0_), custom_call_target="tpu_custom_call" | custom-call | flops 8000000000 | bytes 10485760 | tf_op jit(solution)/shard_map/pallas_call | solution.py:135
  58.2 22.0 %all-to-all-done.1.in_ref = bf16[32,656,128]{2,1,0:T(8,128)(2,1)} async-done(((bf16[32,656,128]{2,1,0:T(8,128)(2,1)}), bf16[32,656,128]{2,1,0:T(8,128)(2,1)}, u32[]{:S(2)}, u32[]{:S(2)}) %all-to-all-start.1) | async-done | bytes 5373984 | tf_op jit(solution)/shard_map/all_to_all | solution.py:355
  80.2 6.4 %all-to-all-start = ((bf16[32,400,128]{2,1,0:T(8,128)(2,1)}), bf16[32,400,128]{2,1,0:T(8,128)(2,1)S(1)}, u32[]{:S(2)}, u32[]{:S(2)}) async-start(bf16[32,400,128]{2,1,0:T(8,128)(2,1)} %bitcast.28), calls=%async_computation | async-start | bytes 6553600 | tf_op jit(solution)/shard_map/all_to_all | solution.py:355
  87.0 1.5 fusion.7
  88.7 2.3 %shard_map.58 = bf16[1,16,128,128]{3,2,1,0:T(8,128)(2,1)S(1)} custom-call(s32[320]{0:T(512)S(1)} %reshape.57.code_ref, bf16[256,128]{1,0:T(8,128)(2,1)S(1)} %copy.9.w_ref, bf16[32,656,128]{2,1,0:T(8,128)(2,1)} %all-to-all-done.1.in_ref), custom_call_target="tpu_custom_call" | custom-call | flops 2500000000 | bytes 2097152 | tf_op jit(solution)/shard_map/pallas_call | solution.py:199
  91.0 1.9 %collective-permute-start = (bf16[8,128,128]{2,1,0:T(8,128)(2,1)S(1)}, bf16[8,128,128]{2,1,0:T(8,128)(2,1)S(1)}, u32[]{:S(2)}, u32[]{:S(2)}) collective-permute-start(bf16[8,128,128]{2,1,0:T(8,128)(2,1)S(1)} %get-tuple-element.20), channel_id=1, source_target_pairs={{0,8},{8,16},{16,24},{24,32},{32,40},{40,48},{48,56},{56,0},{1,9},... | collective-permute-start | bytes 786440 | tf_op jit(solution)/shard_map/ppermute | solution.py:368
  92.9 3.9 %collective-permute-start.1 = (bf16[8,128,128]{2,1,0:T(8,128)(2,1)S(1)}, bf16[8,128,128]{2,1,0:T(8,128)(2,1)S(1)}, u32[]{:S(2)}, u32[]{:S(2)}) collective-permute-start(bf16[8,128,128]{2,1,0:T(8,128)(2,1)S(1)} %get-tuple-element.19), channel_id=1, source_target_pairs={{0,56},{8,0},{16,8},{24,16},{32,24},{40,32},{48,40},{56,48},{1,57}... | collective-permute-start | bytes 786440 | tf_op jit(solution)/shard_map/ppermute | solution.py:369
  96.8 7.4 %shard_map.59.own_ref = bf16[4,16,128,128]{3,2,1,0:T(8,128)(2,1)S(1)} custom-call(s32[320]{0:T(512)S(1)} %reshape.57.code_ref, bf16[256,128]{1,0:T(8,128)(2,1)S(1)} %copy.9.w_ref, bf16[32,656,128]{2,1,0:T(8,128)(2,1)} %all-to-all-done.1.in_ref), custom_call_target="tpu_custom_call" | custom-call | flops 10000000000 | bytes 8388608 | tf_op jit(solution)/shard_map/pallas_call | solution.py:199
  104.4 2.7 %collective-permute-start.3 = (bf16[16,128,128]{2,1,0:T(8,128)(2,1)S(1)}, bf16[16,128,128]{2,1,0:T(8,128)(2,1)S(1)}, u32[]{:S(2)}, u32[]{:S(2)}) collective-permute-start(bf16[16,128,128]{2,1,0:T(8,128)(2,1)S(1)} %get-tuple-element.12), channel_id=1, source_target_pairs={{0,56},{8,0},{16,8},{24,16},{32,24},{40,32},{48,40},{56,48},{1,57}... | collective-permute-start | bytes 1572872 | tf_op jit(solution)/shard_map/ppermute | solution.py:375
  107.1 11.5 %collective-permute-done.2.rising_ref = bf16[16,128,128]{2,1,0:T(8,128)(2,1)S(1)} collective-permute-done((bf16[16,128,128]{2,1,0:T(8,128)(2,1)S(1)}, bf16[16,128,128]{2,1,0:T(8,128)(2,1)S(1)}, u32[]{:S(2)}, u32[]{:S(2)}) %collective-permute-start.2) | collective-permute-done | bytes 524320 | tf_op jit(solution)/shard_map/ppermute | solution.py:374
  118.6 1.2 join.4
  119.8 2.7 %collective-permute-start.5 = (bf16[16,128,128]{2,1,0:T(8,128)(2,1)}, bf16[16,128,128]{2,1,0:T(8,128)(2,1)}, u32[]{:S(2)}, u32[]{:S(2)}) collective-permute-start(bf16[16,128,128]{2,1,0:T(8,128)(2,1)} %get-tuple-element.14), channel_id=1, source_target_pairs={{0,56},{8,0},{16,8},{24,16},{32,24},{40,32},{48,40},{56,48},{1,57}... | collective-permute-start | bytes 1572872 | tf_op jit(solution)/shard_map/ppermute | solution.py:375
  122.4 3.4 %all-to-all-done.in_ref = bf16[32,400,128]{2,1,0:T(8,128)(2,1)S(1)} async-done(((bf16[32,400,128]{2,1,0:T(8,128)(2,1)}), bf16[32,400,128]{2,1,0:T(8,128)(2,1)S(1)}, u32[]{:S(2)}, u32[]{:S(2)}) %all-to-all-start) | async-done | bytes 3276832 | tf_op jit(solution)/shard_map/all_to_all | solution.py:355
  125.9 0.6 fusion.12
  126.6 3.4 %shard_map.60.own_ref = bf16[2,16,128,128]{3,2,1,0:T(8,128)(2,1)S(1)} custom-call(s32[192]{0:T(256)S(1)} %reshape.55.code_ref, bf16[256,128]{1,0:T(8,128)(2,1)S(1)} %copy.9.w_ref, bf16[32,400,128]{2,1,0:T(8,128)(2,1)S(1)} %all-to-all-done.in_ref), custom_call_target="tpu_custom_call" | custom-call | flops 5000000000 | bytes 4194304 | tf_op jit(solution)/shard_map/pallas_call | solution.py:199
  130.0 3.4 %collective-permute-done.4.rising_ref = bf16[16,128,128]{2,1,0:T(8,128)(2,1)} collective-permute-done((bf16[16,128,128]{2,1,0:T(8,128)(2,1)}, bf16[16,128,128]{2,1,0:T(8,128)(2,1)}, u32[]{:S(2)}, u32[]{:S(2)}) %collective-permute-start.4) | collective-permute-done | bytes 524320 | tf_op jit(solution)/shard_map/ppermute | solution.py:374
  133.4 2.3 %join.5 = (bf16[16,128,128]{2,1,0:T(8,128)(2,1)}, bf16[16,128,128]{2,1,0:T(8,128)(2,1)}) custom-call(bf16[16,128,128]{2,1,0:T(8,128)(2,1)} %collective-permute-done.4.rising_ref, bf16[16,128,128]{2,1,0:T(8,128)(2,1)} %collective-permute-done.5.falling_ref, bf16[2,16,128,128]{3,2,1,0:T(8,128)(2,1)S(1)} %shard_map.60.own_ref), custom_call_target="tpu_custom_call" | custom-call | flops 1000000000 | bytes 3145728 | tf_op jit(solution)/shard_map/join/pallas_call | solution.py:238
  135.7 1.1 collective-permute-start.6
  136.8 1.6 collective-permute-start.7
  138.6 1.9 %shard_map.56 = f32[1,16,128,128]{3,2,1,0:T(8,128)S(1)} custom-call(s32[192]{0:T(256)S(1)} %reshape.55.code_ref, bf16[256,128]{1,0:T(8,128)(2,1)S(1)} %copy.9.w_ref, bf16[32,400,128]{2,1,0:T(8,128)(2,1)S(1)} %all-to-all-done.in_ref), custom_call_target="tpu_custom_call" | custom-call | flops 2500000000 | bytes 2097152 | tf_op jit(solution)/shard_map/pallas_call | solution.py:199
  140.5 8.0 %collective-permute-done.6 = bf16[16,128,128]{2,1,0:T(8,128)(2,1)} collective-permute-done((bf16[16,128,128]{2,1,0:T(8,128)(2,1)}, bf16[16,128,128]{2,1,0:T(8,128)(2,1)}, u32[]{:S(2)}, u32[]{:S(2)}) %collective-permute-start.6) | collective-permute-done | bytes 524320 | tf_op jit(solution)/shard_map/ppermute | solution.py:374
  148.5 1.5 fusion.2
  150.0 12.0 %all_to_all.15.in_ref = bf16[4,4,128,128]{3,2,1,0:T(8,128)(2,1)} all-to-all(bf16[4,4,128,128]{3,2,1,0:T(8,128)(2,1)S(1)} %bitcast.29), channel_id=1, replica_groups=mesh['shot_0'=4,'shot_1'=8,'shot_2'=2,'grp'=4] {'grp'}, dimensions={0} | all-to-all | bytes 1048576 | tf_op jit(solution)/shard_map/all_to_all | solution.py:380
  161.9 1.9 %finish.1 = bf16[4,128,512]{2,1,0:T(8,128)(2,1)} custom-call(bf16[4,4,128,128]{3,2,1,0:T(8,128)(2,1)} %all_to_all.15.in_ref), custom_call_target="tpu_custom_call" | custom-call | tf_op jit(solution)/shard_map/finish/pallas_call | solution.py:313
  (29 shorter events, 1.3 us)
Async XLA Ops:
  8.1 8.7 %copy-start.1 = (bf16[64,32]{0,1:T(8,128)(2,1)S(1)}, bf16[64,32]{0,1:T(8,128)(2,1)}, u32[]{:S(2)}) copy-start(bf16[64,32]{0,1:T(8,128)(2,1)} %param.6) | copy-start | bytes 12292
  8.2 10.0 %copy-start = (s32[192,64]{0,1:T(8,128)S(1)}, s32[192,64]{0,1:T(8,128)}, u32[]{:S(2)}) copy-start(s32[192,64]{0,1:T(8,128)} %param.7) | copy-start | bytes 147460
  8.2 72.0 %all-to-all-start.1 = ((bf16[32,656,128]{2,1,0:T(8,128)(2,1)}), bf16[32,656,128]{2,1,0:T(8,128)(2,1)}, u32[]{:S(2)}, u32[]{:S(2)}) async-start(bf16[32,656,128]{2,1,0:T(8,128)(2,1)} %bitcast.27), calls=%async_computation.1 | async-start | bytes 10747904 | tf_op jit(solution)/shard_map/all_to_all | solution.py:355
  80.2 45.7 %all-to-all-start = ((bf16[32,400,128]{2,1,0:T(8,128)(2,1)}), bf16[32,400,128]{2,1,0:T(8,128)(2,1)S(1)}, u32[]{:S(2)}, u32[]{:S(2)}) async-start(bf16[32,400,128]{2,1,0:T(8,128)(2,1)} %bitcast.28), calls=%async_computation | async-start | bytes 6553600 | tf_op jit(solution)/shard_map/all_to_all | solution.py:355
  91.0 13.1 %collective-permute-start = (bf16[8,128,128]{2,1,0:T(8,128)(2,1)S(1)}, bf16[8,128,128]{2,1,0:T(8,128)(2,1)S(1)}, u32[]{:S(2)}, u32[]{:S(2)}) collective-permute-start(bf16[8,128,128]{2,1,0:T(8,128)(2,1)S(1)} %get-tuple-element.20), channel_id=1, source_target_pairs={{0,8},{8,16},{16,24},{24,32},{32,40},{40,48},{48,56},{56,0},{1,9},... | collective-permute-start | bytes 786440 | tf_op jit(solution)/shard_map/ppermute | solution.py:368
  92.9 11.3 %collective-permute-start.1 = (bf16[8,128,128]{2,1,0:T(8,128)(2,1)S(1)}, bf16[8,128,128]{2,1,0:T(8,128)(2,1)S(1)}, u32[]{:S(2)}, u32[]{:S(2)}) collective-permute-start(bf16[8,128,128]{2,1,0:T(8,128)(2,1)S(1)} %get-tuple-element.19), channel_id=1, source_target_pairs={{0,56},{8,0},{16,8},{24,16},{32,24},{40,32},{48,40},{56,48},{1,57}... | collective-permute-start | bytes 786440 | tf_op jit(solution)/shard_map/ppermute | solution.py:369
  104.3 14.3 %collective-permute-start.2 = (bf16[16,128,128]{2,1,0:T(8,128)(2,1)S(1)}, bf16[16,128,128]{2,1,0:T(8,128)(2,1)S(1)}, u32[]{:S(2)}, u32[]{:S(2)}) collective-permute-start(bf16[16,128,128]{2,1,0:T(8,128)(2,1)S(1)} %get-tuple-element.11), channel_id=1, source_target_pairs={{0,8},{8,16},{16,24},{24,32},{32,40},{40,48},{48,56},{56,0},{1,9},... | collective-permute-start | bytes 1572872 | tf_op jit(solution)/shard_map/ppermute | solution.py:374
  104.4 14.2 %collective-permute-start.3 = (bf16[16,128,128]{2,1,0:T(8,128)(2,1)S(1)}, bf16[16,128,128]{2,1,0:T(8,128)(2,1)S(1)}, u32[]{:S(2)}, u32[]{:S(2)}) collective-permute-start(bf16[16,128,128]{2,1,0:T(8,128)(2,1)S(1)} %get-tuple-element.12), channel_id=1, source_target_pairs={{0,56},{8,0},{16,8},{24,16},{32,24},{40,32},{48,40},{56,48},{1,57}... | collective-permute-start | bytes 1572872 | tf_op jit(solution)/shard_map/ppermute | solution.py:375
  119.8 13.6 %collective-permute-start.4 = (bf16[16,128,128]{2,1,0:T(8,128)(2,1)}, bf16[16,128,128]{2,1,0:T(8,128)(2,1)}, u32[]{:S(2)}, u32[]{:S(2)}) collective-permute-start(bf16[16,128,128]{2,1,0:T(8,128)(2,1)} %get-tuple-element.13), channel_id=1, source_target_pairs={{0,8},{8,16},{16,24},{24,32},{32,40},{40,48},{48,56},{56,0},{1,9},... | collective-permute-start | bytes 1572872 | tf_op jit(solution)/shard_map/ppermute | solution.py:374
  119.8 13.6 %collective-permute-start.5 = (bf16[16,128,128]{2,1,0:T(8,128)(2,1)}, bf16[16,128,128]{2,1,0:T(8,128)(2,1)}, u32[]{:S(2)}, u32[]{:S(2)}) collective-permute-start(bf16[16,128,128]{2,1,0:T(8,128)(2,1)} %get-tuple-element.14), channel_id=1, source_target_pairs={{0,56},{8,0},{16,8},{24,16},{32,24},{40,32},{48,40},{56,48},{1,57}... | collective-permute-start | bytes 1572872 | tf_op jit(solution)/shard_map/ppermute | solution.py:375
  135.7 12.8 %collective-permute-start.6 = (bf16[16,128,128]{2,1,0:T(8,128)(2,1)}, bf16[16,128,128]{2,1,0:T(8,128)(2,1)}, u32[]{:S(2)}, u32[]{:S(2)}) collective-permute-start(bf16[16,128,128]{2,1,0:T(8,128)(2,1)} %get-tuple-element.15), channel_id=1, source_target_pairs={{0,8},{8,16},{16,24},{24,32},{32,40},{40,48},{48,56},{56,0},{1,9},... | collective-permute-start | bytes 1572872 | tf_op jit(solution)/shard_map/ppermute | solution.py:374
  136.8 11.7 %collective-permute-start.7 = (bf16[16,128,128]{2,1,0:T(8,128)(2,1)}, bf16[16,128,128]{2,1,0:T(8,128)(2,1)}, u32[]{:S(2)}, u32[]{:S(2)}) collective-permute-start(bf16[16,128,128]{2,1,0:T(8,128)(2,1)} %get-tuple-element.16), channel_id=1, source_target_pairs={{0,56},{8,0},{16,8},{24,16},{32,24},{40,32},{48,40},{56,48},{1,57}... | collective-permute-start | bytes 1572872 | tf_op jit(solution)/shard_map/ppermute | solution.py:375

commit v3 on v2

--- a/solution.py
+++ b/solution.py
@@ -20,7 +20,7 @@
 def pack_kernel(
     first, last, home_ref, tile_ref, slot_ref, live_ref, off_ref, *refs
 ):
-    *total_ref, out_ref, data, zeros, flags, meta, meta_low, count = refs[:-3]
+    *total_ref, out_ref, data, zeros, flags, meta, meta_low, count, goal = refs[:-3]
     in_sems, out_sem, meta_sem = refs[-3:]
     blocks, size, _ = off_ref.shape
     positions = flags.shape[0]
@@ -48,7 +48,7 @@
         count[t] = 0
         return 0
 
-    lax.fori_loop(0, tiles, clear, 0)
+    lax.fori_loop(0, tiles, clear, 0, unroll=8)
     live = live_ref[...].astype(jnp.float32)
     twice = jnp.concatenate([live, live], axis=0)
     for low in range(0, positions, LANES):
@@ -69,25 +69,22 @@
     def target(column, slot):
         return out_ref.at[column, :, pl.ds(pl.multiple_of(slot * size, size), size), :]
 
-    def send(b, _):
+    def plan(b, _):
         tile = tile_ref[b]
         rank = count[tile]
         count[tile] = rank + 1
         column, slot, mine = place(tile)
+        goal[b] = jnp.where(mine, column * slots + slot + rank, -1)
 
         @pl.when(mine)
         def _():
-            pltpu.make_async_copy(data.at[:, b], target(column, slot + rank), out_sem).start()
             mark = (slot_ref[b] + 1).astype(jnp.float32)
             row = flags[pl.ds(2 * b, 1), :] + flags[pl.ds(2 * b + 1, 1), :]
             meta[column, pl.ds(slot + rank, 1), :] = row * mark
 
         return 0
 
-    for g in range(parts):
-        for q in range(quarters):
-            load(g, q).wait()
-        lax.fori_loop(g * step, (g + 1) * step, send, 0)
+    lax.fori_loop(0, blocks, plan, 0, unroll=4)
 
     def fill(tile, _):
         used = count[tile]
@@ -100,7 +97,7 @@
 
         return 0
 
-    lax.fori_loop(0, tiles, fill, 0)
+    lax.fori_loop(0, tiles, fill, 0, unroll=4)
     if total_ref:
         rest = total_ref[0][...]
         for term in range(3):
@@ -110,13 +107,29 @@
                 meta[column, slots + term : slots + term + 1, :] = part
     meta_low[...] = meta[...].astype(jnp.bfloat16)
 
+    def send(b, _):
+        at = goal[b]
+
+        @pl.when(at >= 0)
+        def _():
+            pltpu.make_async_copy(
+                data.at[:, b], target(at // slots, at % slots), out_sem
+            ).start()
+
+        return 0
+
     def meta_copy(q):
         return pltpu.make_async_copy(
             meta_low, out_ref.at[:, q, pl.ds(slots * size, meta.shape[1]), :], meta_sem
         )
 
-    for q in range(quarters):
-        meta_copy(q).start()
+    for g in range(parts):
+        for q in range(quarters):
+            load(g, q).wait()
+        lax.fori_loop(g * step, (g + 1) * step, send, 0, unroll=4)
+        if g == parts // 2:
+            for q in range(quarters):
+                meta_copy(q).start()
     whole = out_ref.at[:, :, pl.ds(0, slots * size), :]
     pltpu.make_async_copy(whole, whole, out_sem).wait()
     for q in range(quarters):
@@ -146,6 +159,7 @@
             pltpu.VMEM((columns, meta_rows, LANES), jnp.float32),
             pltpu.VMEM((columns, meta_rows, LANES), jnp.bfloat16),
             pltpu.SMEM((tile_count,), jnp.int32),
+            pltpu.SMEM((count,), jnp.int32),
             pltpu.SemaphoreType.DMA((parts,)),
             pltpu.SemaphoreType.DMA,
             pltpu.SemaphoreType.DMA,
@@ -157,15 +171,29 @@
     )(home, tiles, slots, live, blocks, *carried)
 
 
-def stack_kernel(slots, shift, code_ref, w_ref, in_ref, out_ref, acc):
+def stack_kernel(slots, shift, joined, code_ref, w_ref, in_ref, *refs):
+    acc = refs[-1]
     place, step = pl.program_id(0), pl.program_id(1)
     per, _, _ = in_ref.shape
     traces, lanes = acc.shape[1:]
     angles = traces // 2
 
-    @pl.when(step == 0)
-    def _():
-        acc[...] = jnp.zeros_like(acc)
+    if joined:
+        passed = (refs[0:2], refs[2:4])
+        images = passed[0][0].shape[0]
+        for at in range(2):
+
+            @pl.when((step == 0) & (place == at))
+            def _():
+                for half in range(2):
+                    acc[:images, half * angles : (half + 1) * angles] = passed[at][half][
+                        ...
+                    ].astype(jnp.float32)
+    else:
+
+        @pl.when(step == 0)
+        def _():
+            acc[...] = jnp.zeros_like(acc)
 
     row = lax.broadcasted_iota(jnp.int32, (angles, lanes), 0)
     for u in range(per):
@@ -179,9 +207,15 @@
                 angle = jnp.where(row < cut, angle, 0.0).astype(jnp.bfloat16)
                 acc[label, low : low + angles, :] += angle.astype(jnp.float32)
 
-    @pl.when(step == pl.num_programs(1) - 1)
-    def _():
-        out_ref[0] = acc[: out_ref.shape[1]].astype(out_ref.dtype)
+    outs = (refs[4:6], refs[6:8]) if joined else (refs[0:2],)
+    for at, pair in enumerate(outs):
+
+        @pl.when((step == pl.num_programs(1) - 1) & ((place == at) | (not joined)))
+        def _():
+            for half, ref in enumerate(pair):
+                images = ref.shape[-3]
+                value = acc[:images, half * angles : (half + 1) * angles]
+                ref[...] = value.astype(ref.dtype).reshape(ref.shape)
 
 
 def codes(arrived, slots, size, tile_rows):
@@ -192,61 +226,82 @@
     return jnp.sum(live + jnp.where(lane == 0, label, 0), axis=2).reshape(-1)
 
 
-def stack(code, weights, arrived, slots, shift, count, tile_rows, traces, dtype):
+def stack(code, weights, arrived, slots, shift, count, tile_rows, traces, dtype, passed=()):
     sources, _, lanes = arrived.shape
     depth = weights.shape[1]
     per = 16
+    half = (tile_rows, traces // 2, lanes)
+    shape = jax.ShapeDtypeStruct((count,) + half, dtype)
+    spec = pl.BlockSpec((1,) + half, lambda d, i: (d, 0, 0, 0))
+    outs, specs = (shape, shape), (spec, spec)
+    if passed:
+        outs = (jax.ShapeDtypeStruct(half, dtype),) * 4
+        specs = (pl.BlockSpec(memory_space=pltpu.VMEM),) * 4
     return pl.pallas_call(
-        functools.partial(stack_kernel, slots, shift),
+        functools.partial(stack_kernel, slots, shift, bool(passed)),
         grid=(count, sources // per),
-        out_shape=jax.ShapeDtypeStruct((count, tile_rows, traces, lanes), dtype),
+        out_shape=outs,
         in_specs=[
             pl.BlockSpec(memory_space=pltpu.SMEM),
             pl.BlockSpec(weights.shape, lambda d, i: (0, 0)),
             pl.BlockSpec((per, depth, lanes), lambda d, i: (i, shift + d, 0)),
-        ],
-        out_specs=pl.BlockSpec((1, tile_rows, traces, lanes), lambda d, i: (d, 0, 0, 0)),
+        ]
+        + [pl.BlockSpec(memory_space=pltpu.VMEM)] * len(passed),
+        out_specs=specs,
         scratch_shapes=[pltpu.VMEM((tile_rows + 1, traces, lanes), jnp.float32)],
         compiler_params=pltpu.CompilerParams(vmem_limit_bytes=16 * 2**20),
         cost_estimate=pl.CostEstimate(
             flops=2_500_000_000 * count, bytes_accessed=2**21 * count, transcendentals=0
         ),
-    )(code, weights, arrived)
-
-
-def join_kernel(half, rising_ref, falling_ref, own_ref, up_ref, down_ref):
-    def added(out, passed, own, low, high):
-        value = passed.astype(jnp.float32) + own_ref[own, low:high].astype(jnp.float32)
-        out[low:high] = value.astype(out.dtype)
-
-    rows = up_ref.shape[0]
-    if half:
-        middle = rows // 2
-        added(up_ref, rising_ref[...], 0, 0, middle)
-        up_ref[middle:] = own_ref[0, middle:]
-        down_ref[:middle] = own_ref[1, :middle]
-        added(down_ref, falling_ref[...], 1, middle, rows)
-    else:
-        added(up_ref, rising_ref[...], 0, 0, rows)
-        added(down_ref, falling_ref[...], 1, 0, rows)
-
-
-def join(half, rising, falling, own, pair):
+    )(code, weights, arrived, *passed)
+
+
+def join_kernel(at, passed_ref, own_ref, out_ref):
+    value = passed_ref[...].astype(jnp.float32) + own_ref[at].astype(jnp.float32)
+    out_ref[...] = value.astype(out_ref.dtype)
+
+
+def join(passed, own, at):
     vmem = pl.BlockSpec(memory_space=pltpu.VMEM)
-    shape = jax.ShapeDtypeStruct(own.shape[1:], own.dtype)
-    block = (2,) + own.shape[1:]
     return pl.pallas_call(
-        functools.partial(join_kernel, half),
-        grid=(1,),
-        out_shape=(shape, shape),
-        in_specs=[vmem, vmem, pl.BlockSpec(block, lambda i: (pair, 0, 0, 0))],
-        out_specs=(vmem, vmem),
-        compiler_params=pltpu.CompilerParams(vmem_limit_bytes=16 * 2**20),
+        functools.partial(join_kernel, at),
+        out_shape=jax.ShapeDtypeStruct(passed.shape, passed.dtype),
+        in_specs=[vmem, vmem],
+        out_specs=vmem,
+        compiler_params=pltpu.CompilerParams(vmem_limit_bytes=8 * 2**20),
         cost_estimate=pl.CostEstimate(
-            flops=1_000_000_000, bytes_accessed=3 * 2**20, transcendentals=0
+            flops=500_000_000, bytes_accessed=2**20, transcendentals=0
         ),
         name="join",
-    )(rising, falling, own)
+    )(passed, own)
+
+
+def total_kernel(side_ref, gain_ref, own_ref, rising_ref, falling_ref, *out_refs):
+    images = out_refs[0].shape[0]
+    gain = gain_ref[...]
+    for k, out_ref in enumerate(out_refs):
+        start = (side_ref[0] + k) % len(out_refs) * images
+        for i in range(images):
+            value = own_ref[0, start + i] + rising_ref[start + i].astype(jnp.float32)
+            value = (value + falling_ref[start + i].astype(jnp.float32)) * gain
+            out_ref[i] = value.astype(out_ref.dtype)
+
+
+def total(side, gain, own, rising, falling, quarters):
+    vmem = pl.BlockSpec(memory_space=pltpu.VMEM)
+    rows, angles, lanes = rising.shape
+    shape = jax.ShapeDtypeStruct((rows // quarters, angles, lanes), jnp.bfloat16)
+    return pl.pallas_call(
+        total_kernel,
+        out_shape=(shape,) * quarters,
+        in_specs=[pl.BlockSpec(memory_space=pltpu.SMEM), vmem, vmem, vmem, vmem],
+        out_specs=(vmem,) * quarters,
+        compiler_params=pltpu.CompilerParams(vmem_limit_bytes=8 * 2**20),
+        cost_estimate=pl.CostEstimate(
+            flops=500_000_000, bytes_accessed=2**20, transcendentals=0
+        ),
+        name="total",
+    )(side, gain, own, rising, falling)
 
 
 def moments_kernel(group, cut_ref, w_ref, in_ref, out_ref):
@@ -300,23 +355,28 @@
     return jnp.sum(squares, axis=1), jnp.sum(live, axis=0).astype(jnp.float32)
 
 
-def finish_kernel(in_ref, out_ref):
-    quarters, images, _, lanes = in_ref.shape
-    for q in range(quarters):
-        for k in range(images):
-            out_ref[k, :, q * lanes : (q + 1) * lanes] = in_ref[q, k]
-
-
-def finish(swapped):
-    quarters, images, traces, lanes = swapped.shape
+def finish_kernel(side_ref, *refs):
+    out_ref = refs[-1]
+    halves = (refs[: len(refs) // 2], refs[len(refs) // 2 : -1])
+    angles, lanes = refs[0].shape[1:]
+    for half, parts in enumerate(halves):
+        for k, ref in enumerate(parts):
+            quarter = (side_ref[0] - k + len(parts)) % len(parts)
+            start = pl.multiple_of(quarter * lanes, lanes)
+            out_ref[:, half * angles : (half + 1) * angles, pl.ds(start, lanes)] = ref[...]
+
+
+def finish(side, first, second):
+    images, angles, lanes = first[0].shape
     vmem = pl.BlockSpec(memory_space=pltpu.VMEM)
     return pl.pallas_call(
         finish_kernel,
-        out_shape=jax.ShapeDtypeStruct((images, traces, quarters * lanes), swapped.dtype),
-        in_specs=[vmem],
+        out_shape=jax.ShapeDtypeStruct((images, 2 * angles, len(first) * lanes), jnp.bfloat16),
+        in_specs=[pl.BlockSpec(memory_space=pltpu.SMEM)] + [vmem] * (2 * len(first)),
         out_specs=vmem,
+        compiler_params=pltpu.CompilerParams(vmem_limit_bytes=8 * 2**20),
         name="finish",
-    )(swapped)
+    )(side, *first, *second)
 
 
 def work(offsets, slant_weights, live, block_tile, image_slot):
@@ -332,8 +392,6 @@
     blocks = offsets.reshape(block_count, size, depth)
     tiles = block_tile[:, 0]
     home = lax.axis_index("shot_1").reshape(1)
-    up = [(i, (i + 1) % RING) for i in range(RING)]
-    down = [(i, (i - 1) % RING) for i in range(RING)]
 
     def diagonal(count):
         return jnp.kron(jnp.eye(count, dtype=jnp.bfloat16), slant_weights)
@@ -346,39 +404,53 @@
     arrived, code = [], []
     for n, piece in enumerate(PIECES):
         slots = (piece[1] - piece[0]) * CAP
-        carried = [totals] if n else []
+        carried = [totals] if n == 1 else []
         sent = pack(
             piece, home, tiles, image_slot, live.T, blocks, carried,
             columns, quarters, tile_count,
         )
+        if n == 1:
+            low = slots * (size + 1)
         sent = sent.reshape((columns * quarters,) + sent.shape[2:])
         arrived.append(lax.all_to_all(sent, PLANE, 0, 0, tiled=True))
         code.append(codes(arrived[-1], slots, size, tile_rows))
-    low = slots * (size + 1)
     totals = jnp.sum(arrived[1][:, low : low + 3].astype(jnp.float32), axis=(0, 1))
     gain = lax.rsqrt(totals[:angles] / (depth * totals[angles:]) + 1e-06)
 
-    def stacked(n, shift, count, dtype):
+    def stacked(n, shift, count, dtype, passed=()):
         slots = (PIECES[n][1] - PIECES[n][0]) * CAP
         return stack(
-            code[n], pair, arrived[n], slots, shift, count, tile_rows, traces, dtype
+            code[n], pair, arrived[n], slots, shift, count, tile_rows, traces, dtype, passed
         )
 
-    far = stacked(0, 0, 1, jnp.bfloat16)[0]
-    rising = lax.ppermute(far[: tile_rows // 2], "shot_1", up)
-    falling = lax.ppermute(far[tile_rows // 2 :], "shot_1", down)
-    middle = stacked(0, 1, 4, jnp.bfloat16)
-    near = stacked(1, 0, 2, jnp.bfloat16)
-    for n, (parts, at) in enumerate(((middle, 0), (middle, 1), (near, 0))):
-        rising, falling = join(n == 0, rising, falling, parts, at)
-        rising = lax.ppermute(rising, "shot_1", up)
-        falling = lax.ppermute(falling, "shot_1", down)
-    own = stacked(1, 2, 1, jnp.float32)[0]
-    total = own + rising.astype(jnp.float32) + falling.astype(jnp.float32)
-    image = (total * jnp.tile(gain, 2)[None, :, None]).astype(jnp.bfloat16)
-    image = image.reshape(quarters, 4, traces, LANES)
-    swapped = lax.all_to_all(image, "grp", 0, 0, tiled=True)
-    return finish(swapped)
+    def move(array, axis, shift):
+        count = lax.axis_size(axis)
+        return lax.ppermute(array, axis, [(i, (i + shift) % count) for i in range(count)])
+
+    far = stacked(0, 0, 1, jnp.bfloat16)
+    rising = [move(far[0][0], "shot_1", 1), None]
+    falling = [None, move(far[1][0], "shot_1", -1)]
+    for place in ((0, 1), (0, 3)):
+        parts = stacked(*place, 2, jnp.bfloat16)
+        for half in range(2):
+            for chain, at, shift in ((rising, 0, 1), (falling, 1, -1)):
+                if chain[half] is None:
+                    chain[half] = parts[half][at]
+                else:
+                    chain[half] = join(chain[half], parts[half], at)
+                chain[half] = move(chain[half], "shot_1", shift)
+    parts = stacked(1, 0, 2, jnp.bfloat16, rising + falling)
+    for half in (1, 0):
+        rising[half] = move(parts[half], "shot_1", 1)
+        falling[half] = move(parts[2 + half], "shot_1", -1)
+    own = stacked(1, 2, 1, jnp.float32)
+    side = lax.axis_index("grp").reshape(1)
+    scale = jnp.broadcast_to(gain[:, None], (angles, LANES))
+    ends = []
+    for half in range(2):
+        parts = total(side, scale, own[half], rising[half], falling[half], quarters)
+        ends.append([parts[0]] + [move(parts[k], "grp", k) for k in range(1, quarters)])
+    return finish(side, *ends)
 
 
 def solution(mesh):

time: 167 us -> 160 us (0.958)
  starting transfers between devices: 28.9 us -> 51.3 us
  waiting for transfers between devices: 48.2 us -> 34.3 us
  blocking collectives: 30.3 us -> 18.2 us
    ppermute x8 -> x20, starting transfers between devices: 13.8 us -> 36.1 us  [move(): lax.ppermute(array, axis, [(i, (i + shift) % count) for i in range(count)])]
    ppermute x8 -> x20, waiting for transfers between devices: 22.8 us -> 4.65 us  [move(): lax.ppermute(array, axis, [(i, (i + shift) % count) for i in range(count)])]
    all_to_all x1 -> x0, blocking collectives: 12 us -> none  [work(): swapped = lax.all_to_all(image, 'grp', 0, 0, tiled=True)]
    all_to_all x2, waiting for transfers between devices: 25.4 us -> 29.6 us  [work(): arrived.append(lax.all_to_all(sent, PLANE, 0, 0, tiled=True))]
    pallas_call x8 -> x14, Pallas kernels: 20.5 us -> 20.7 us  [the longest x5 16.4 us: stack(): pl.pallas_call(functools.partial(stack_kernel, slots, shift, bool(passed)...]
  transfers between devices with their start and end apart: 10 -> 22, of which waited for: 5 -> 5; matrix products, arithmetic and copies ran while one was open for 4% -> 4% of each run, Pallas kernels for 22% -> 22%
where the time goes in v3:
time: 160 us; the launch traced here: 158 us
  starting transfers between devices  51.3 us (32%)
  Pallas kernels  48.4 us (30%)
  waiting for transfers between devices  34.3 us (21%)
  blocking collectives  18.2 us (11%)
  other arithmetic  4.03 us (3%)
  local copies, waits for them, and re-layouts  1.75 us (1%)
    ppermute x20, starting transfers between devices, move(): lax.ppermute(array, axis, [(i, (i + shift) % count) for i in range(count)])  36.1 us
    all_to_all x2, waiting for transfers between devices, work(): arrived.append(lax.all_to_all(sent, PLANE, 0, 0, tiled=True))  29.6 us
    psum x1, blocking collectives, work(): totals = lax.psum(totals, 'shot_1')[None, :]  18.2 us
    pallas_call x5, Pallas kernels, stack(): pl.pallas_call(functools.partial(stack_kernel, slots, shift, bool(passed)...  16.4 us
    pallas_call x2, Pallas kernels, pack(): pl.pallas_call(functools.partial(pack_kernel, first, last), out_shape=jax...  15.4 us
    all_to_all x2, starting transfers between devices, work(): arrived.append(lax.all_to_all(sent, PLANE, 0, 0, tiled=True))  15.2 us
    pallas_call x1, Pallas kernels, moments(): pl.pallas_call(functools.partial(moments_kernel, weights.shape[0] // angl...  12.3 us
    ppermute x20, waiting for transfers between devices, move(): lax.ppermute(array, axis, [(i, (i + shift) % count) for i in range(count)])  4.65 us
  transfers between devices with their start and end apart: 22, of which 5 were waited for; matrix products, arithmetic and copies ran while one was open for 4% of the time, Pallas kernels for 22%

profile of v3, /device:TPU:1, one launch (start us, length us, event | category | flops | bytes accessed | tf_op | source)
XLA Modules:
  0.0 158.3 jit_solution(18111354955243824313)
XLA Ops:
  0.0 7.9 %shard_map.57 = bf16[8,4,656,128]{3,2,1,0:T(8,128)(2,1)} custom-call(s32[1]{0:T(128)} %bitcast.1.home_ref, s32[96]{0:T(128)} %bitcast.29, s32[96]{0:T(128)} %slot_ref.3, s32[64,192]{1,0:T(8,128)} %bitcast.25, bf16[96,64,512]{2,1,0:T(8,128)(2,1)} %bitcast.27), custom_call_target="tpu_custom_call" | custom-call | flops 8000000000 | bytes 10485760 | tf_op jit(solution)/shard_map/pallas_call | solution.py:148
  7.9 8.8 %all-to-all-start.1 = ((bf16[32,656,128]{2,1,0:T(8,128)(2,1)}), bf16[32,656,128]{2,1,0:T(8,128)(2,1)}, u32[]{:S(2)}, u32[]{:S(2)}) async-start(bf16[32,656,128]{2,1,0:T(8,128)(2,1)} %bitcast.23), calls=%async_computation.1 | async-start | bytes 10747904 | tf_op jit(solution)/shard_map/all_to_all | solution.py:415
  17.2 0.8 copy.8.w_ref
  18.6 12.3 %moments.1 = f32[64,128]{1,0:T(8,128)} custom-call(s32[192]{0:T(256)} %get-tuple-element.45.cut_ref, bf16[512,256]{1,0:T(8,128)(2,1)} %copy.8.w_ref, bf16[192,32,512]{2,1,0:T(8,128)(2,1)} %in_ref.1), custom_call_target="tpu_custom_call" | custom-call | flops 10000000000 | bytes 6291456 | tf_op jit(solution)/shard_map/moments/pallas_call | solution.py:339
  30.9 0.9 reduce_sum.55
  31.8 18.2 %psum.7.refs_0_ = f32[1,128]{1,0:T(1,128)} all-reduce(f32[1,128]{1,0:T(1,128)S(1)} %maximum_bitcast_fusion), channel_id=1, replica_groups=mesh['shot_0'=4,'shot_1'=8,'shot_2'=2,'grp'=4] {'shot_1'}, use_global_device_ids=true, to_apply=%region_3.4 | all-reduce | flops 128 | bytes 1024 | tf_op jit(solution)/shard_map/psum | solution.py:401
  50.0 7.5 %shard_map.55 = bf16[8,4,400,128]{3,2,1,0:T(8,128)(2,1)} custom-call(s32[1]{0:T(128)} %bitcast.1.home_ref, s32[96]{0:T(128)} %bitcast.30, s32[96]{0:T(128)} %slot_ref.3, s32[64,192]{1,0:T(8,128)} %bitcast.26, bf16[96,64,512]{2,1,0:T(8,128)(2,1)} %bitcast.28, f32[1,128]{1,0:T(1,128)} %psum.7.refs_0_), custom_call_target="tpu_custom_call" | custom-call | flops 8000000000 | bytes 10485760 | tf_op jit(solution)/shard_map/pallas_call | solution.py:148
  57.5 22.6 %all-to-all-done.1.in_ref = bf16[32,656,128]{2,1,0:T(8,128)(2,1)} async-done(((bf16[32,656,128]{2,1,0:T(8,128)(2,1)}), bf16[32,656,128]{2,1,0:T(8,128)(2,1)}, u32[]{:S(2)}, u32[]{:S(2)}) %all-to-all-start.1) | async-done | bytes 5373984 | tf_op jit(solution)/shard_map/all_to_all | solution.py:415
  80.1 6.4 %all-to-all-start = ((bf16[32,400,128]{2,1,0:T(8,128)(2,1)}), bf16[32,400,128]{2,1,0:T(8,128)(2,1)S(1)}, u32[]{:S(2)}, u32[]{:S(2)}) async-start(bf16[32,400,128]{2,1,0:T(8,128)(2,1)} %bitcast.24), calls=%async_computation | async-start | bytes 6553600 | tf_op jit(solution)/shard_map/all_to_all | solution.py:415
  86.9 1.5 fusion.4
  88.6 2.3 %shard_map.58 = (bf16[1,16,64,128]{3,2,1,0:T(8,128)(2,1)S(1)}, bf16[1,16,64,128]{3,2,1,0:T(8,128)(2,1)S(1)}) custom-call(s32[320]{0:T(512)S(1)} %reshape.55.code_ref, bf16[256,128]{1,0:T(8,128)(2,1)S(1)} %copy.9.w_ref, bf16[32,656,128]{2,1,0:T(8,128)(2,1)} %all-to-all-done.1.in_ref), custom_call_target="tpu_custom_call" | custom-call | flops 2500000000 | bytes 2097152 | tf_op jit(solution)/shard_map/pallas_call | solution.py:240
  90.9 5.5 %collective-permute-start.7 = (bf16[16,64,128]{2,1,0:T(8,128)(2,1)S(1)}, bf16[16,64,128]{2,1,0:T(8,128)(2,1)S(1)}, u32[]{:S(2)}, u32[]{:S(2)}) collective-permute-start(bf16[16,64,128]{2,1,0:T(8,128)(2,1)S(1)} %bitcast.22), channel_id=1, source_target_pairs={{0,56},{8,0},{16,8},{24,16},{32,24},{40,32},{48,40},{56,48},{1,57}... | collective-permute-start | bytes 786440 | tf_op jit(solution)/shard_map/ppermute | solution.py:428
  96.4 4.0 %shard_map.59 = (bf16[2,16,64,128]{3,2,1,0:T(8,128)(2,1)S(1)}, bf16[2,16,64,128]{3,2,1,0:T(8,128)(2,1)S(1)}) custom-call(s32[320]{0:T(512)S(1)} %reshape.55.code_ref, bf16[256,128]{1,0:T(8,128)(2,1)S(1)} %copy.9.w_ref, bf16[32,656,128]{2,1,0:T(8,128)(2,1)} %all-to-all-done.1.in_ref), custom_call_target="tpu_custom_call" | custom-call | flops 5000000000 | bytes 4194304 | tf_op jit(solution)/shard_map/pallas_call | solution.py:240
  100.4 2.8 %collective-permute-start.5 = (bf16[16,64,128]{2,1,0:T(8,128)(2,1)S(1)}, bf16[16,64,128]{2,1,0:T(8,128)(2,1)S(1)}, u32[]{:S(2)}, u32[]{:S(2)}) collective-permute-start(bf16[16,64,128]{2,1,0:T(8,128)(2,1)S(1)} %slice_bitcast_fusion), channel_id=1, source_target_pairs={{0,56},{8,0},{16,8},{24,16},{32,24},{40,32},{48,40},{56,48},{1,57}... | collective-permute-start | bytes 786440 | tf_op jit(solution)/shard_map/ppermute | solution.py:428
  103.3 2.7 %collective-permute-start.8 = (bf16[16,64,128]{2,1,0:T(8,128)(2,1)S(1)}, bf16[16,64,128]{2,1,0:T(8,128)(2,1)S(1)}, u32[]{:S(2)}, u32[]{:S(2)}) collective-permute-start(bf16[16,64,128]{2,1,0:T(8,128)(2,1)S(1)} %join.10), channel_id=1, source_target_pairs={{0,56},{8,0},{16,8},{24,16},{32,24},{40,32},{48,40},{56,48},{1,57}... | collective-permute-start | bytes 786440 | tf_op jit(solution)/shard_map/ppermute | solution.py:428
  106.2 4.0 %shard_map.60 = (bf16[2,16,64,128]{3,2,1,0:T(8,128)(2,1)S(1)}, bf16[2,16,64,128]{3,2,1,0:T(8,128)(2,1)S(1)}) custom-call(s32[320]{0:T(512)S(1)} %reshape.55.code_ref, bf16[256,128]{1,0:T(8,128)(2,1)S(1)} %copy.9.w_ref, bf16[32,656,128]{2,1,0:T(8,128)(2,1)} %all-to-all-done.1.in_ref), custom_call_target="tpu_custom_call" | custom-call | flops 5000000000 | bytes 4194304 | tf_op jit(solution)/shard_map/pallas_call | solution.py:240
  111.1 2.6 %collective-permute-start.6 = (bf16[16,64,128]{2,1,0:T(8,128)(2,1)}, bf16[16,64,128]{2,1,0:T(8,128)(2,1)}, u32[]{:S(2)}, u32[]{:S(2)}) collective-permute-start(bf16[16,64,128]{2,1,0:T(8,128)(2,1)} %join.9), channel_id=1, source_target_pairs={{0,56},{8,0},{16,8},{24,16},{32,24},{40,32},{48,40},{56,48},{1,57}... | collective-permute-start | bytes 786440 | tf_op jit(solution)/shard_map/ppermute | solution.py:428
  115.2 2.7 %collective-permute-start.9 = (bf16[16,64,128]{2,1,0:T(8,128)(2,1)}, bf16[16,64,128]{2,1,0:T(8,128)(2,1)}, u32[]{:S(2)}, u32[]{:S(2)}) collective-permute-start(bf16[16,64,128]{2,1,0:T(8,128)(2,1)} %join.11), channel_id=1, source_target_pairs={{0,56},{8,0},{16,8},{24,16},{32,24},{40,32},{48,40},{56,48},{1,57}... | collective-permute-start | bytes 786440 | tf_op jit(solution)/shard_map/ppermute | solution.py:428
  118.7 7.1 %all-to-all-done.in_ref = bf16[32,400,128]{2,1,0:T(8,128)(2,1)S(1)} async-done(((bf16[32,400,128]{2,1,0:T(8,128)(2,1)}), bf16[32,400,128]{2,1,0:T(8,128)(2,1)S(1)}, u32[]{:S(2)}, u32[]{:S(2)}) %all-to-all-start) | async-done | bytes 3276832 | tf_op jit(solution)/shard_map/all_to_all | solution.py:415
  126.5 1.9 %shard_map.56 = (f32[1,16,64,128]{3,2,1,0:T(8,128)S(1)}, f32[1,16,64,128]{3,2,1,0:T(8,128)S(1)}) custom-call(s32[192]{0:T(256)S(1)} %reshape.53.code_ref, bf16[256,128]{1,0:T(8,128)(2,1)S(1)} %copy.9.w_ref, bf16[32,400,128]{2,1,0:T(8,128)(2,1)S(1)} %all-to-all-done.in_ref), custom_call_target="tpu_custom_call" | custom-call | flops 2500000000 | bytes 2097152 | tf_op jit(solution)/shard_map/pallas_call | solution.py:240
  128.5 4.2 %shard_map.61 = (bf16[16,64,128]{2,1,0:T(8,128)(2,1)S(1)}, bf16[16,64,128]{2,1,0:T(8,128)(2,1)S(1)}, bf16[16,64,128]{2,1,0:T(8,128)(2,1)S(1)}, bf16[16,64,128]{2,1,0:T(8,128)(2,1)S(1)}) custom-call(s32[192]{0:T(256)S(1)} %reshape.53.code_ref, bf16[256,128]{1,0:T(8,128)(2,1)S(1)} %copy.9.w_ref, bf16[32,400,128]{2,1,0:T(8,128)(2,1)S(1)} %all-to-all-done.in_ref, ...), custom_call_target="tpu_custom_call" | custom-call | flops 5000000000 | bytes 4194304 | tf_op jit(solution)/shard_map/pallas_call | solution.py:240
  132.6 1.6 %collective-permute-start.15 = (bf16[16,64,128]{2,1,0:T(8,128)(2,1)S(1)}, bf16[16,64,128]{2,1,0:T(8,128)(2,1)S(1)}, u32[]{:S(2)}, u32[]{:S(2)}) collective-permute-start(bf16[16,64,128]{2,1,0:T(8,128)(2,1)S(1)} %get-tuple-element.39), channel_id=1, source_target_pairs={{0,8},{8,16},{16,24},{24,32},{32,40},{40,48},{48,56},{56,0},{1,9},... | collective-permute-start | bytes 786440 | tf_op jit(solution)/shard_map/ppermute | solution.py:428
  134.3 3.9 %collective-permute-start.16 = (bf16[16,64,128]{2,1,0:T(8,128)(2,1)S(1)}, bf16[16,64,128]{2,1,0:T(8,128)(2,1)S(1)}, u32[]{:S(2)}, u32[]{:S(2)}) collective-permute-start(bf16[16,64,128]{2,1,0:T(8,128)(2,1)S(1)} %get-tuple-element.40), channel_id=1, source_target_pairs={{0,56},{8,0},{16,8},{24,16},{32,24},{40,32},{48,40},{56,48},{1,57}... | collective-permute-start | bytes 786440 | tf_op jit(solution)/shard_map/ppermute | solution.py:428
  138.3 2.7 %collective-permute-start.11 = (bf16[16,64,128]{2,1,0:T(8,128)(2,1)S(1)}, bf16[16,64,128]{2,1,0:T(8,128)(2,1)S(1)}, u32[]{:S(2)}, u32[]{:S(2)}) collective-permute-start(bf16[16,64,128]{2,1,0:T(8,128)(2,1)S(1)} %get-tuple-element.33), channel_id=1, source_target_pairs={{0,56},{8,0},{16,8},{24,16},{32,24},{40,32},{48,40},{56,48},{1,57}... | collective-permute-start | bytes 786440 | tf_op jit(solution)/shard_map/ppermute | solution.py:428
  141.1 2.7 %collective-permute-done.15.rising_ref = bf16[16,64,128]{2,1,0:T(8,128)(2,1)S(1)} collective-permute-done((bf16[16,64,128]{2,1,0:T(8,128)(2,1)S(1)}, bf16[16,64,128]{2,1,0:T(8,128)(2,1)S(1)}, u32[]{:S(2)}, u32[]{:S(2)}) %collective-permute-start.15) | collective-permute-done | bytes 262176 | tf_op jit(solution)/shard_map/ppermute | solution.py:428
  143.9 2.9 %collective-permute-start.17 = (bf16[4,64,128]{2,1,0:T(8,128)(2,1)S(1)}, bf16[4,64,128]{2,1,0:T(8,128)(2,1)S(1)}, u32[]{:S(2)}, u32[]{:S(2)}) collective-permute-start(bf16[4,64,128]{2,1,0:T(8,128)(2,1)S(1)} %get-tuple-element.42), channel_id=1, source_target_pairs={{0,1},{1,2},{2,3},{3,0},{4,5},{5,6},{6,7},{7,4},{8,9},{9,10},{10,1... | collective-permute-start | bytes 196616 | tf_op jit(solution)/shard_map/ppermute | solution.py:428
  146.8 3.2 %collective-permute-start.18 = (bf16[4,64,128]{2,1,0:T(8,128)(2,1)S(1)}, bf16[4,64,128]{2,1,0:T(8,128)(2,1)S(1)}, u32[]{:S(2)}, u32[]{:S(2)}) collective-permute-start(bf16[4,64,128]{2,1,0:T(8,128)(2,1)S(1)} %get-tuple-element.43), channel_id=1, source_target_pairs={{0,2},{1,3},{2,0},{3,1},{4,6},{5,7},{6,4},{7,5},{8,10},{9,11},{10,... | collective-permute-start | bytes 196616 | tf_op jit(solution)/shard_map/ppermute | solution.py:428
  150.2 2.2 %collective-permute-start.12 = (bf16[4,64,128]{2,1,0:T(8,128)(2,1)S(1)}, bf16[4,64,128]{2,1,0:T(8,128)(2,1)S(1)}, u32[]{:S(2)}, u32[]{:S(2)}) collective-permute-start(bf16[4,64,128]{2,1,0:T(8,128)(2,1)S(1)} %get-tuple-element.35), channel_id=1, source_target_pairs={{0,1},{1,2},{2,3},{3,0},{4,5},{5,6},{6,7},{7,4},{8,9},{9,10},{10,1... | collective-permute-start | bytes 196616 | tf_op jit(solution)/shard_map/ppermute | solution.py:428
  152.3 1.6 %collective-permute-start.13 = (bf16[4,64,128]{2,1,0:T(8,128)(2,1)S(1)}, bf16[4,64,128]{2,1,0:T(8,128)(2,1)S(1)}, u32[]{:S(2)}, u32[]{:S(2)}) collective-permute-start(bf16[4,64,128]{2,1,0:T(8,128)(2,1)S(1)} %get-tuple-element.36), channel_id=1, source_target_pairs={{0,2},{1,3},{2,0},{3,1},{4,6},{5,7},{6,4},{7,5},{8,10},{9,11},{10,... | collective-permute-start | bytes 196616 | tf_op jit(solution)/shard_map/ppermute | solution.py:428
  154.0 1.5 collective-permute-start.14
  155.4 1.6 %collective-permute-done.13.refs_2_ = bf16[4,64,128]{2,1,0:T(8,128)(2,1)S(1)} collective-permute-done((bf16[4,64,128]{2,1,0:T(8,128)(2,1)S(1)}, bf16[4,64,128]{2,1,0:T(8,128)(2,1)S(1)}, u32[]{:S(2)}, u32[]{:S(2)}) %collective-permute-start.13) | collective-permute-done | bytes 65568 | tf_op jit(solution)/shard_map/ppermute | solution.py:428
  157.4 0.9 finish.1
  (57 shorter events, 6.6 us)
Async XLA Ops:
  7.9 8.9 %copy-start.1 = (bf16[64,32]{0,1:T(8,128)(2,1)S(1)}, bf16[64,32]{0,1:T(8,128)(2,1)}, u32[]{:S(2)}) copy-start(bf16[64,32]{0,1:T(8,128)(2,1)} %param.6) | copy-start | bytes 12292
  7.9 10.1 %copy-start = (s32[192,64]{0,1:T(8,128)S(1)}, s32[192,64]{0,1:T(8,128)}, u32[]{:S(2)}) copy-start(s32[192,64]{0,1:T(8,128)} %param.7) | copy-start | bytes 147460
  7.9 72.2 %all-to-all-start.1 = ((bf16[32,656,128]{2,1,0:T(8,128)(2,1)}), bf16[32,656,128]{2,1,0:T(8,128)(2,1)}, u32[]{:S(2)}, u32[]{:S(2)}) async-start(bf16[32,656,128]{2,1,0:T(8,128)(2,1)} %bitcast.23), calls=%async_computation.1 | async-start | bytes 10747904 | tf_op jit(solution)/shard_map/all_to_all | solution.py:415
  80.1 45.7 %all-to-all-start = ((bf16[32,400,128]{2,1,0:T(8,128)(2,1)}), bf16[32,400,128]{2,1,0:T(8,128)(2,1)S(1)}, u32[]{:S(2)}, u32[]{:S(2)}) async-start(bf16[32,400,128]{2,1,0:T(8,128)(2,1)} %bitcast.24), calls=%async_computation | async-start | bytes 6553600 | tf_op jit(solution)/shard_map/all_to_all | solution.py:415
  90.9 12.4 %collective-permute-start.7 = (bf16[16,64,128]{2,1,0:T(8,128)(2,1)S(1)}, bf16[16,64,128]{2,1,0:T(8,128)(2,1)S(1)}, u32[]{:S(2)}, u32[]{:S(2)}) collective-permute-start(bf16[16,64,128]{2,1,0:T(8,128)(2,1)S(1)} %bitcast.22), channel_id=1, source_target_pairs={{0,56},{8,0},{16,8},{24,16},{32,24},{40,32},{48,40},{56,48},{1,57}... | collective-permute-start | bytes 786440 | tf_op jit(solution)/shard_map/ppermute | solution.py:428
  96.4 9.7 %collective-permute-start = (bf16[16,64,128]{2,1,0:T(8,128)(2,1)S(1)}, bf16[16,64,128]{2,1,0:T(8,128)(2,1)S(1)}, u32[]{:S(2)}, u32[]{:S(2)}) collective-permute-start(bf16[16,64,128]{2,1,0:T(8,128)(2,1)S(1)} %bitcast.21), channel_id=1, source_target_pairs={{0,8},{8,16},{16,24},{24,32},{32,40},{40,48},{48,56},{56,0},{1,9},... | collective-permute-start | bytes 786440 | tf_op jit(solution)/shard_map/ppermute | solution.py:428
  100.4 9.9 %collective-permute-start.5 = (bf16[16,64,128]{2,1,0:T(8,128)(2,1)S(1)}, bf16[16,64,128]{2,1,0:T(8,128)(2,1)S(1)}, u32[]{:S(2)}, u32[]{:S(2)}) collective-permute-start(bf16[16,64,128]{2,1,0:T(8,128)(2,1)S(1)} %slice_bitcast_fusion), channel_id=1, source_target_pairs={{0,56},{8,0},{16,8},{24,16},{32,24},{40,32},{48,40},{56,48},{1,57}... | collective-permute-start | bytes 786440 | tf_op jit(solution)/shard_map/ppermute | solution.py:428
  103.2 10.5 %collective-permute-start.3 = (bf16[16,64,128]{2,1,0:T(8,128)(2,1)S(1)}, bf16[16,64,128]{2,1,0:T(8,128)(2,1)S(1)}, u32[]{:S(2)}, u32[]{:S(2)}) collective-permute-start(bf16[16,64,128]{2,1,0:T(8,128)(2,1)S(1)} %slice_bitcast_fusion.1), channel_id=1, source_target_pairs={{0,8},{8,16},{16,24},{24,32},{32,40},{40,48},{48,56},{56,0},{1,9},... | collective-permute-start | bytes 786440 | tf_op jit(solution)/shard_map/ppermute | solution.py:428
  103.3 11.1 %collective-permute-start.8 = (bf16[16,64,128]{2,1,0:T(8,128)(2,1)S(1)}, bf16[16,64,128]{2,1,0:T(8,128)(2,1)S(1)}, u32[]{:S(2)}, u32[]{:S(2)}) collective-permute-start(bf16[16,64,128]{2,1,0:T(8,128)(2,1)S(1)} %join.10), channel_id=1, source_target_pairs={{0,56},{8,0},{16,8},{24,16},{32,24},{40,32},{48,40},{56,48},{1,57}... | collective-permute-start | bytes 786440 | tf_op jit(solution)/shard_map/ppermute | solution.py:428
  106.1 11.8 %collective-permute-start.1 = (bf16[16,64,128]{2,1,0:T(8,128)(2,1)S(1)}, bf16[16,64,128]{2,1,0:T(8,128)(2,1)S(1)}, u32[]{:S(2)}, u32[]{:S(2)}) collective-permute-start(bf16[16,64,128]{2,1,0:T(8,128)(2,1)S(1)} %join.6), channel_id=1, source_target_pairs={{0,8},{8,16},{16,24},{24,32},{32,40},{40,48},{48,56},{56,0},{1,9},... | collective-permute-start | bytes 786440 | tf_op jit(solution)/shard_map/ppermute | solution.py:428
  111.1 17.4 %collective-permute-start.6 = (bf16[16,64,128]{2,1,0:T(8,128)(2,1)}, bf16[16,64,128]{2,1,0:T(8,128)(2,1)}, u32[]{:S(2)}, u32[]{:S(2)}) collective-permute-start(bf16[16,64,128]{2,1,0:T(8,128)(2,1)} %join.9), channel_id=1, source_target_pairs={{0,56},{8,0},{16,8},{24,16},{32,24},{40,32},{48,40},{56,48},{1,57}... | collective-permute-start | bytes 786440 | tf_op jit(solution)/shard_map/ppermute | solution.py:428
  114.5 14.0 %collective-permute-start.4 = (bf16[16,64,128]{2,1,0:T(8,128)(2,1)}, bf16[16,64,128]{2,1,0:T(8,128)(2,1)}, u32[]{:S(2)}, u32[]{:S(2)}) collective-permute-start(bf16[16,64,128]{2,1,0:T(8,128)(2,1)} %join.8), channel_id=1, source_target_pairs={{0,8},{8,16},{16,24},{24,32},{32,40},{40,48},{48,56},{56,0},{1,9},... | collective-permute-start | bytes 786440 | tf_op jit(solution)/shard_map/ppermute | solution.py:428
  115.2 13.2 %collective-permute-start.9 = (bf16[16,64,128]{2,1,0:T(8,128)(2,1)}, bf16[16,64,128]{2,1,0:T(8,128)(2,1)}, u32[]{:S(2)}, u32[]{:S(2)}) collective-permute-start(bf16[16,64,128]{2,1,0:T(8,128)(2,1)} %join.11), channel_id=1, source_target_pairs={{0,56},{8,0},{16,8},{24,16},{32,24},{40,32},{48,40},{56,48},{1,57}... | collective-permute-start | bytes 786440 | tf_op jit(solution)/shard_map/ppermute | solution.py:428
  118.7 9.8 %collective-permute-start.2 = (bf16[16,64,128]{2,1,0:T(8,128)(2,1)}, bf16[16,64,128]{2,1,0:T(8,128)(2,1)}, u32[]{:S(2)}, u32[]{:S(2)}) collective-permute-start(bf16[16,64,128]{2,1,0:T(8,128)(2,1)} %join.7), channel_id=1, source_target_pairs={{0,8},{8,16},{16,24},{24,32},{32,40},{40,48},{48,56},{56,0},{1,9},... | collective-permute-start | bytes 786440 | tf_op jit(solution)/shard_map/ppermute | solution.py:428
  132.6 11.1 %collective-permute-start.15 = (bf16[16,64,128]{2,1,0:T(8,128)(2,1)S(1)}, bf16[16,64,128]{2,1,0:T(8,128)(2,1)S(1)}, u32[]{:S(2)}, u32[]{:S(2)}) collective-permute-start(bf16[16,64,128]{2,1,0:T(8,128)(2,1)S(1)} %get-tuple-element.39), channel_id=1, source_target_pairs={{0,8},{8,16},{16,24},{24,32},{32,40},{40,48},{48,56},{56,0},{1,9},... | collective-permute-start | bytes 786440 | tf_op jit(solution)/shard_map/ppermute | solution.py:428
  134.3 9.5 %collective-permute-start.16 = (bf16[16,64,128]{2,1,0:T(8,128)(2,1)S(1)}, bf16[16,64,128]{2,1,0:T(8,128)(2,1)S(1)}, u32[]{:S(2)}, u32[]{:S(2)}) collective-permute-start(bf16[16,64,128]{2,1,0:T(8,128)(2,1)S(1)} %get-tuple-element.40), channel_id=1, source_target_pairs={{0,56},{8,0},{16,8},{24,16},{32,24},{40,32},{48,40},{56,48},{1,57}... | collective-permute-start | bytes 786440 | tf_op jit(solution)/shard_map/ppermute | solution.py:428
  138.3 11.8 %collective-permute-start.10 = (bf16[16,64,128]{2,1,0:T(8,128)(2,1)S(1)}, bf16[16,64,128]{2,1,0:T(8,128)(2,1)S(1)}, u32[]{:S(2)}, u32[]{:S(2)}) collective-permute-start(bf16[16,64,128]{2,1,0:T(8,128)(2,1)S(1)} %get-tuple-element.32), channel_id=1, source_target_pairs={{0,8},{8,16},{16,24},{24,32},{32,40},{40,48},{48,56},{56,0},{1,9},... | collective-permute-start | bytes 786440 | tf_op jit(solution)/shard_map/ppermute | solution.py:428
  138.3 11.7 %collective-permute-start.11 = (bf16[16,64,128]{2,1,0:T(8,128)(2,1)S(1)}, bf16[16,64,128]{2,1,0:T(8,128)(2,1)S(1)}, u32[]{:S(2)}, u32[]{:S(2)}) collective-permute-start(bf16[16,64,128]{2,1,0:T(8,128)(2,1)S(1)} %get-tuple-element.33), channel_id=1, source_target_pairs={{0,56},{8,0},{16,8},{24,16},{32,24},{40,32},{48,40},{56,48},{1,57}... | collective-permute-start | bytes 786440 | tf_op jit(solution)/shard_map/ppermute | solution.py:428
  143.9 10.0 %collective-permute-start.17 = (bf16[4,64,128]{2,1,0:T(8,128)(2,1)S(1)}, bf16[4,64,128]{2,1,0:T(8,128)(2,1)S(1)}, u32[]{:S(2)}, u32[]{:S(2)}) collective-permute-start(bf16[4,64,128]{2,1,0:T(8,128)(2,1)S(1)} %get-tuple-element.42), channel_id=1, source_target_pairs={{0,1},{1,2},{2,3},{3,0},{4,5},{5,6},{6,7},{7,4},{8,9},{9,10},{10,1... | collective-permute-start | bytes 196616 | tf_op jit(solution)/shard_map/ppermute | solution.py:428
  146.8 8.6 %collective-permute-start.18 = (bf16[4,64,128]{2,1,0:T(8,128)(2,1)S(1)}, bf16[4,64,128]{2,1,0:T(8,128)(2,1)S(1)}, u32[]{:S(2)}, u32[]{:S(2)}) collective-permute-start(bf16[4,64,128]{2,1,0:T(8,128)(2,1)S(1)} %get-tuple-element.43), channel_id=1, source_target_pairs={{0,2},{1,3},{2,0},{3,1},{4,6},{5,7},{6,4},{7,5},{8,10},{9,11},{10,... | collective-permute-start | bytes 196616 | tf_op jit(solution)/shard_map/ppermute | solution.py:428
  150.0 5.4 %collective-permute-start.19 = (bf16[4,64,128]{2,1,0:T(8,128)(2,1)S(1)}, bf16[4,64,128]{2,1,0:T(8,128)(2,1)S(1)}, u32[]{:S(2)}, u32[]{:S(2)}) collective-permute-start(bf16[4,64,128]{2,1,0:T(8,128)(2,1)S(1)} %get-tuple-element.44), channel_id=1, source_target_pairs={{0,3},{1,0},{2,1},{3,2},{4,7},{5,4},{6,5},{7,6},{8,11},{9,8},{10,9... | collective-permute-start | bytes 196616 | tf_op jit(solution)/shard_map/ppermute | solution.py:428
  150.2 5.3 %collective-permute-start.12 = (bf16[4,64,128]{2,1,0:T(8,128)(2,1)S(1)}, bf16[4,64,128]{2,1,0:T(8,128)(2,1)S(1)}, u32[]{:S(2)}, u32[]{:S(2)}) collective-permute-start(bf16[4,64,128]{2,1,0:T(8,128)(2,1)S(1)} %get-tuple-element.35), channel_id=1, source_target_pairs={{0,1},{1,2},{2,3},{3,0},{4,5},{5,6},{6,7},{7,4},{8,9},{9,10},{10,1... | collective-permute-start | bytes 196616 | tf_op jit(solution)/shard_map/ppermute | solution.py:428
  152.3 4.7 %collective-permute-start.13 = (bf16[4,64,128]{2,1,0:T(8,128)(2,1)S(1)}, bf16[4,64,128]{2,1,0:T(8,128)(2,1)S(1)}, u32[]{:S(2)}, u32[]{:S(2)}) collective-permute-start(bf16[4,64,128]{2,1,0:T(8,128)(2,1)S(1)} %get-tuple-element.36), channel_id=1, source_target_pairs={{0,2},{1,3},{2,0},{3,1},{4,6},{5,7},{6,4},{7,5},{8,10},{9,11},{10,... | collective-permute-start | bytes 196616 | tf_op jit(solution)/shard_map/ppermute | solution.py:428
  154.0 3.4 %collective-permute-start.14 = (bf16[4,64,128]{2,1,0:T(8,128)(2,1)S(1)}, bf16[4,64,128]{2,1,0:T(8,128)(2,1)S(1)}, u32[]{:S(2)}, u32[]{:S(2)}) collective-permute-start(bf16[4,64,128]{2,1,0:T(8,128)(2,1)S(1)} %get-tuple-element.37), channel_id=1, source_target_pairs={{0,3},{1,0},{2,1},{3,2},{4,7},{5,4},{6,5},{7,6},{8,11},{9,8},{10,9... | collective-permute-start | bytes 196616 | tf_op jit(solution)/shard_map/ppermute | solution.py:428

commit v4 on v3

--- a/solution.py
+++ b/solution.py
@@ -14,19 +14,24 @@
 RING = 8
 LANES = 128
 CAP = 2
-PIECES = ((0, 5), (5, 8))
+FAR = (0, 5)
 
 
 def pack_kernel(
-    first, last, home_ref, tile_ref, slot_ref, live_ref, off_ref, *refs
+    first, last, groups, carry, moved, home_ref, tile_ref, slot_ref, live_ref, off_ref, *refs
 ):
-    *total_ref, out_ref, data, zeros, flags, meta, meta_low, count, goal = refs[:-3]
-    in_sems, out_sem, meta_sem = refs[-3:]
+    total_ref, moved_refs = refs[:carry], refs[carry : carry + moved]
+    out_refs = refs[carry + moved : carry + moved + groups]
+    data, zeros, flags, meta, meta_low, count, goal = refs[carry + moved + groups :][:7]
+    in_sems, out_sem, meta_sem, moved_sem = refs[-4:]
     blocks, size, _ = off_ref.shape
     positions = flags.shape[0]
     quarters = data.shape[0]
     tiles = count.shape[0]
-    slots = (last - first) * CAP
+    slots = (last - first) // groups * CAP
+    columns = out_refs[0].shape[0]
+    meta_at = slots * size * (1 + moved)
+    meta_rows = meta.shape[1]
     parts = in_sems.shape[0]
     step = blocks // parts
     home = home_ref[0]
@@ -41,6 +46,25 @@
     for g in range(parts):
         for q in range(quarters):
             load(g, q).start()
+
+    def pass_on(m):
+        rows = slots * size
+        moves = (
+            (0, (m + 1) * rows, rows),
+            (rows, meta_at + (m + 1) * meta_rows, meta_rows),
+        )
+        return [
+            pltpu.make_async_copy(
+                moved_refs[m].at[:, :, pl.ds(source, length), :],
+                out_refs[0].at[:, :, pl.ds(goal_row, length), :],
+                moved_sem.at[2 * m + n],
+            )
+            for n, (source, goal_row, length) in enumerate(moves)
+        ]
+
+    for m in range(moved):
+        for copy in pass_on(m):
+            copy.start()
     zeros[...] = jnp.zeros_like(zeros)
     meta[...] = jnp.zeros_like(meta)
 
@@ -64,17 +88,29 @@
         order = jnp.maximum(7 - 2 * near + (ahead > RING // 2).astype(jnp.int32), 0)
         column = (tile // (2 * RING)) * 2 + tile % 2
         mine = (order >= first) & (order < last)
+        if groups > 1:
+            return (order - first) * columns + column, 0, mine
         return column, (order - first) * CAP, mine
 
-    def target(column, slot):
-        return out_ref.at[column, :, pl.ds(pl.multiple_of(slot * size, size), size), :]
+    def start(source, line, slot):
+        rows = pl.ds(pl.multiple_of(slot * size, size), size)
+        for k, out_ref in enumerate(out_refs):
+            if groups == 1:
+                target = out_ref.at[line, :, rows, :]
+                pltpu.make_async_copy(source, target, out_sem).start()
+            else:
+
+                @pl.when((line >= k * columns) & (line < (k + 1) * columns))
+                def _():
+                    target = out_ref.at[line - k * columns, :, rows, :]
+                    pltpu.make_async_copy(source, target, out_sem).start()
 
     def plan(b, _):
         tile = tile_ref[b]
         rank = count[tile]
         count[tile] = rank + 1
         column, slot, mine = place(tile)
-        goal[b] = jnp.where(mine, column * slots + slot + rank, -1)
+        goal[b] = jnp.where(mine, column * 64 + slot + rank, -1)
 
         @pl.when(mine)
         def _():
@@ -93,7 +129,7 @@
 
             @pl.when(mine & (used <= rank))
             def _():
-                pltpu.make_async_copy(zeros, target(column, slot + rank), out_sem).start()
+                start(zeros, column, slot + rank)
 
         return 0
 
@@ -112,94 +148,99 @@
 
         @pl.when(at >= 0)
         def _():
+            start(data.at[:, b], at >> 6, at & 63)
+
+        return 0
+
+    def meta_copies():
+        return [
             pltpu.make_async_copy(
-                data.at[:, b], target(at // slots, at % slots), out_sem
-            ).start()
-
-        return 0
-
-    def meta_copy(q):
-        return pltpu.make_async_copy(
-            meta_low, out_ref.at[:, q, pl.ds(slots * size, meta.shape[1]), :], meta_sem
-        )
+                meta_low.at[pl.ds(k * columns, columns)],
+                out_ref.at[:, q, pl.ds(meta_at, meta_rows), :],
+                meta_sem,
+            )
+            for k, out_ref in enumerate(out_refs)
+            for q in range(quarters)
+        ]
 
     for g in range(parts):
         for q in range(quarters):
             load(g, q).wait()
         lax.fori_loop(g * step, (g + 1) * step, send, 0, unroll=4)
         if g == parts // 2:
-            for q in range(quarters):
-                meta_copy(q).start()
-    whole = out_ref.at[:, :, pl.ds(0, slots * size), :]
-    pltpu.make_async_copy(whole, whole, out_sem).wait()
-    for q in range(quarters):
-        meta_copy(q).wait()
-
-
-def pack(piece, home, tiles, slots, live, blocks, carried, columns, quarters, tile_count):
+            for copy in meta_copies():
+                copy.start()
+    for out_ref in out_refs:
+        whole = out_ref.at[:, :, pl.ds(0, slots * size), :]
+        pltpu.make_async_copy(whole, whole, out_sem).wait()
+    for copy in meta_copies():
+        copy.wait()
+    for m in range(moved):
+        for copy in pass_on(m):
+            copy.wait()
+
+
+def pack(
+    piece, home, tiles, slots, live, blocks, columns, quarters, tile_count,
+    groups=1, carried=(), moved=(),
+):
     first, last = piece
     count, size, _ = blocks.shape
-    rows = (last - first) * CAP
-    meta_rows = -(-(rows + 3 * len(carried)) // 16) * 16
+    rows = (last - first) // groups * CAP
+    meta_rows = -(-(rows + 3 * len(carried)) // 8) * 8
+    length = (rows * size + meta_rows) * (1 + len(moved))
+    parts = 8
     vmem = pl.BlockSpec(memory_space=pltpu.VMEM)
-    parts = 8
     hbm = pl.BlockSpec(memory_space=pltpu.HBM)
     smem = pl.BlockSpec(memory_space=pltpu.SMEM)
+    shape = jax.ShapeDtypeStruct((columns, quarters, length, LANES), jnp.bfloat16)
     return pl.pallas_call(
-        functools.partial(pack_kernel, first, last),
-        out_shape=jax.ShapeDtypeStruct(
-            (columns, quarters, rows * size + meta_rows, LANES), jnp.bfloat16
-        ),
-        in_specs=[smem, smem, smem, vmem, hbm] + [vmem] * len(carried),
-        out_specs=hbm,
+        functools.partial(pack_kernel, first, last, groups, len(carried), len(moved)),
+        out_shape=(shape,) * groups,
+        in_specs=[smem, smem, smem, vmem, hbm] + [vmem] * (len(carried) + len(moved)),
+        out_specs=(hbm,) * groups,
         scratch_shapes=[
             pltpu.VMEM((quarters, count, size, LANES), jnp.bfloat16),
             pltpu.VMEM((quarters, size, LANES), jnp.bfloat16),
             pltpu.VMEM((2 * count, LANES), jnp.float32),
-            pltpu.VMEM((columns, meta_rows, LANES), jnp.float32),
-            pltpu.VMEM((columns, meta_rows, LANES), jnp.bfloat16),
+            pltpu.VMEM((groups * columns, meta_rows, LANES), jnp.float32),
+            pltpu.VMEM((groups * columns, meta_rows, LANES), jnp.bfloat16),
             pltpu.SMEM((tile_count,), jnp.int32),
             pltpu.SMEM((count,), jnp.int32),
             pltpu.SemaphoreType.DMA((parts,)),
             pltpu.SemaphoreType.DMA,
             pltpu.SemaphoreType.DMA,
+            pltpu.SemaphoreType.DMA((max(2 * len(moved), 1),)),
         ],
-        compiler_params=pltpu.CompilerParams(vmem_limit_bytes=60 * 2**20),
+        compiler_params=pltpu.CompilerParams(
+            vmem_limit_bytes=62 * 2**20
+        ),
         cost_estimate=pl.CostEstimate(
             flops=8_000_000_000, bytes_accessed=10 * 2**20, transcendentals=0
         ),
-    )(home, tiles, slots, live, blocks, *carried)
-
-
-def stack_kernel(slots, shift, joined, code_ref, w_ref, in_ref, *refs):
-    acc = refs[-1]
+    )(home, tiles, slots, live, blocks, *carried, *moved)
+
+
+def stack_kernel(codes_each, stride, shift, merge, code_ref, w_ref, in_ref, first_ref, second_ref, acc):
     place, step = pl.program_id(0), pl.program_id(1)
-    per, _, _ = in_ref.shape
+    per = in_ref.shape[0]
     traces, lanes = acc.shape[1:]
     angles = traces // 2
-
-    if joined:
-        passed = (refs[0:2], refs[2:4])
-        images = passed[0][0].shape[0]
-        for at in range(2):
-
-            @pl.when((step == 0) & (place == at))
-            def _():
-                for half in range(2):
-                    acc[:images, half * angles : (half + 1) * angles] = passed[at][half][
-                        ...
-                    ].astype(jnp.float32)
-    else:
-
-        @pl.when(step == 0)
-        def _():
-            acc[...] = jnp.zeros_like(acc)
-
+    begins, ends = step == 0, step == pl.num_programs(1) - 1
+    if merge:
+        begins = begins & (place == 0)
+        ends = ends & (place == pl.num_programs(0) - 1)
+
+    @pl.when(begins)
+    def _():
+        acc[...] = jnp.zeros_like(acc)
+
+    weights = w_ref[...].T
     row = lax.broadcasted_iota(jnp.int32, (angles, lanes), 0)
     for u in range(per):
-        product = jnp.dot(w_ref[...], in_ref[u], preferred_element_type=jnp.float32)
+        product = jnp.dot(weights, in_ref[u], preferred_element_type=jnp.float32)
         for j in range(CAP):
-            code = code_ref[(step * per + u) * slots + (shift + place) * CAP + j]
+            code = code_ref[(step * per + u) * codes_each + (shift + place) * stride + j]
             label = code >> 14
             for half, cut in enumerate(((code >> 7) & 127, code & 127)):
                 low = half * angles
@@ -207,53 +248,47 @@
                 angle = jnp.where(row < cut, angle, 0.0).astype(jnp.bfloat16)
                 acc[label, low : low + angles, :] += angle.astype(jnp.float32)
 
-    outs = (refs[4:6], refs[6:8]) if joined else (refs[0:2],)
-    for at, pair in enumerate(outs):
-
-        @pl.when((step == pl.num_programs(1) - 1) & ((place == at) | (not joined)))
-        def _():
-            for half, ref in enumerate(pair):
-                images = ref.shape[-3]
-                value = acc[:images, half * angles : (half + 1) * angles]
-                ref[...] = value.astype(ref.dtype).reshape(ref.shape)
-
-
-def codes(arrived, slots, size, tile_rows):
-    flags = arrived[:, slots * size : slots * size + slots, :].astype(jnp.int32)
+    @pl.when(ends)
+    def _():
+        images = first_ref.shape[1]
+        first_ref[0] = acc[:images, :angles].astype(first_ref.dtype)
+        second_ref[0] = acc[:images, angles:].astype(second_ref.dtype)
+
+
+def codes(arrived, rows, tile_rows):
+    flags = arrived[:, rows:].astype(jnp.int32)
     lane = lax.broadcasted_iota(jnp.int32, flags.shape, 2)
     live = (flags > 0).astype(jnp.int32) * jnp.where(lane < LANES // 2, 128, 1)
     label = jnp.where(flags > 0, flags - 1, tile_rows) * 16384
     return jnp.sum(live + jnp.where(lane == 0, label, 0), axis=2).reshape(-1)
 
 
-def stack(code, weights, arrived, slots, shift, count, tile_rows, traces, dtype, passed=()):
+def stack(code, weights, arrived, shift, count, stride, merge, tile_rows, traces, dtype):
     sources, _, lanes = arrived.shape
-    depth = weights.shape[1]
+    codes_each = code.shape[0] // sources
+    height = weights.shape[0]
     per = 16
     half = (tile_rows, traces // 2, lanes)
-    shape = jax.ShapeDtypeStruct((count,) + half, dtype)
-    spec = pl.BlockSpec((1,) + half, lambda d, i: (d, 0, 0, 0))
-    outs, specs = (shape, shape), (spec, spec)
-    if passed:
-        outs = (jax.ShapeDtypeStruct(half, dtype),) * 4
-        specs = (pl.BlockSpec(memory_space=pltpu.VMEM),) * 4
+    shape = jax.ShapeDtypeStruct((1 if merge else count,) + half, dtype)
+    spec = pl.BlockSpec((1,) + half, lambda d, i: (0 if merge else d, 0, 0, 0))
     return pl.pallas_call(
-        functools.partial(stack_kernel, slots, shift, bool(passed)),
+        functools.partial(stack_kernel, codes_each, stride, shift, merge),
         grid=(count, sources // per),
-        out_shape=outs,
+        out_shape=(shape, shape),
         in_specs=[
             pl.BlockSpec(memory_space=pltpu.SMEM),
             pl.BlockSpec(weights.shape, lambda d, i: (0, 0)),
-            pl.BlockSpec((per, depth, lanes), lambda d, i: (i, shift + d, 0)),
-        ]
-        + [pl.BlockSpec(memory_space=pltpu.VMEM)] * len(passed),
-        out_specs=specs,
+            pl.BlockSpec((per, height, lanes), lambda d, i: (i, shift + d, 0)),
+        ],
+        out_specs=(spec, spec),
         scratch_shapes=[pltpu.VMEM((tile_rows + 1, traces, lanes), jnp.float32)],
-        compiler_params=pltpu.CompilerParams(vmem_limit_bytes=16 * 2**20),
+        compiler_params=pltpu.CompilerParams(
+            vmem_limit_bytes=(44 if merge else 16) * 2**20
+        ),
         cost_estimate=pl.CostEstimate(
             flops=2_500_000_000 * count, bytes_accessed=2**21 * count, transcendentals=0
         ),
-    )(code, weights, arrived, *passed)
+    )(code, weights, arrived)
 
 
 def join_kernel(at, passed_ref, own_ref, out_ref):
@@ -282,7 +317,7 @@
     for k, out_ref in enumerate(out_refs):
         start = (side_ref[0] + k) % len(out_refs) * images
         for i in range(images):
-            value = own_ref[0, start + i] + rising_ref[start + i].astype(jnp.float32)
+            value = own_ref[0, start + i].astype(jnp.float32) + rising_ref[start + i].astype(jnp.float32)
             value = (value + falling_ref[start + i].astype(jnp.float32)) * gain
             out_ref[i] = value.astype(out_ref.dtype)
 
@@ -324,7 +359,6 @@
                 gathers[:, q * lanes : (q + 1) * lanes],
                 preferred_element_type=jnp.float32,
             )
-            product = product.astype(jnp.bfloat16).astype(jnp.float32)
             square = product * product if square is None else square + product * product
         for j in range(group):
             cut = cut_ref[step * count + part * group + j]
@@ -400,50 +434,58 @@
     totals = jnp.concatenate([squares, counts])
     totals = lax.psum(totals, "shot_1")[None, :]
 
-    pair = diagonal(2 * CAP)
-    arrived, code = [], []
-    for n, piece in enumerate(PIECES):
-        slots = (piece[1] - piece[0]) * CAP
-        carried = [totals] if n == 1 else []
-        sent = pack(
-            piece, home, tiles, image_slot, live.T, blocks, carried,
-            columns, quarters, tile_count,
-        )
-        if n == 1:
-            low = slots * (size + 1)
-        sent = sent.reshape((columns * quarters,) + sent.shape[2:])
-        arrived.append(lax.all_to_all(sent, PLANE, 0, 0, tiled=True))
-        code.append(codes(arrived[-1], slots, size, tile_rows))
-    totals = jnp.sum(arrived[1][:, low : low + 3].astype(jnp.float32), axis=(0, 1))
-    gain = lax.rsqrt(totals[:angles] / (depth * totals[angles:]) + 1e-06)
-
-    def stacked(n, shift, count, dtype, passed=()):
-        slots = (PIECES[n][1] - PIECES[n][0]) * CAP
-        return stack(
-            code[n], pair, arrived[n], slots, shift, count, tile_rows, traces, dtype, passed
-        )
+    pair = jnp.kron(jnp.eye(2 * CAP, dtype=jnp.bfloat16), slant_weights.T)
 
     def move(array, axis, shift):
         count = lax.axis_size(axis)
         return lax.ppermute(array, axis, [(i, (i + shift) % count) for i in range(count)])
 
-    far = stacked(0, 0, 1, jnp.bfloat16)
+    def packed(piece, **more):
+        return pack(
+            piece, home, tiles, image_slot, live.T, blocks,
+            columns, quarters, tile_count, **more,
+        )
+
+    def exchange(sent):
+        sent = sent.reshape((columns * quarters,) + sent.shape[2:])
+        return lax.all_to_all(sent, PLANE, 0, 0, tiled=True)
+
+    arrived = exchange(packed(FAR)[0])
+    near = packed((FAR[1], RING - 1), groups=2)
+    above = move(near[0], "shot_1", 1)
+    below = move(near[1], "shot_1", -1)
+    totals, pair = lax.optimization_barrier((totals, pair))
+    own_piece = packed((RING - 1, RING), carried=(totals,), moved=(above, below))
+    beside = exchange(own_piece[0])
+    near_rows = 3 * CAP * size
+    low = near_rows + CAP
+    totals = jnp.sum(beside[:, low : low + 3].astype(jnp.float32), axis=(0, 1))
+    gain = lax.rsqrt(totals[:angles] / (depth * totals[angles:]) + 1e-06)
+    far_code = codes(arrived, FAR[1] * CAP * size, tile_rows)
+
+    def stacked(shift, count):
+        return stack(
+            far_code, pair, arrived, shift, count, CAP, False,
+            tile_rows, traces, jnp.bfloat16,
+        )
+
+    far = stacked(0, 1)
     rising = [move(far[0][0], "shot_1", 1), None]
     falling = [None, move(far[1][0], "shot_1", -1)]
-    for place in ((0, 1), (0, 3)):
-        parts = stacked(*place, 2, jnp.bfloat16)
+    for n, shift in ((2, 1), (3, 3)):
+        parts = stacked(shift, 2)
         for half in range(2):
-            for chain, at, shift in ((rising, 0, 1), (falling, 1, -1)):
+            for chain, at, way in ((rising, 0, 1), (falling, 1, -1)):
                 if chain[half] is None:
                     chain[half] = parts[half][at]
                 else:
                     chain[half] = join(chain[half], parts[half], at)
-                chain[half] = move(chain[half], "shot_1", shift)
-    parts = stacked(1, 0, 2, jnp.bfloat16, rising + falling)
-    for half in (1, 0):
-        rising[half] = move(parts[half], "shot_1", 1)
-        falling[half] = move(parts[2 + half], "shot_1", -1)
-    own = stacked(1, 2, 1, jnp.float32)
+                hops = way * (2 if n == 3 else 1)
+                chain[half] = move(chain[half], "shot_1", hops)
+    own = stack(
+        codes(beside, near_rows, tile_rows), pair, beside, 0, 3,
+        (beside.shape[1] - near_rows) // 3, True, tile_rows, traces, jnp.bfloat16,
+    )
     side = lax.axis_index("grp").reshape(1)
     scale = jnp.broadcast_to(gain[:, None], (angles, LANES))
     ends = []

time: 160 us -> 247 us (1.54)
  waiting for transfers between devices: 34.3 us -> 113 us
  Pallas kernels: 48.4 us -> 53.8 us
    all_to_all x2, waiting for transfers between devices: 29.6 us -> 87.1 us  [exchange(): return lax.all_to_all(sent, PLANE, 0, 0, tiled=True)]
    ppermute x20 -> x18, waiting for transfers between devices: 4.65 us -> 25.9 us  [move(): lax.ppermute(array, axis, [(i, (i + shift) % count) for i in range(count)])]
    pallas_call x7, Pallas kernels: 31.8 us -> 40 us  [the longest x3 23.4 us: pack(): pl.pallas_call(functools.partial(pack_kernel, first, last, groups, len(ca...]
    pallas_call x6, Pallas kernels: 3.19 us -> 0.38 us  [join(): pl.pallas_call(functools.partial(join_kernel, at), out_shape=jax.ShapeDty...]
    ppermute x20 -> x18, starting transfers between devices: 36.1 us -> 34.3 us  [move(): lax.ppermute(array, axis, [(i, (i + shift) % count) for i in range(count)])]
  transfers between devices with their start and end apart: 22 -> 20, of which waited for: 5 -> 7; matrix products, arithmetic and copies ran while one was open for 4% -> 2% of each run, Pallas kernels for 22% -> 14%
where the time goes in v4:
time: 247 us; the launch traced here: 245 us
  waiting for transfers between devices  113 us (46%)
  Pallas kernels  53.8 us (22%)
  starting transfers between devices  51.7 us (21%)
  blocking collectives  17.9 us (7%)
  other arithmetic  5.86 us (2%)
  local copies, waits for them, and re-layouts  2.6 us (1%)
    all_to_all x2, waiting for transfers between devices, exchange(): return lax.all_to_all(sent, PLANE, 0, 0, tiled=True)  87.1 us
    ppermute x18, starting transfers between devices, move(): lax.ppermute(array, axis, [(i, (i + shift) % count) for i in range(count)])  34.3 us
    ppermute x18, waiting for transfers between devices, move(): lax.ppermute(array, axis, [(i, (i + shift) % count) for i in range(count)])  25.9 us
    pallas_call x3, Pallas kernels, pack(): pl.pallas_call(functools.partial(pack_kernel, first, last, groups, len(ca...  23.4 us
    psum x1, blocking collectives, work(): totals = lax.psum(totals, 'shot_1')[None, :]  17.9 us
    all_to_all x2, starting transfers between devices, exchange(): return lax.all_to_all(sent, PLANE, 0, 0, tiled=True)  17.4 us
    pallas_call x4, Pallas kernels, stack(): pl.pallas_call(functools.partial(stack_kernel, codes_each, stride, shift,...  16.6 us
    pallas_call x1, Pallas kernels, moments(): pl.pallas_call(functools.partial(moments_kernel, weights.shape[0] // angl...  12.3 us
  transfers between devices with their start and end apart: 20, of which 7 were waited for; matrix products, arithmetic and copies ran while one was open for 2% of the time, Pallas kernels for 14%

profile of v4, /device:TPU:1, one launch (start us, length us, event | category | flops | bytes accessed | tf_op | source)
XLA Modules:
  0.0 244.9 jit_solution(2111803663471416957)
XLA Ops:
  0.0 7.8 %shard_map.55 = (bf16[8,4,136,128]{3,2,1,0:T(8,128)(2,1)}, bf16[8,4,136,128]{3,2,1,0:T(8,128)(2,1)}) custom-call(s32[1]{0:T(128)} %bitcast.1.home_ref, s32[96]{0:T(128)} %bitcast.31, s32[96]{0:T(128)} %slot_ref.5, s32[64,192]{1,0:T(8,128)} %bitcast.24, bf16[96,64,512]{2,1,0:T(8,128)(2,1)} %bitcast.28), custom_call_target="tpu_custom_call" | custom-call | flops 8000000000 | bytes 10485760 | tf_op jit(solution)/shard_map/pallas_call | solution.py:197
  7.8 2.4 collective-permute-start
  10.2 4.1 %collective-permute-start.1 = (bf16[8,4,136,128]{3,2,1,0:T(8,128)(2,1)}, bf16[8,4,136,128]{3,2,1,0:T(8,128)(2,1)}, u32[]{:S(2)}, u32[]{:S(2)}) collective-permute-start(bf16[8,4,136,128]{3,2,1,0:T(8,128)(2,1)} %get-tuple-element.27), channel_id=1, source_target_pairs={{0,56},{8,0},{16,8},{24,16},{32,24},{40,32},{48,40},{56,48},{1,57}... | collective-permute-start | bytes 3342344 | tf_op jit(solution)/shard_map/ppermute | solution.py:441
  16.6 12.3 %moments.1 = f32[64,128]{1,0:T(8,128)} custom-call(s32[192]{0:T(256)} %get-tuple-element.45.cut_ref, bf16[512,256]{1,0:T(8,128)(2,1)} %copy.7.w_ref, bf16[192,32,512]{2,1,0:T(8,128)(2,1)} %in_ref.1), custom_call_target="tpu_custom_call" | custom-call | flops 10000000000 | bytes 6291456 | tf_op jit(solution)/shard_map/moments/pallas_call | solution.py:373
  29.8 17.9 %psum.7.refs_0_ = f32[1,128]{1,0:T(1,128)} all-reduce(f32[1,128]{1,0:T(1,128)S(1)} %maximum_bitcast_fusion), channel_id=1, replica_groups=mesh['shot_0'=4,'shot_1'=8,'shot_2'=2,'grp'=4] {'shot_1'}, use_global_device_ids=true, to_apply=%region_3.4 | all-reduce | flops 128 | bytes 1024 | tf_op jit(solution)/shard_map/psum | solution.py:435
  47.7 1.0 copy-done.2
  48.7 7.7 %shard_map.56 = bf16[8,4,408,128]{3,2,1,0:T(8,128)(2,1)} custom-call(s32[1]{0:T(128)} %bitcast.1.home_ref, s32[96]{0:T(128)} %bitcast.32, s32[96]{0:T(128)} %slot_ref.5, s32[64,192]{1,0:T(8,128)} %bitcast.25, bf16[96,64,512]{2,1,0:T(8,128)(2,1)} %bitcast.29, f32[1,128]{1,0:T(1,128)} %psum.7.refs_0_, bf16[8,4,136,128]{3,2,1,0:T(8,128)(2,1)} %copy-done.2, ...), custom_call_target="tpu_custom_call" | custom-call | flops 8000000000 | bytes 10485760 | tf_op jit(solution)/shard_map/pallas_call | solution.py:197
  56.5 11.2 %all-to-all-start = ((bf16[32,408,128]{2,1,0:T(8,128)(2,1)}), bf16[32,408,128]{2,1,0:T(8,128)(2,1)}, u32[]{:S(2)}, u32[]{:S(2)}) async-start(bf16[32,408,128]{2,1,0:T(8,128)(2,1)} %bitcast.23), calls=%async_computation | async-start | bytes 6684672 | tf_op jit(solution)/shard_map/all_to_all | solution.py:451
  67.6 7.9 %shard_map.58 = bf16[8,4,656,128]{3,2,1,0:T(8,128)(2,1)} custom-call(s32[1]{0:T(128)} %bitcast.1.home_ref, s32[96]{0:T(128)} %bitcast.33, s32[96]{0:T(128)} %slot_ref.5, s32[64,192]{1,0:T(8,128)} %bitcast.26, bf16[96,64,512]{2,1,0:T(8,128)(2,1)} %bitcast.30), custom_call_target="tpu_custom_call" | custom-call | flops 8000000000 | bytes 10485760 | tf_op jit(solution)/shard_map/pallas_call | solution.py:197
  75.5 32.1 %all-to-all-done.in_ref = bf16[32,408,128]{2,1,0:T(8,128)(2,1)} async-done(((bf16[32,408,128]{2,1,0:T(8,128)(2,1)}), bf16[32,408,128]{2,1,0:T(8,128)(2,1)}, u32[]{:S(2)}, u32[]{:S(2)}) %all-to-all-start) | async-done | bytes 3342368 | tf_op jit(solution)/shard_map/all_to_all | solution.py:451
  107.7 6.2 %all-to-all-start.1 = ((bf16[32,656,128]{2,1,0:T(8,128)(2,1)}), bf16[32,656,128]{2,1,0:T(8,128)(2,1)}, u32[]{:S(2)}, u32[]{:S(2)}) async-start(bf16[32,656,128]{2,1,0:T(8,128)(2,1)} %bitcast.22), calls=%async_computation.1 | async-start | bytes 10747904 | tf_op jit(solution)/shard_map/all_to_all | solution.py:451
  113.9 1.6 fusion.4
  116.4 5.8 %shard_map.57 = (bf16[1,16,64,128]{3,2,1,0:T(8,128)(2,1)S(1)}, bf16[1,16,64,128]{3,2,1,0:T(8,128)(2,1)S(1)}) custom-call(s32[768]{0:T(1024)S(1)} %reshape.54.code_ref, bf16[128,256]{1,0:T(8,128)(2,1)S(1)} %mul.79.w_ref, bf16[32,408,128]{2,1,0:T(8,128)(2,1)} %all-to-all-done.in_ref), custom_call_target="tpu_custom_call" | custom-call | flops 7500000256 | bytes 6291456 | tf_op jit(solution)/shard_map/pallas_call | solution.py:274
  122.3 54.9 %all-to-all-done.1.in_ref = bf16[32,656,128]{2,1,0:T(8,128)(2,1)} async-done(((bf16[32,656,128]{2,1,0:T(8,128)(2,1)}), bf16[32,656,128]{2,1,0:T(8,128)(2,1)}, u32[]{:S(2)}, u32[]{:S(2)}) %all-to-all-start.1) | async-done | bytes 5373984 | tf_op jit(solution)/shard_map/all_to_all | solution.py:451
  177.2 1.5 fusion.9
  178.8 2.4 shard_map.59
  181.3 4.2 %shard_map.60 = (bf16[2,16,64,128]{3,2,1,0:T(8,128)(2,1)S(1)}, bf16[2,16,64,128]{3,2,1,0:T(8,128)(2,1)S(1)}) custom-call(s32[512]{0:T(512)S(1)} %reshape.56.code_ref, bf16[128,256]{1,0:T(8,128)(2,1)S(1)} %mul.79.w_ref, bf16[32,656,128]{2,1,0:T(8,128)(2,1)} %all-to-all-done.1.in_ref), custom_call_target="tpu_custom_call" | custom-call | flops 5000000000 | bytes 4194304 | tf_op jit(solution)/shard_map/pallas_call | solution.py:274
  185.5 1.5 collective-permute-start.10
  187.1 2.8 %collective-permute-start.5 = (bf16[16,64,128]{2,1,0:T(8,128)(2,1)S(1)}, bf16[16,64,128]{2,1,0:T(8,128)(2,1)S(1)}, u32[]{:S(2)}, u32[]{:S(2)}) collective-permute-start(bf16[16,64,128]{2,1,0:T(8,128)(2,1)S(1)} %slice_bitcast_fusion.1), channel_id=1, source_target_pairs={{0,56},{8,0},{16,8},{24,16},{32,24},{40,32},{48,40},{56,48},{1,57}... | collective-permute-start | bytes 786440 | tf_op jit(solution)/shard_map/ppermute | solution.py:441
  190.2 8.9 %collective-permute-done.2.passed_ref = bf16[16,64,128]{2,1,0:T(8,128)(2,1)S(1)} collective-permute-done((bf16[16,64,128]{2,1,0:T(8,128)(2,1)S(1)}, bf16[16,64,128]{2,1,0:T(8,128)(2,1)S(1)}, u32[]{:S(2)}, u32[]{:S(2)}) %collective-permute-start.2) | collective-permute-done | bytes 262176 | tf_op jit(solution)/shard_map/ppermute | solution.py:441
  199.2 4.2 %shard_map.61 = (bf16[2,16,64,128]{3,2,1,0:T(8,128)(2,1)S(1)}, bf16[2,16,64,128]{3,2,1,0:T(8,128)(2,1)S(1)}) custom-call(s32[512]{0:T(512)S(1)} %reshape.56.code_ref, bf16[128,256]{1,0:T(8,128)(2,1)S(1)} %mul.79.w_ref, bf16[32,656,128]{2,1,0:T(8,128)(2,1)} %all-to-all-done.1.in_ref), custom_call_target="tpu_custom_call" | custom-call | flops 5000000000 | bytes 4194304 | tf_op jit(solution)/shard_map/pallas_call | solution.py:274
  203.5 1.2 collective-permute-start.11
  204.8 2.5 %collective-permute-start.6 = (bf16[16,64,128]{2,1,0:T(8,128)(2,1)S(1)}, bf16[16,64,128]{2,1,0:T(8,128)(2,1)S(1)}, u32[]{:S(2)}, u32[]{:S(2)}) collective-permute-start(bf16[16,64,128]{2,1,0:T(8,128)(2,1)S(1)} %join.8), channel_id=1, source_target_pairs={{0,48},{8,56},{16,0},{24,8},{32,16},{40,24},{48,32},{56,40},{1,49}... | collective-permute-start | bytes 786440 | tf_op jit(solution)/shard_map/ppermute | solution.py:441
  208.3 1.7 collective-permute-start.4
  210.0 3.5 %collective-permute-done.11.rising_ref = bf16[16,64,128]{2,1,0:T(8,128)(2,1)S(1)} collective-permute-done((bf16[16,64,128]{2,1,0:T(8,128)(2,1)S(1)}, bf16[16,64,128]{2,1,0:T(8,128)(2,1)S(1)}, u32[]{:S(2)}, u32[]{:S(2)}) %collective-permute-start.11) | collective-permute-done | bytes 262176 | tf_op jit(solution)/shard_map/ppermute | solution.py:441
  213.5 10.7 %collective-permute-done.14.falling_ref = bf16[16,64,128]{2,1,0:T(8,128)(2,1)S(1)} collective-permute-done((bf16[16,64,128]{2,1,0:T(8,128)(2,1)S(1)}, bf16[16,64,128]{2,1,0:T(8,128)(2,1)S(1)}, u32[]{:S(2)}, u32[]{:S(2)}) %collective-permute-start.14) | collective-permute-done | bytes 262176 | tf_op jit(solution)/shard_map/ppermute | solution.py:441
  224.3 11.0 %collective-permute-start.15 = (bf16[4,64,128]{2,1,0:T(8,128)(2,1)S(1)}, bf16[4,64,128]{2,1,0:T(8,128)(2,1)S(1)}, u32[]{:S(2)}, u32[]{:S(2)}) collective-permute-start(bf16[4,64,128]{2,1,0:T(8,128)(2,1)S(1)} %get-tuple-element.42), channel_id=1, source_target_pairs={{0,1},{1,2},{2,3},{3,0},{4,5},{5,6},{6,7},{7,4},{8,9},{9,10},{10,1... | collective-permute-start | bytes 196616 | tf_op jit(solution)/shard_map/ppermute | solution.py:441
  235.4 1.7 collective-permute-start.16
  238.7 1.3 collective-permute-start.8
  240.0 1.2 collective-permute-start.9
  241.2 1.2 collective-permute-done.7.refs_1_
  242.4 1.6 collective-permute-done.8.refs_2_
  (54 shorter events, 8.6 us)
Async XLA Ops:
  0.0 14.4 %copy-start.1 = (bf16[64,32]{0,1:T(8,128)(2,1)S(1)}, bf16[64,32]{0,1:T(8,128)(2,1)}, u32[]{:S(2)}) copy-start(bf16[64,32]{0,1:T(8,128)(2,1)} %param.6) | copy-start | bytes 12292
  0.0 15.8 %copy-start = (s32[192,64]{0,1:T(8,128)S(1)}, s32[192,64]{0,1:T(8,128)}, u32[]{:S(2)}) copy-start(s32[192,64]{0,1:T(8,128)} %param.7) | copy-start | bytes 147460
  7.8 39.9 %collective-permute-start = (bf16[8,4,136,128]{3,2,1,0:T(8,128)(2,1)}, bf16[8,4,136,128]{3,2,1,0:T(8,128)(2,1)S(1)}, u32[]{:S(2)}, u32[]{:S(2)}) collective-permute-start(bf16[8,4,136,128]{3,2,1,0:T(8,128)(2,1)} %get-tuple-element.26), channel_id=1, source_target_pairs={{0,8},{8,16},{16,24},{24,32},{32,40},{40,48},{48,56},{56,0},{1,9},... | collective-permute-start | bytes 3342344 | tf_op jit(solution)/shard_map/ppermute | solution.py:441
  10.2 37.5 %collective-permute-start.1 = (bf16[8,4,136,128]{3,2,1,0:T(8,128)(2,1)}, bf16[8,4,136,128]{3,2,1,0:T(8,128)(2,1)}, u32[]{:S(2)}, u32[]{:S(2)}) collective-permute-start(bf16[8,4,136,128]{3,2,1,0:T(8,128)(2,1)} %get-tuple-element.27), channel_id=1, source_target_pairs={{0,56},{8,0},{16,8},{24,16},{32,24},{40,32},{48,40},{56,48},{1,57}... | collective-permute-start | bytes 3342344 | tf_op jit(solution)/shard_map/ppermute | solution.py:441
  47.7 1.0 copy-start.2
  56.5 51.2 %all-to-all-start = ((bf16[32,408,128]{2,1,0:T(8,128)(2,1)}), bf16[32,408,128]{2,1,0:T(8,128)(2,1)}, u32[]{:S(2)}, u32[]{:S(2)}) async-start(bf16[32,408,128]{2,1,0:T(8,128)(2,1)} %bitcast.23), calls=%async_computation | async-start | bytes 6684672 | tf_op jit(solution)/shard_map/all_to_all | solution.py:451
  107.7 69.5 %all-to-all-start.1 = ((bf16[32,656,128]{2,1,0:T(8,128)(2,1)}), bf16[32,656,128]{2,1,0:T(8,128)(2,1)}, u32[]{:S(2)}, u32[]{:S(2)}) async-start(bf16[32,656,128]{2,1,0:T(8,128)(2,1)} %bitcast.22), calls=%async_computation.1 | async-start | bytes 10747904 | tf_op jit(solution)/shard_map/all_to_all | solution.py:451
  181.2 8.8 %collective-permute-start.12 = (bf16[16,64,128]{2,1,0:T(8,128)(2,1)S(1)}, bf16[16,64,128]{2,1,0:T(8,128)(2,1)S(1)}, u32[]{:S(2)}, u32[]{:S(2)}) collective-permute-start(bf16[16,64,128]{2,1,0:T(8,128)(2,1)S(1)} %bitcast.21), channel_id=1, source_target_pairs={{0,56},{8,0},{16,8},{24,16},{32,24},{40,32},{48,40},{56,48},{1,57}... | collective-permute-start | bytes 786440 | tf_op jit(solution)/shard_map/ppermute | solution.py:441
  185.5 17.9 %collective-permute-start.10 = (bf16[16,64,128]{2,1,0:T(8,128)(2,1)S(1)}, bf16[16,64,128]{2,1,0:T(8,128)(2,1)S(1)}, u32[]{:S(2)}, u32[]{:S(2)}) collective-permute-start(bf16[16,64,128]{2,1,0:T(8,128)(2,1)S(1)} %slice_bitcast_fusion), channel_id=1, source_target_pairs={{0,8},{8,16},{16,24},{24,32},{32,40},{40,48},{48,56},{56,0},{1,9},... | collective-permute-start | bytes 786440 | tf_op jit(solution)/shard_map/ppermute | solution.py:441
  187.0 12.0 %collective-permute-start.2 = (bf16[16,64,128]{2,1,0:T(8,128)(2,1)S(1)}, bf16[16,64,128]{2,1,0:T(8,128)(2,1)S(1)}, u32[]{:S(2)}, u32[]{:S(2)}) collective-permute-start(bf16[16,64,128]{2,1,0:T(8,128)(2,1)S(1)} %bitcast.20), channel_id=1, source_target_pairs={{0,8},{8,16},{16,24},{24,32},{32,40},{40,48},{48,56},{56,0},{1,9},... | collective-permute-start | bytes 786440 | tf_op jit(solution)/shard_map/ppermute | solution.py:441
  187.1 17.6 %collective-permute-start.5 = (bf16[16,64,128]{2,1,0:T(8,128)(2,1)S(1)}, bf16[16,64,128]{2,1,0:T(8,128)(2,1)S(1)}, u32[]{:S(2)}, u32[]{:S(2)}) collective-permute-start(bf16[16,64,128]{2,1,0:T(8,128)(2,1)S(1)} %slice_bitcast_fusion.1), channel_id=1, source_target_pairs={{0,56},{8,0},{16,8},{24,16},{32,24},{40,32},{48,40},{56,48},{1,57}... | collective-permute-start | bytes 786440 | tf_op jit(solution)/shard_map/ppermute | solution.py:441
  190.0 17.2 %collective-permute-start.13 = (bf16[16,64,128]{2,1,0:T(8,128)(2,1)S(1)}, bf16[16,64,128]{2,1,0:T(8,128)(2,1)S(1)}, u32[]{:S(2)}, u32[]{:S(2)}) collective-permute-start(bf16[16,64,128]{2,1,0:T(8,128)(2,1)S(1)} %join.10), channel_id=1, source_target_pairs={{0,56},{8,0},{16,8},{24,16},{32,24},{40,32},{48,40},{56,48},{1,57}... | collective-permute-start | bytes 786440 | tf_op jit(solution)/shard_map/ppermute | solution.py:441
  199.1 9.1 %collective-permute-start.3 = (bf16[16,64,128]{2,1,0:T(8,128)(2,1)S(1)}, bf16[16,64,128]{2,1,0:T(8,128)(2,1)S(1)}, u32[]{:S(2)}, u32[]{:S(2)}) collective-permute-start(bf16[16,64,128]{2,1,0:T(8,128)(2,1)S(1)} %join.6), channel_id=1, source_target_pairs={{0,8},{8,16},{16,24},{24,32},{32,40},{40,48},{48,56},{56,0},{1,9},... | collective-permute-start | bytes 786440 | tf_op jit(solution)/shard_map/ppermute | solution.py:441
  203.5 10.0 %collective-permute-start.11 = (bf16[16,64,128]{2,1,0:T(8,128)(2,1)S(1)}, bf16[16,64,128]{2,1,0:T(8,128)(2,1)S(1)}, u32[]{:S(2)}, u32[]{:S(2)}) collective-permute-start(bf16[16,64,128]{2,1,0:T(8,128)(2,1)S(1)} %join.9), channel_id=1, source_target_pairs={{0,16},{8,24},{16,32},{24,40},{32,48},{40,56},{48,0},{56,8},{1,17}... | collective-permute-start | bytes 786440 | tf_op jit(solution)/shard_map/ppermute | solution.py:441
  204.8 33.1 %collective-permute-start.6 = (bf16[16,64,128]{2,1,0:T(8,128)(2,1)S(1)}, bf16[16,64,128]{2,1,0:T(8,128)(2,1)S(1)}, u32[]{:S(2)}, u32[]{:S(2)}) collective-permute-start(bf16[16,64,128]{2,1,0:T(8,128)(2,1)S(1)} %join.8), channel_id=1, source_target_pairs={{0,48},{8,56},{16,0},{24,8},{32,16},{40,24},{48,32},{56,40},{1,49}... | collective-permute-start | bytes 786440 | tf_op jit(solution)/shard_map/ppermute | solution.py:441
  207.4 16.8 %collective-permute-start.14 = (bf16[16,64,128]{2,1,0:T(8,128)(2,1)S(1)}, bf16[16,64,128]{2,1,0:T(8,128)(2,1)S(1)}, u32[]{:S(2)}, u32[]{:S(2)}) collective-permute-start(bf16[16,64,128]{2,1,0:T(8,128)(2,1)S(1)} %join.11), channel_id=1, source_target_pairs={{0,48},{8,56},{16,0},{24,8},{32,16},{40,24},{48,32},{56,40},{1,49}... | collective-permute-start | bytes 786440 | tf_op jit(solution)/shard_map/ppermute | solution.py:441
  208.3 29.6 %collective-permute-start.4 = (bf16[16,64,128]{2,1,0:T(8,128)(2,1)S(1)}, bf16[16,64,128]{2,1,0:T(8,128)(2,1)S(1)}, u32[]{:S(2)}, u32[]{:S(2)}) collective-permute-start(bf16[16,64,128]{2,1,0:T(8,128)(2,1)S(1)} %join.7), channel_id=1, source_target_pairs={{0,16},{8,24},{16,32},{24,40},{32,48},{40,56},{48,0},{56,8},{1,17}... | collective-permute-start | bytes 786440 | tf_op jit(solution)/shard_map/ppermute | solution.py:441
  224.3 15.7 %collective-permute-start.15 = (bf16[4,64,128]{2,1,0:T(8,128)(2,1)S(1)}, bf16[4,64,128]{2,1,0:T(8,128)(2,1)S(1)}, u32[]{:S(2)}, u32[]{:S(2)}) collective-permute-start(bf16[4,64,128]{2,1,0:T(8,128)(2,1)S(1)} %get-tuple-element.42), channel_id=1, source_target_pairs={{0,1},{1,2},{2,3},{3,0},{4,5},{5,6},{6,7},{7,4},{8,9},{9,10},{10,1... | collective-permute-start | bytes 196616 | tf_op jit(solution)/shard_map/ppermute | solution.py:441
  235.4 5.8 %collective-permute-start.16 = (bf16[4,64,128]{2,1,0:T(8,128)(2,1)S(1)}, bf16[4,64,128]{2,1,0:T(8,128)(2,1)S(1)}, u32[]{:S(2)}, u32[]{:S(2)}) collective-permute-start(bf16[4,64,128]{2,1,0:T(8,128)(2,1)S(1)} %get-tuple-element.43), channel_id=1, source_target_pairs={{0,2},{1,3},{2,0},{3,1},{4,6},{5,7},{6,4},{7,5},{8,10},{9,11},{10,... | collective-permute-start | bytes 196616 | tf_op jit(solution)/shard_map/ppermute | solution.py:441
  237.1 4.2 %collective-permute-start.17 = (bf16[4,64,128]{2,1,0:T(8,128)(2,1)S(1)}, bf16[4,64,128]{2,1,0:T(8,128)(2,1)S(1)}, u32[]{:S(2)}, u32[]{:S(2)}) collective-permute-start(bf16[4,64,128]{2,1,0:T(8,128)(2,1)S(1)} %get-tuple-element.44), channel_id=1, source_target_pairs={{0,3},{1,0},{2,1},{3,2},{4,7},{5,4},{6,5},{7,6},{8,11},{9,8},{10,9... | collective-permute-start | bytes 196616 | tf_op jit(solution)/shard_map/ppermute | solution.py:441
  238.0 4.4 %collective-permute-start.7 = (bf16[4,64,128]{2,1,0:T(8,128)(2,1)S(1)}, bf16[4,64,128]{2,1,0:T(8,128)(2,1)S(1)}, u32[]{:S(2)}, u32[]{:S(2)}) collective-permute-start(bf16[4,64,128]{2,1,0:T(8,128)(2,1)S(1)} %get-tuple-element.34), channel_id=1, source_target_pairs={{0,1},{1,2},{2,3},{3,0},{4,5},{5,6},{6,7},{7,4},{8,9},{9,10},{10,1... | collective-permute-start | bytes 196616 | tf_op jit(solution)/shard_map/ppermute | solution.py:441
  238.7 5.3 %collective-permute-start.8 = (bf16[4,64,128]{2,1,0:T(8,128)(2,1)S(1)}, bf16[4,64,128]{2,1,0:T(8,128)(2,1)S(1)}, u32[]{:S(2)}, u32[]{:S(2)}) collective-permute-start(bf16[4,64,128]{2,1,0:T(8,128)(2,1)S(1)} %get-tuple-element.35), channel_id=1, source_target_pairs={{0,2},{1,3},{2,0},{3,1},{4,6},{5,7},{6,4},{7,5},{8,10},{9,11},{10,... | collective-permute-start | bytes 196616 | tf_op jit(solution)/shard_map/ppermute | solution.py:441
  240.0 4.0 %collective-permute-start.9 = (bf16[4,64,128]{2,1,0:T(8,128)(2,1)S(1)}, bf16[4,64,128]{2,1,0:T(8,128)(2,1)S(1)}, u32[]{:S(2)}, u32[]{:S(2)}) collective-permute-start(bf16[4,64,128]{2,1,0:T(8,128)(2,1)S(1)} %get-tuple-element.36), channel_id=1, source_target_pairs={{0,3},{1,0},{2,1},{3,2},{4,7},{5,4},{6,5},{7,6},{8,11},{9,8},{10,9... | collective-permute-start | bytes 196616 | tf_op jit(solution)/shard_map/ppermute | solution.py:441

commit v5 on v4

--- a/solution.py
+++ b/solution.py
@@ -245,8 +245,7 @@
             for half, cut in enumerate(((code >> 7) & 127, code & 127)):
                 low = half * angles
                 angle = product[j * traces + low : j * traces + low + angles]
-                angle = jnp.where(row < cut, angle, 0.0).astype(jnp.bfloat16)
-                acc[label, low : low + angles, :] += angle.astype(jnp.float32)
+                acc[label, low : low + angles, :] += jnp.where(row < cut, angle, 0.0)
 
     @pl.when(ends)
     def _():
@@ -311,32 +310,37 @@
     )(passed, own)
 
 
-def total_kernel(side_ref, gain_ref, own_ref, rising_ref, falling_ref, *out_refs):
+def total_kernel(side_ref, gain_ref, *refs):
+    own, rising, falling, out_refs = refs[0:2], refs[2:4], refs[4:6], refs[6:]
     images = out_refs[0].shape[0]
     gain = gain_ref[...]
+    angles = gain.shape[0]
     for k, out_ref in enumerate(out_refs):
         start = (side_ref[0] + k) % len(out_refs) * images
         for i in range(images):
-            value = own_ref[0, start + i].astype(jnp.float32) + rising_ref[start + i].astype(jnp.float32)
-            value = (value + falling_ref[start + i].astype(jnp.float32)) * gain
-            out_ref[i] = value.astype(out_ref.dtype)
+            for half in range(2):
+                value = own[half][0, start + i].astype(jnp.float32)
+                value = value + rising[half][start + i].astype(jnp.float32)
+                value = (value + falling[half][start + i].astype(jnp.float32)) * gain
+                low = half * angles
+                out_ref[i, low : low + angles] = value.astype(out_ref.dtype)
 
 
 def total(side, gain, own, rising, falling, quarters):
     vmem = pl.BlockSpec(memory_space=pltpu.VMEM)
-    rows, angles, lanes = rising.shape
-    shape = jax.ShapeDtypeStruct((rows // quarters, angles, lanes), jnp.bfloat16)
+    rows, angles, lanes = rising[0].shape
+    shape = jax.ShapeDtypeStruct((rows // quarters, 2 * angles, lanes), jnp.bfloat16)
     return pl.pallas_call(
         total_kernel,
         out_shape=(shape,) * quarters,
-        in_specs=[pl.BlockSpec(memory_space=pltpu.SMEM), vmem, vmem, vmem, vmem],
+        in_specs=[pl.BlockSpec(memory_space=pltpu.SMEM)] + [vmem] * 7,
         out_specs=(vmem,) * quarters,
         compiler_params=pltpu.CompilerParams(vmem_limit_bytes=8 * 2**20),
         cost_estimate=pl.CostEstimate(
-            flops=500_000_000, bytes_accessed=2**20, transcendentals=0
+            flops=500_000_000, bytes_accessed=2 * 2**20, transcendentals=0
         ),
         name="total",
-    )(side, gain, own, rising, falling)
+    )(side, gain, *own, *rising, *falling)
 
 
 def moments_kernel(group, cut_ref, w_ref, in_ref, out_ref):
@@ -390,27 +394,25 @@
 
 
 def finish_kernel(side_ref, *refs):
-    out_ref = refs[-1]
-    halves = (refs[: len(refs) // 2], refs[len(refs) // 2 : -1])
-    angles, lanes = refs[0].shape[1:]
-    for half, parts in enumerate(halves):
-        for k, ref in enumerate(parts):
-            quarter = (side_ref[0] - k + len(parts)) % len(parts)
-            start = pl.multiple_of(quarter * lanes, lanes)
-            out_ref[:, half * angles : (half + 1) * angles, pl.ds(start, lanes)] = ref[...]
-
-
-def finish(side, first, second):
-    images, angles, lanes = first[0].shape
+    out_ref, parts = refs[-1], refs[:-1]
+    lanes = parts[0].shape[2]
+    for k, ref in enumerate(parts):
+        quarter = (side_ref[0] - k + len(parts)) % len(parts)
+        start = pl.multiple_of(quarter * lanes, lanes)
+        out_ref[:, :, pl.ds(start, lanes)] = ref[...]
+
+
+def finish(side, parts):
+    images, traces, lanes = parts[0].shape
     vmem = pl.BlockSpec(memory_space=pltpu.VMEM)
     return pl.pallas_call(
         finish_kernel,
-        out_shape=jax.ShapeDtypeStruct((images, 2 * angles, len(first) * lanes), jnp.bfloat16),
-        in_specs=[pl.BlockSpec(memory_space=pltpu.SMEM)] + [vmem] * (2 * len(first)),
+        out_shape=jax.ShapeDtypeStruct((images, traces, len(parts) * lanes), jnp.bfloat16),
+        in_specs=[pl.BlockSpec(memory_space=pltpu.SMEM)] + [vmem] * len(parts),
         out_specs=vmem,
         compiler_params=pltpu.CompilerParams(vmem_limit_bytes=8 * 2**20),
         name="finish",
-    )(side, *first, *second)
+    )(side, *parts)
 
 
 def work(offsets, slant_weights, live, block_tile, image_slot):
@@ -488,11 +490,9 @@
     )
     side = lax.axis_index("grp").reshape(1)
     scale = jnp.broadcast_to(gain[:, None], (angles, LANES))
-    ends = []
-    for half in range(2):
-        parts = total(side, scale, own[half], rising[half], falling[half], quarters)
-        ends.append([parts[0]] + [move(parts[k], "grp", k) for k in range(1, quarters)])
-    return finish(side, *ends)
+    parts = total(side, scale, own, rising, falling, quarters)
+    ends = [parts[0]] + [move(parts[k], "grp", k) for k in range(1, quarters)]
+    return finish(side, ends)
 
 
 def solution(mesh):

time: 247 us -> 237 us (0.960)
  starting transfers between devices: 51.7 us -> 43 us
    ppermute x18 -> x15, starting transfers between devices: 34.3 us -> 25.5 us  [move(): lax.ppermute(array, axis, [(i, (i + shift) % count) for i in range(count)])]
    ppermute x18 -> x15, waiting for transfers between devices: 25.9 us -> 24.3 us  [move(): lax.ppermute(array, axis, [(i, (i + shift) % count) for i in range(count)])]
  transfers between devices with their start and end apart: 20 -> 17, of which waited for: 7 -> 9; matrix products, arithmetic and copies ran while one was open for 2% -> 2% of each run, Pallas kernels for 14% -> 14%
where the time goes in v5:
time: 237 us; the launch traced here: 235 us
  waiting for transfers between devices  113 us (48%)
  Pallas kernels  52.7 us (22%)
  starting transfers between devices  43 us (18%)
  blocking collectives  17.9 us (8%)
  other arithmetic  5.82 us (2%)
  local copies, waits for them, and re-layouts  2.59 us (1%)
    all_to_all x2, waiting for transfers between devices, exchange(): return lax.all_to_all(sent, PLANE, 0, 0, tiled=True)  88.3 us
    ppermute x15, starting transfers between devices, move(): lax.ppermute(array, axis, [(i, (i + shift) % count) for i in range(count)])  25.5 us
    ppermute x15, waiting for transfers between devices, move(): lax.ppermute(array, axis, [(i, (i + shift) % count) for i in range(count)])  24.3 us
    pallas_call x3, Pallas kernels, pack(): pl.pallas_call(functools.partial(pack_kernel, first, last, groups, len(ca...  23.4 us
    psum x1, blocking collectives, work(): totals = lax.psum(totals, 'shot_1')[None, :]  17.9 us
    all_to_all x2, starting transfers between devices, exchange(): return lax.all_to_all(sent, PLANE, 0, 0, tiled=True)  17.4 us
    pallas_call x4, Pallas kernels, stack(): pl.pallas_call(functools.partial(stack_kernel, codes_each, stride, shift,...  15.5 us
    pallas_call x1, Pallas kernels, moments(): pl.pallas_call(functools.partial(moments_kernel, weights.shape[0] // angl...  12.3 us
  transfers between devices with their start and end apart: 17, of which 9 were waited for; matrix products, arithmetic and copies ran while one was open for 2% of the time, Pallas kernels for 14%

profile of v5, /device:TPU:1, one launch (start us, length us, event | category | flops | bytes accessed | tf_op | source)
XLA Modules:
  0.0 234.8 jit_solution(14659169653705122767)
XLA Ops:
  0.0 7.8 %shard_map.55 = (bf16[8,4,136,128]{3,2,1,0:T(8,128)(2,1)}, bf16[8,4,136,128]{3,2,1,0:T(8,128)(2,1)}) custom-call(s32[1]{0:T(128)} %bitcast.1.home_ref, s32[96]{0:T(128)} %bitcast.31, s32[96]{0:T(128)} %slot_ref.5, s32[64,192]{1,0:T(8,128)} %bitcast.24, bf16[96,64,512]{2,1,0:T(8,128)(2,1)} %bitcast.28), custom_call_target="tpu_custom_call" | custom-call | flops 8000000000 | bytes 10485760 | tf_op jit(solution)/shard_map/pallas_call | solution.py:197
  7.8 2.4 %collective-permute-start = (bf16[8,4,136,128]{3,2,1,0:T(8,128)(2,1)}, bf16[8,4,136,128]{3,2,1,0:T(8,128)(2,1)S(1)}, u32[]{:S(2)}, u32[]{:S(2)}) collective-permute-start(bf16[8,4,136,128]{3,2,1,0:T(8,128)(2,1)} %get-tuple-element.22), channel_id=1, source_target_pairs={{0,8},{8,16},{16,24},{24,32},{32,40},{40,48},{48,56},{56,0},{1,9},... | collective-permute-start | bytes 3342344 | tf_op jit(solution)/shard_map/ppermute | solution.py:443
  10.2 4.1 %collective-permute-start.1 = (bf16[8,4,136,128]{3,2,1,0:T(8,128)(2,1)}, bf16[8,4,136,128]{3,2,1,0:T(8,128)(2,1)}, u32[]{:S(2)}, u32[]{:S(2)}) collective-permute-start(bf16[8,4,136,128]{3,2,1,0:T(8,128)(2,1)} %get-tuple-element.23), channel_id=1, source_target_pairs={{0,56},{8,0},{16,8},{24,16},{32,24},{40,32},{48,40},{56,48},{1,57}... | collective-permute-start | bytes 3342344 | tf_op jit(solution)/shard_map/ppermute | solution.py:443
  16.5 12.3 %moments.1 = f32[64,128]{1,0:T(8,128)} custom-call(s32[192]{0:T(256)} %get-tuple-element.37.cut_ref, bf16[512,256]{1,0:T(8,128)(2,1)} %copy.7.w_ref, bf16[192,32,512]{2,1,0:T(8,128)(2,1)} %in_ref.1), custom_call_target="tpu_custom_call" | custom-call | flops 10000000000 | bytes 6291456 | tf_op jit(solution)/shard_map/moments/pallas_call | solution.py:377
  28.8 0.9 reduce_sum.55
  29.8 17.9 %psum.7.refs_0_ = f32[1,128]{1,0:T(1,128)} all-reduce(f32[1,128]{1,0:T(1,128)S(1)} %maximum_bitcast_fusion), channel_id=1, replica_groups=mesh['shot_0'=4,'shot_1'=8,'shot_2'=2,'grp'=4] {'shot_1'}, use_global_device_ids=true, to_apply=%region_3.4 | all-reduce | flops 128 | bytes 1024 | tf_op jit(solution)/shard_map/psum | solution.py:437
  47.7 1.0 copy-done.2
  48.7 7.7 %shard_map.56 = bf16[8,4,408,128]{3,2,1,0:T(8,128)(2,1)} custom-call(s32[1]{0:T(128)} %bitcast.1.home_ref, s32[96]{0:T(128)} %bitcast.32, s32[96]{0:T(128)} %slot_ref.5, s32[64,192]{1,0:T(8,128)} %bitcast.25, bf16[96,64,512]{2,1,0:T(8,128)(2,1)} %bitcast.29, f32[1,128]{1,0:T(1,128)} %psum.7.refs_0_, bf16[8,4,136,128]{3,2,1,0:T(8,128)(2,1)} %copy-done.2, ...), custom_call_target="tpu_custom_call" | custom-call | flops 8000000000 | bytes 10485760 | tf_op jit(solution)/shard_map/pallas_call | solution.py:197
  56.4 11.2 %all-to-all-start = ((bf16[32,408,128]{2,1,0:T(8,128)(2,1)}), bf16[32,408,128]{2,1,0:T(8,128)(2,1)}, u32[]{:S(2)}, u32[]{:S(2)}) async-start(bf16[32,408,128]{2,1,0:T(8,128)(2,1)} %bitcast.23), calls=%async_computation | async-start | bytes 6684672 | tf_op jit(solution)/shard_map/all_to_all | solution.py:453
  67.7 7.8 %shard_map.58 = bf16[8,4,656,128]{3,2,1,0:T(8,128)(2,1)} custom-call(s32[1]{0:T(128)} %bitcast.1.home_ref, s32[96]{0:T(128)} %bitcast.33, s32[96]{0:T(128)} %slot_ref.5, s32[64,192]{1,0:T(8,128)} %bitcast.26, bf16[96,64,512]{2,1,0:T(8,128)(2,1)} %bitcast.30), custom_call_target="tpu_custom_call" | custom-call | flops 8000000000 | bytes 10485760 | tf_op jit(solution)/shard_map/pallas_call | solution.py:197
  75.5 32.2 %all-to-all-done.in_ref = bf16[32,408,128]{2,1,0:T(8,128)(2,1)} async-done(((bf16[32,408,128]{2,1,0:T(8,128)(2,1)}), bf16[32,408,128]{2,1,0:T(8,128)(2,1)}, u32[]{:S(2)}, u32[]{:S(2)}) %all-to-all-start) | async-done | bytes 3342368 | tf_op jit(solution)/shard_map/all_to_all | solution.py:453
  107.7 6.2 %all-to-all-start.1 = ((bf16[32,656,128]{2,1,0:T(8,128)(2,1)}), bf16[32,656,128]{2,1,0:T(8,128)(2,1)}, u32[]{:S(2)}, u32[]{:S(2)}) async-start(bf16[32,656,128]{2,1,0:T(8,128)(2,1)} %bitcast.22), calls=%async_computation.1 | async-start | bytes 10747904 | tf_op jit(solution)/shard_map/all_to_all | solution.py:453
  113.9 1.6 fusion.4
  115.6 5.5 %shard_map.57 = (bf16[1,16,64,128]{3,2,1,0:T(8,128)(2,1)S(1)}, bf16[1,16,64,128]{3,2,1,0:T(8,128)(2,1)S(1)}) custom-call(s32[768]{0:T(1024)S(1)} %reshape.54.code_ref, bf16[128,256]{1,0:T(8,128)(2,1)S(1)} %mul.79.w_ref, bf16[32,408,128]{2,1,0:T(8,128)(2,1)} %all-to-all-done.in_ref), custom_call_target="tpu_custom_call" | custom-call | flops 7500000256 | bytes 6291456 | tf_op jit(solution)/shard_map/pallas_call | solution.py:273
  121.0 56.2 %all-to-all-done.1.in_ref = bf16[32,656,128]{2,1,0:T(8,128)(2,1)} async-done(((bf16[32,656,128]{2,1,0:T(8,128)(2,1)}), bf16[32,656,128]{2,1,0:T(8,128)(2,1)}, u32[]{:S(2)}, u32[]{:S(2)}) %all-to-all-start.1) | async-done | bytes 5373984 | tf_op jit(solution)/shard_map/all_to_all | solution.py:453
  177.2 1.5 fusion.9
  178.8 2.2 shard_map.59
  181.1 1.5 collective-permute-start.2
  182.6 3.9 %shard_map.60 = (bf16[2,16,64,128]{3,2,1,0:T(8,128)(2,1)S(1)}, bf16[2,16,64,128]{3,2,1,0:T(8,128)(2,1)S(1)}) custom-call(s32[512]{0:T(512)S(1)} %reshape.56.code_ref, bf16[128,256]{1,0:T(8,128)(2,1)S(1)} %mul.79.w_ref, bf16[32,656,128]{2,1,0:T(8,128)(2,1)} %all-to-all-done.1.in_ref), custom_call_target="tpu_custom_call" | custom-call | flops 5000000000 | bytes 4194304 | tf_op jit(solution)/shard_map/pallas_call | solution.py:273
  186.5 1.4 collective-permute-start.7
  188.2 2.8 %collective-permute-start.10 = (bf16[16,64,128]{2,1,0:T(8,128)(2,1)S(1)}, bf16[16,64,128]{2,1,0:T(8,128)(2,1)S(1)}, u32[]{:S(2)}, u32[]{:S(2)}) collective-permute-start(bf16[16,64,128]{2,1,0:T(8,128)(2,1)S(1)} %join.10), channel_id=1, source_target_pairs={{0,56},{8,0},{16,8},{24,16},{32,24},{40,32},{48,40},{56,48},{1,57}... | collective-permute-start | bytes 786440 | tf_op jit(solution)/shard_map/ppermute | solution.py:443
  191.2 3.9 %shard_map.61 = (bf16[2,16,64,128]{3,2,1,0:T(8,128)(2,1)S(1)}, bf16[2,16,64,128]{3,2,1,0:T(8,128)(2,1)S(1)}) custom-call(s32[512]{0:T(512)S(1)} %reshape.56.code_ref, bf16[128,256]{1,0:T(8,128)(2,1)S(1)} %mul.79.w_ref, bf16[32,656,128]{2,1,0:T(8,128)(2,1)} %all-to-all-done.1.in_ref), custom_call_target="tpu_custom_call" | custom-call | flops 5000000000 | bytes 4194304 | tf_op jit(solution)/shard_map/pallas_call | solution.py:273
  195.2 1.2 collective-permute-start.8
  196.5 1.3 collective-permute-start.6
  198.7 2.0 collective-permute-start.11
  201.3 0.9 convert_reduce_fusion
  202.2 6.6 %collective-permute-done.8.refs_4_ = bf16[16,64,128]{2,1,0:T(8,128)(2,1)S(1)} collective-permute-done((bf16[16,64,128]{2,1,0:T(8,128)(2,1)S(1)}, bf16[16,64,128]{2,1,0:T(8,128)(2,1)S(1)}, u32[]{:S(2)}, u32[]{:S(2)}) %collective-permute-start.8) | collective-permute-done | bytes 262176 | tf_op jit(solution)/shard_map/ppermute | solution.py:443
  208.8 12.5 %collective-permute-done.11.refs_5_ = bf16[16,64,128]{2,1,0:T(8,128)(2,1)S(1)} collective-permute-done((bf16[16,64,128]{2,1,0:T(8,128)(2,1)S(1)}, bf16[16,64,128]{2,1,0:T(8,128)(2,1)S(1)}, u32[]{:S(2)}, u32[]{:S(2)}) %collective-permute-start.11) | collective-permute-done | bytes 262176 | tf_op jit(solution)/shard_map/ppermute | solution.py:443
  221.7 5.7 %collective-permute-start.12 = (bf16[4,128,128]{2,1,0:T(8,128)(2,1)S(1)}, bf16[4,128,128]{2,1,0:T(8,128)(2,1)S(1)}, u32[]{:S(2)}, u32[]{:S(2)}) collective-permute-start(bf16[4,128,128]{2,1,0:T(8,128)(2,1)S(1)} %get-tuple-element.34), channel_id=1, source_target_pairs={{0,1},{1,2},{2,3},{3,0},{4,5},{5,6},{6,7},{7,4},{8,9},{9,10},{10,1... | collective-permute-start | bytes 393224 | tf_op jit(solution)/shard_map/ppermute | solution.py:443
  227.3 2.5 %collective-permute-start.14 = (bf16[4,128,128]{2,1,0:T(8,128)(2,1)S(1)}, bf16[4,128,128]{2,1,0:T(8,128)(2,1)S(1)}, u32[]{:S(2)}, u32[]{:S(2)}) collective-permute-start(bf16[4,128,128]{2,1,0:T(8,128)(2,1)S(1)} %get-tuple-element.36), channel_id=1, source_target_pairs={{0,3},{1,0},{2,1},{3,2},{4,7},{5,4},{6,5},{7,6},{8,11},{9,8},{10,9... | collective-permute-start | bytes 393224 | tf_op jit(solution)/shard_map/ppermute | solution.py:443
  230.2 3.5 %collective-permute-done.13.refs_2_ = bf16[4,128,128]{2,1,0:T(8,128)(2,1)S(1)} collective-permute-done((bf16[4,128,128]{2,1,0:T(8,128)(2,1)S(1)}, bf16[4,128,128]{2,1,0:T(8,128)(2,1)S(1)}, u32[]{:S(2)}, u32[]{:S(2)}) %collective-permute-start.13) | collective-permute-done | bytes 131104 | tf_op jit(solution)/shard_map/ppermute | solution.py:443
  233.9 0.9 finish.1
  (47 shorter events, 5.5 us)
Async XLA Ops:
  0.0 14.4 %copy-start.1 = (bf16[64,32]{0,1:T(8,128)(2,1)S(1)}, bf16[64,32]{0,1:T(8,128)(2,1)}, u32[]{:S(2)}) copy-start(bf16[64,32]{0,1:T(8,128)(2,1)} %param.6) | copy-start | bytes 12292
  0.0 15.8 %copy-start = (s32[192,64]{0,1:T(8,128)S(1)}, s32[192,64]{0,1:T(8,128)}, u32[]{:S(2)}) copy-start(s32[192,64]{0,1:T(8,128)} %param.7) | copy-start | bytes 147460
  7.8 39.9 %collective-permute-start = (bf16[8,4,136,128]{3,2,1,0:T(8,128)(2,1)}, bf16[8,4,136,128]{3,2,1,0:T(8,128)(2,1)S(1)}, u32[]{:S(2)}, u32[]{:S(2)}) collective-permute-start(bf16[8,4,136,128]{3,2,1,0:T(8,128)(2,1)} %get-tuple-element.22), channel_id=1, source_target_pairs={{0,8},{8,16},{16,24},{24,32},{32,40},{40,48},{48,56},{56,0},{1,9},... | collective-permute-start | bytes 3342344 | tf_op jit(solution)/shard_map/ppermute | solution.py:443
  10.2 37.5 %collective-permute-start.1 = (bf16[8,4,136,128]{3,2,1,0:T(8,128)(2,1)}, bf16[8,4,136,128]{3,2,1,0:T(8,128)(2,1)}, u32[]{:S(2)}, u32[]{:S(2)}) collective-permute-start(bf16[8,4,136,128]{3,2,1,0:T(8,128)(2,1)} %get-tuple-element.23), channel_id=1, source_target_pairs={{0,56},{8,0},{16,8},{24,16},{32,24},{40,32},{48,40},{56,48},{1,57}... | collective-permute-start | bytes 3342344 | tf_op jit(solution)/shard_map/ppermute | solution.py:443
  47.7 1.0 copy-start.2
  56.4 51.2 %all-to-all-start = ((bf16[32,408,128]{2,1,0:T(8,128)(2,1)}), bf16[32,408,128]{2,1,0:T(8,128)(2,1)}, u32[]{:S(2)}, u32[]{:S(2)}) async-start(bf16[32,408,128]{2,1,0:T(8,128)(2,1)} %bitcast.23), calls=%async_computation | async-start | bytes 6684672 | tf_op jit(solution)/shard_map/all_to_all | solution.py:453
  107.7 69.5 %all-to-all-start.1 = ((bf16[32,656,128]{2,1,0:T(8,128)(2,1)}), bf16[32,656,128]{2,1,0:T(8,128)(2,1)}, u32[]{:S(2)}, u32[]{:S(2)}) async-start(bf16[32,656,128]{2,1,0:T(8,128)(2,1)} %bitcast.22), calls=%async_computation.1 | async-start | bytes 10747904 | tf_op jit(solution)/shard_map/all_to_all | solution.py:453
  181.1 7.1 %collective-permute-start.9 = (bf16[16,64,128]{2,1,0:T(8,128)(2,1)S(1)}, bf16[16,64,128]{2,1,0:T(8,128)(2,1)S(1)}, u32[]{:S(2)}, u32[]{:S(2)}) collective-permute-start(bf16[16,64,128]{2,1,0:T(8,128)(2,1)S(1)} %bitcast.21), channel_id=1, source_target_pairs={{0,56},{8,0},{16,8},{24,16},{32,24},{40,32},{48,40},{56,48},{1,57}... | collective-permute-start | bytes 786440 | tf_op jit(solution)/shard_map/ppermute | solution.py:443
  181.1 9.9 %collective-permute-start.2 = (bf16[16,64,128]{2,1,0:T(8,128)(2,1)S(1)}, bf16[16,64,128]{2,1,0:T(8,128)(2,1)S(1)}, u32[]{:S(2)}, u32[]{:S(2)}) collective-permute-start(bf16[16,64,128]{2,1,0:T(8,128)(2,1)S(1)} %bitcast.20), channel_id=1, source_target_pairs={{0,8},{8,16},{16,24},{24,32},{32,40},{40,48},{48,56},{56,0},{1,9},... | collective-permute-start | bytes 786440 | tf_op jit(solution)/shard_map/ppermute | solution.py:443
  186.5 8.6 %collective-permute-start.7 = (bf16[16,64,128]{2,1,0:T(8,128)(2,1)S(1)}, bf16[16,64,128]{2,1,0:T(8,128)(2,1)S(1)}, u32[]{:S(2)}, u32[]{:S(2)}) collective-permute-start(bf16[16,64,128]{2,1,0:T(8,128)(2,1)S(1)} %slice_bitcast_fusion), channel_id=1, source_target_pairs={{0,56},{8,0},{16,8},{24,16},{32,24},{40,32},{48,40},{56,48},{1,57}... | collective-permute-start | bytes 786440 | tf_op jit(solution)/shard_map/ppermute | solution.py:443
  187.9 8.5 %collective-permute-start.5 = (bf16[16,64,128]{2,1,0:T(8,128)(2,1)S(1)}, bf16[16,64,128]{2,1,0:T(8,128)(2,1)S(1)}, u32[]{:S(2)}, u32[]{:S(2)}) collective-permute-start(bf16[16,64,128]{2,1,0:T(8,128)(2,1)S(1)} %slice_bitcast_fusion.1), channel_id=1, source_target_pairs={{0,8},{8,16},{16,24},{24,32},{32,40},{40,48},{48,56},{56,0},{1,9},... | collective-permute-start | bytes 786440 | tf_op jit(solution)/shard_map/ppermute | solution.py:443
  188.2 10.4 %collective-permute-start.10 = (bf16[16,64,128]{2,1,0:T(8,128)(2,1)S(1)}, bf16[16,64,128]{2,1,0:T(8,128)(2,1)S(1)}, u32[]{:S(2)}, u32[]{:S(2)}) collective-permute-start(bf16[16,64,128]{2,1,0:T(8,128)(2,1)S(1)} %join.10), channel_id=1, source_target_pairs={{0,56},{8,0},{16,8},{24,16},{32,24},{40,32},{48,40},{56,48},{1,57}... | collective-permute-start | bytes 786440 | tf_op jit(solution)/shard_map/ppermute | solution.py:443
  191.1 9.9 %collective-permute-start.3 = (bf16[16,64,128]{2,1,0:T(8,128)(2,1)S(1)}, bf16[16,64,128]{2,1,0:T(8,128)(2,1)S(1)}, u32[]{:S(2)}, u32[]{:S(2)}) collective-permute-start(bf16[16,64,128]{2,1,0:T(8,128)(2,1)S(1)} %join.6), channel_id=1, source_target_pairs={{0,8},{8,16},{16,24},{24,32},{32,40},{40,48},{48,56},{56,0},{1,9},... | collective-permute-start | bytes 786440 | tf_op jit(solution)/shard_map/ppermute | solution.py:443
  195.2 13.6 %collective-permute-start.8 = (bf16[16,64,128]{2,1,0:T(8,128)(2,1)S(1)}, bf16[16,64,128]{2,1,0:T(8,128)(2,1)S(1)}, u32[]{:S(2)}, u32[]{:S(2)}) collective-permute-start(bf16[16,64,128]{2,1,0:T(8,128)(2,1)S(1)} %join.9), channel_id=1, source_target_pairs={{0,48},{8,56},{16,0},{24,8},{32,16},{40,24},{48,32},{56,40},{1,49}... | collective-permute-start | bytes 786440 | tf_op jit(solution)/shard_map/ppermute | solution.py:443
  196.5 12.3 %collective-permute-start.6 = (bf16[16,64,128]{2,1,0:T(8,128)(2,1)S(1)}, bf16[16,64,128]{2,1,0:T(8,128)(2,1)S(1)}, u32[]{:S(2)}, u32[]{:S(2)}) collective-permute-start(bf16[16,64,128]{2,1,0:T(8,128)(2,1)S(1)} %join.8), channel_id=1, source_target_pairs={{0,16},{8,24},{16,32},{24,40},{32,48},{40,56},{48,0},{56,8},{1,17}... | collective-permute-start | bytes 786440 | tf_op jit(solution)/shard_map/ppermute | solution.py:443
  198.7 22.7 %collective-permute-start.11 = (bf16[16,64,128]{2,1,0:T(8,128)(2,1)S(1)}, bf16[16,64,128]{2,1,0:T(8,128)(2,1)S(1)}, u32[]{:S(2)}, u32[]{:S(2)}) collective-permute-start(bf16[16,64,128]{2,1,0:T(8,128)(2,1)S(1)} %join.11), channel_id=1, source_target_pairs={{0,48},{8,56},{16,0},{24,8},{32,16},{40,24},{48,32},{56,40},{1,49}... | collective-permute-start | bytes 786440 | tf_op jit(solution)/shard_map/ppermute | solution.py:443
  201.0 20.3 %collective-permute-start.4 = (bf16[16,64,128]{2,1,0:T(8,128)(2,1)S(1)}, bf16[16,64,128]{2,1,0:T(8,128)(2,1)S(1)}, u32[]{:S(2)}, u32[]{:S(2)}) collective-permute-start(bf16[16,64,128]{2,1,0:T(8,128)(2,1)S(1)} %join.7), channel_id=1, source_target_pairs={{0,16},{8,24},{16,32},{24,40},{32,48},{40,56},{48,0},{56,8},{1,17}... | collective-permute-start | bytes 786440 | tf_op jit(solution)/shard_map/ppermute | solution.py:443
  221.7 8.5 %collective-permute-start.12 = (bf16[4,128,128]{2,1,0:T(8,128)(2,1)S(1)}, bf16[4,128,128]{2,1,0:T(8,128)(2,1)S(1)}, u32[]{:S(2)}, u32[]{:S(2)}) collective-permute-start(bf16[4,128,128]{2,1,0:T(8,128)(2,1)S(1)} %get-tuple-element.34), channel_id=1, source_target_pairs={{0,1},{1,2},{2,3},{3,0},{4,5},{5,6},{6,7},{7,4},{8,9},{9,10},{10,1... | collective-permute-start | bytes 393224 | tf_op jit(solution)/shard_map/ppermute | solution.py:443
  227.3 6.3 %collective-permute-start.13 = (bf16[4,128,128]{2,1,0:T(8,128)(2,1)S(1)}, bf16[4,128,128]{2,1,0:T(8,128)(2,1)S(1)}, u32[]{:S(2)}, u32[]{:S(2)}) collective-permute-start(bf16[4,128,128]{2,1,0:T(8,128)(2,1)S(1)} %get-tuple-element.35), channel_id=1, source_target_pairs={{0,2},{1,3},{2,0},{3,1},{4,6},{5,7},{6,4},{7,5},{8,10},{9,11},{10,... | collective-permute-start | bytes 393224 | tf_op jit(solution)/shard_map/ppermute | solution.py:443
  227.3 6.5 %collective-permute-start.14 = (bf16[4,128,128]{2,1,0:T(8,128)(2,1)S(1)}, bf16[4,128,128]{2,1,0:T(8,128)(2,1)S(1)}, u32[]{:S(2)}, u32[]{:S(2)}) collective-permute-start(bf16[4,128,128]{2,1,0:T(8,128)(2,1)S(1)} %get-tuple-element.36), channel_id=1, source_target_pairs={{0,3},{1,0},{2,1},{3,2},{4,7},{5,4},{6,5},{7,6},{8,11},{9,8},{10,9... | collective-permute-start | bytes 393224 | tf_op jit(solution)/shard_map/ppermute | solution.py:443

commit v6 on v5

--- a/solution.py
+++ b/solution.py
@@ -310,13 +310,13 @@
     )(passed, own)
 
 
-def total_kernel(side_ref, gain_ref, *refs):
+def total_kernel(ahead, quarters, side_ref, gain_ref, *refs):
     own, rising, falling, out_refs = refs[0:2], refs[2:4], refs[4:6], refs[6:]
     images = out_refs[0].shape[0]
     gain = gain_ref[...]
     angles = gain.shape[0]
-    for k, out_ref in enumerate(out_refs):
-        start = (side_ref[0] + k) % len(out_refs) * images
+    for k, out_ref in zip(ahead, out_refs):
+        start = (side_ref[0] + k) % quarters * images
         for i in range(images):
             for half in range(2):
                 value = own[half][0, start + i].astype(jnp.float32)
@@ -326,15 +326,15 @@
                 out_ref[i, low : low + angles] = value.astype(out_ref.dtype)
 
 
-def total(side, gain, own, rising, falling, quarters):
+def total(ahead, side, gain, own, rising, falling, quarters):
     vmem = pl.BlockSpec(memory_space=pltpu.VMEM)
     rows, angles, lanes = rising[0].shape
     shape = jax.ShapeDtypeStruct((rows // quarters, 2 * angles, lanes), jnp.bfloat16)
     return pl.pallas_call(
-        total_kernel,
-        out_shape=(shape,) * quarters,
+        functools.partial(total_kernel, ahead, quarters),
+        out_shape=(shape,) * len(ahead),
         in_specs=[pl.BlockSpec(memory_space=pltpu.SMEM)] + [vmem] * 7,
-        out_specs=(vmem,) * quarters,
+        out_specs=(vmem,) * len(ahead),
         compiler_params=pltpu.CompilerParams(vmem_limit_bytes=8 * 2**20),
         cost_estimate=pl.CostEstimate(
             flops=500_000_000, bytes_accessed=2 * 2**20, transcendentals=0
@@ -490,8 +490,10 @@
     )
     side = lax.axis_index("grp").reshape(1)
     scale = jnp.broadcast_to(gain[:, None], (angles, LANES))
-    parts = total(side, scale, own, rising, falling, quarters)
-    ends = [parts[0]] + [move(parts[k], "grp", k) for k in range(1, quarters)]
+    away = tuple(range(1, quarters))
+    parts = total(away, side, scale, own, rising, falling, quarters)
+    ends = list(total((0,), side, scale, own, rising, falling, quarters))
+    ends += [move(part, "grp", k) for k, part in zip(away, parts)]
     return finish(side, ends)
 
 

time: 237 us -> 237 us (level)
  no operation moved by 1% of the time
where the time goes in v6:
time: 237 us; the launch traced here: 235 us
  waiting for transfers between devices  113 us (48%)
  Pallas kernels  52.7 us (22%)
  starting transfers between devices  42.9 us (18%)
  blocking collectives  17.9 us (8%)
  other arithmetic  5.82 us (2%)
  local copies, waits for them, and re-layouts  2.59 us (1%)
    all_to_all x2, waiting for transfers between devices, exchange(): return lax.all_to_all(sent, PLANE, 0, 0, tiled=True)  88.3 us
    ppermute x15, starting transfers between devices, move(): lax.ppermute(array, axis, [(i, (i + shift) % count) for i in range(count)])  25.5 us
    ppermute x15, waiting for transfers between devices, move(): lax.ppermute(array, axis, [(i, (i + shift) % count) for i in range(count)])  24.2 us
    pallas_call x3, Pallas kernels, pack(): pl.pallas_call(functools.partial(pack_kernel, first, last, groups, len(ca...  23.4 us
    psum x1, blocking collectives, work(): totals = lax.psum(totals, 'shot_1')[None, :]  17.9 us
    all_to_all x2, starting transfers between devices, exchange(): return lax.all_to_all(sent, PLANE, 0, 0, tiled=True)  17.4 us
    pallas_call x4, Pallas kernels, stack(): pl.pallas_call(functools.partial(stack_kernel, codes_each, stride, shift,...  15.5 us
    pallas_call x1, Pallas kernels, moments(): pl.pallas_call(functools.partial(moments_kernel, weights.shape[0] // angl...  12.3 us
  transfers between devices with their start and end apart: 17, of which 9 were waited for; matrix products, arithmetic and copies ran while one was open for 2% of the time, Pallas kernels for 14%

profile of v6, /device:TPU:1, one launch (start us, length us, event | category | flops | bytes accessed | tf_op | source)
XLA Modules:
  0.0 234.7 jit_solution(12622336735131727297)
XLA Ops:
  0.0 7.8 %shard_map.55 = (bf16[8,4,136,128]{3,2,1,0:T(8,128)(2,1)}, bf16[8,4,136,128]{3,2,1,0:T(8,128)(2,1)}) custom-call(s32[1]{0:T(128)} %bitcast.1.home_ref, s32[96]{0:T(128)} %bitcast.31, s32[96]{0:T(128)} %slot_ref.5, s32[64,192]{1,0:T(8,128)} %bitcast.24, bf16[96,64,512]{2,1,0:T(8,128)(2,1)} %bitcast.28), custom_call_target="tpu_custom_call" | custom-call | flops 8000000000 | bytes 10485760 | tf_op jit(solution)/shard_map/pallas_call | solution.py:197
  7.8 2.4 %collective-permute-start = (bf16[8,4,136,128]{3,2,1,0:T(8,128)(2,1)}, bf16[8,4,136,128]{3,2,1,0:T(8,128)(2,1)S(1)}, u32[]{:S(2)}, u32[]{:S(2)}) collective-permute-start(bf16[8,4,136,128]{3,2,1,0:T(8,128)(2,1)} %get-tuple-element.21), channel_id=1, source_target_pairs={{0,8},{8,16},{16,24},{24,32},{32,40},{40,48},{48,56},{56,0},{1,9},... | collective-permute-start | bytes 3342344 | tf_op jit(solution)/shard_map/ppermute | solution.py:443
  10.2 4.1 %collective-permute-start.1 = (bf16[8,4,136,128]{3,2,1,0:T(8,128)(2,1)}, bf16[8,4,136,128]{3,2,1,0:T(8,128)(2,1)}, u32[]{:S(2)}, u32[]{:S(2)}) collective-permute-start(bf16[8,4,136,128]{3,2,1,0:T(8,128)(2,1)} %get-tuple-element.22), channel_id=1, source_target_pairs={{0,56},{8,0},{16,8},{24,16},{32,24},{40,32},{48,40},{56,48},{1,57}... | collective-permute-start | bytes 3342344 | tf_op jit(solution)/shard_map/ppermute | solution.py:443
  16.5 12.3 %moments.1 = f32[64,128]{1,0:T(8,128)} custom-call(s32[192]{0:T(256)} %get-tuple-element.35.cut_ref, bf16[512,256]{1,0:T(8,128)(2,1)} %copy.7.w_ref, bf16[192,32,512]{2,1,0:T(8,128)(2,1)} %in_ref.1), custom_call_target="tpu_custom_call" | custom-call | flops 10000000000 | bytes 6291456 | tf_op jit(solution)/shard_map/moments/pallas_call | solution.py:377
  29.8 17.9 %psum.7.refs_0_ = f32[1,128]{1,0:T(1,128)} all-reduce(f32[1,128]{1,0:T(1,128)S(1)} %maximum_bitcast_fusion), channel_id=1, replica_groups=mesh['shot_0'=4,'shot_1'=8,'shot_2'=2,'grp'=4] {'shot_1'}, use_global_device_ids=true, to_apply=%region_3.4 | all-reduce | flops 128 | bytes 1024 | tf_op jit(solution)/shard_map/psum | solution.py:437
  47.7 1.0 copy-done.2
  48.7 7.7 %shard_map.56 = bf16[8,4,408,128]{3,2,1,0:T(8,128)(2,1)} custom-call(s32[1]{0:T(128)} %bitcast.1.home_ref, s32[96]{0:T(128)} %bitcast.32, s32[96]{0:T(128)} %slot_ref.5, s32[64,192]{1,0:T(8,128)} %bitcast.25, bf16[96,64,512]{2,1,0:T(8,128)(2,1)} %bitcast.29, f32[1,128]{1,0:T(1,128)} %psum.7.refs_0_, bf16[8,4,136,128]{3,2,1,0:T(8,128)(2,1)} %copy-done.2, ...), custom_call_target="tpu_custom_call" | custom-call | flops 8000000000 | bytes 10485760 | tf_op jit(solution)/shard_map/pallas_call | solution.py:197
  56.4 11.2 %all-to-all-start = ((bf16[32,408,128]{2,1,0:T(8,128)(2,1)}), bf16[32,408,128]{2,1,0:T(8,128)(2,1)}, u32[]{:S(2)}, u32[]{:S(2)}) async-start(bf16[32,408,128]{2,1,0:T(8,128)(2,1)} %bitcast.23), calls=%async_computation | async-start | bytes 6684672 | tf_op jit(solution)/shard_map/all_to_all | solution.py:453
  67.7 7.8 %shard_map.58 = bf16[8,4,656,128]{3,2,1,0:T(8,128)(2,1)} custom-call(s32[1]{0:T(128)} %bitcast.1.home_ref, s32[96]{0:T(128)} %bitcast.33, s32[96]{0:T(128)} %slot_ref.5, s32[64,192]{1,0:T(8,128)} %bitcast.26, bf16[96,64,512]{2,1,0:T(8,128)(2,1)} %bitcast.30), custom_call_target="tpu_custom_call" | custom-call | flops 8000000000 | bytes 10485760 | tf_op jit(solution)/shard_map/pallas_call | solution.py:197
  75.5 32.2 %all-to-all-done.in_ref = bf16[32,408,128]{2,1,0:T(8,128)(2,1)} async-done(((bf16[32,408,128]{2,1,0:T(8,128)(2,1)}), bf16[32,408,128]{2,1,0:T(8,128)(2,1)}, u32[]{:S(2)}, u32[]{:S(2)}) %all-to-all-start) | async-done | bytes 3342368 | tf_op jit(solution)/shard_map/all_to_all | solution.py:453
  107.7 6.2 %all-to-all-start.1 = ((bf16[32,656,128]{2,1,0:T(8,128)(2,1)}), bf16[32,656,128]{2,1,0:T(8,128)(2,1)}, u32[]{:S(2)}, u32[]{:S(2)}) async-start(bf16[32,656,128]{2,1,0:T(8,128)(2,1)} %bitcast.22), calls=%async_computation.1 | async-start | bytes 10747904 | tf_op jit(solution)/shard_map/all_to_all | solution.py:453
  113.9 1.6 fusion.4
  115.6 5.5 %shard_map.57 = (bf16[1,16,64,128]{3,2,1,0:T(8,128)(2,1)S(1)}, bf16[1,16,64,128]{3,2,1,0:T(8,128)(2,1)S(1)}) custom-call(s32[768]{0:T(1024)S(1)} %reshape.54.code_ref, bf16[128,256]{1,0:T(8,128)(2,1)S(1)} %mul.79.w_ref, bf16[32,408,128]{2,1,0:T(8,128)(2,1)} %all-to-all-done.in_ref), custom_call_target="tpu_custom_call" | custom-call | flops 7500000256 | bytes 6291456 | tf_op jit(solution)/shard_map/pallas_call | solution.py:273
  121.0 56.2 %all-to-all-done.1.in_ref = bf16[32,656,128]{2,1,0:T(8,128)(2,1)} async-done(((bf16[32,656,128]{2,1,0:T(8,128)(2,1)}), bf16[32,656,128]{2,1,0:T(8,128)(2,1)}, u32[]{:S(2)}, u32[]{:S(2)}) %all-to-all-start.1) | async-done | bytes 5373984 | tf_op jit(solution)/shard_map/all_to_all | solution.py:453
  177.2 1.5 fusion.9
  178.8 2.2 shard_map.59
  181.2 1.5 collective-permute-start.2
  182.6 3.9 %shard_map.60 = (bf16[2,16,64,128]{3,2,1,0:T(8,128)(2,1)S(1)}, bf16[2,16,64,128]{3,2,1,0:T(8,128)(2,1)S(1)}) custom-call(s32[512]{0:T(512)S(1)} %reshape.56.code_ref, bf16[128,256]{1,0:T(8,128)(2,1)S(1)} %mul.79.w_ref, bf16[32,656,128]{2,1,0:T(8,128)(2,1)} %all-to-all-done.1.in_ref), custom_call_target="tpu_custom_call" | custom-call | flops 5000000000 | bytes 4194304 | tf_op jit(solution)/shard_map/pallas_call | solution.py:273
  186.5 1.4 collective-permute-start.7
  188.2 2.8 %collective-permute-start.10 = (bf16[16,64,128]{2,1,0:T(8,128)(2,1)S(1)}, bf16[16,64,128]{2,1,0:T(8,128)(2,1)S(1)}, u32[]{:S(2)}, u32[]{:S(2)}) collective-permute-start(bf16[16,64,128]{2,1,0:T(8,128)(2,1)S(1)} %join.10), channel_id=1, source_target_pairs={{0,56},{8,0},{16,8},{24,16},{32,24},{40,32},{48,40},{56,48},{1,57}... | collective-permute-start | bytes 786440 | tf_op jit(solution)/shard_map/ppermute | solution.py:443
  191.2 3.9 %shard_map.61 = (bf16[2,16,64,128]{3,2,1,0:T(8,128)(2,1)S(1)}, bf16[2,16,64,128]{3,2,1,0:T(8,128)(2,1)S(1)}) custom-call(s32[512]{0:T(512)S(1)} %reshape.56.code_ref, bf16[128,256]{1,0:T(8,128)(2,1)S(1)} %mul.79.w_ref, bf16[32,656,128]{2,1,0:T(8,128)(2,1)} %all-to-all-done.1.in_ref), custom_call_target="tpu_custom_call" | custom-call | flops 5000000000 | bytes 4194304 | tf_op jit(solution)/shard_map/pallas_call | solution.py:273
  195.2 1.2 collective-permute-start.8
  196.5 1.3 collective-permute-start.6
  197.8 0.9 collective-permute-done.10.passed_ref
  198.7 1.9 collective-permute-start.11
  201.3 0.9 convert_reduce_fusion
  202.3 6.6 %collective-permute-done.8.refs_4_ = bf16[16,64,128]{2,1,0:T(8,128)(2,1)S(1)} collective-permute-done((bf16[16,64,128]{2,1,0:T(8,128)(2,1)S(1)}, bf16[16,64,128]{2,1,0:T(8,128)(2,1)S(1)}, u32[]{:S(2)}, u32[]{:S(2)}) %collective-permute-start.8) | collective-permute-done | bytes 262176 | tf_op jit(solution)/shard_map/ppermute | solution.py:443
  208.8 12.5 %collective-permute-done.11.refs_5_ = bf16[16,64,128]{2,1,0:T(8,128)(2,1)S(1)} collective-permute-done((bf16[16,64,128]{2,1,0:T(8,128)(2,1)S(1)}, bf16[16,64,128]{2,1,0:T(8,128)(2,1)S(1)}, u32[]{:S(2)}, u32[]{:S(2)}) %collective-permute-start.11) | collective-permute-done | bytes 262176 | tf_op jit(solution)/shard_map/ppermute | solution.py:443
  221.6 5.7 %collective-permute-start.12 = (bf16[4,128,128]{2,1,0:T(8,128)(2,1)S(1)}, bf16[4,128,128]{2,1,0:T(8,128)(2,1)S(1)}, u32[]{:S(2)}, u32[]{:S(2)}) collective-permute-start(bf16[4,128,128]{2,1,0:T(8,128)(2,1)S(1)} %get-tuple-element.32), channel_id=1, source_target_pairs={{0,1},{1,2},{2,3},{3,0},{4,5},{5,6},{6,7},{7,4},{8,9},{9,10},{10,1... | collective-permute-start | bytes 393224 | tf_op jit(solution)/shard_map/ppermute | solution.py:443
  227.3 2.5 %collective-permute-start.14 = (bf16[4,128,128]{2,1,0:T(8,128)(2,1)S(1)}, bf16[4,128,128]{2,1,0:T(8,128)(2,1)S(1)}, u32[]{:S(2)}, u32[]{:S(2)}) collective-permute-start(bf16[4,128,128]{2,1,0:T(8,128)(2,1)S(1)} %get-tuple-element.34), channel_id=1, source_target_pairs={{0,3},{1,0},{2,1},{3,2},{4,7},{5,4},{6,5},{7,6},{8,11},{9,8},{10,9... | collective-permute-start | bytes 393224 | tf_op jit(solution)/shard_map/ppermute | solution.py:443
  230.1 3.5 %collective-permute-done.13.refs_2_ = bf16[4,128,128]{2,1,0:T(8,128)(2,1)S(1)} collective-permute-done((bf16[4,128,128]{2,1,0:T(8,128)(2,1)S(1)}, bf16[4,128,128]{2,1,0:T(8,128)(2,1)S(1)}, u32[]{:S(2)}, u32[]{:S(2)}) %collective-permute-start.13) | collective-permute-done | bytes 131104 | tf_op jit(solution)/shard_map/ppermute | solution.py:443
  233.8 0.9 finish.1
  (48 shorter events, 5.6 us)
Async XLA Ops:
  0.0 14.4 %copy-start.1 = (bf16[64,32]{0,1:T(8,128)(2,1)S(1)}, bf16[64,32]{0,1:T(8,128)(2,1)}, u32[]{:S(2)}) copy-start(bf16[64,32]{0,1:T(8,128)(2,1)} %param.6) | copy-start | bytes 12292
  0.0 15.8 %copy-start = (s32[192,64]{0,1:T(8,128)S(1)}, s32[192,64]{0,1:T(8,128)}, u32[]{:S(2)}) copy-start(s32[192,64]{0,1:T(8,128)} %param.7) | copy-start | bytes 147460
  7.8 39.9 %collective-permute-start = (bf16[8,4,136,128]{3,2,1,0:T(8,128)(2,1)}, bf16[8,4,136,128]{3,2,1,0:T(8,128)(2,1)S(1)}, u32[]{:S(2)}, u32[]{:S(2)}) collective-permute-start(bf16[8,4,136,128]{3,2,1,0:T(8,128)(2,1)} %get-tuple-element.21), channel_id=1, source_target_pairs={{0,8},{8,16},{16,24},{24,32},{32,40},{40,48},{48,56},{56,0},{1,9},... | collective-permute-start | bytes 3342344 | tf_op jit(solution)/shard_map/ppermute | solution.py:443
  10.2 37.5 %collective-permute-start.1 = (bf16[8,4,136,128]{3,2,1,0:T(8,128)(2,1)}, bf16[8,4,136,128]{3,2,1,0:T(8,128)(2,1)}, u32[]{:S(2)}, u32[]{:S(2)}) collective-permute-start(bf16[8,4,136,128]{3,2,1,0:T(8,128)(2,1)} %get-tuple-element.22), channel_id=1, source_target_pairs={{0,56},{8,0},{16,8},{24,16},{32,24},{40,32},{48,40},{56,48},{1,57}... | collective-permute-start | bytes 3342344 | tf_op jit(solution)/shard_map/ppermute | solution.py:443
  47.7 1.0 copy-start.2
  56.4 51.2 %all-to-all-start = ((bf16[32,408,128]{2,1,0:T(8,128)(2,1)}), bf16[32,408,128]{2,1,0:T(8,128)(2,1)}, u32[]{:S(2)}, u32[]{:S(2)}) async-start(bf16[32,408,128]{2,1,0:T(8,128)(2,1)} %bitcast.23), calls=%async_computation | async-start | bytes 6684672 | tf_op jit(solution)/shard_map/all_to_all | solution.py:453
  107.7 69.5 %all-to-all-start.1 = ((bf16[32,656,128]{2,1,0:T(8,128)(2,1)}), bf16[32,656,128]{2,1,0:T(8,128)(2,1)}, u32[]{:S(2)}, u32[]{:S(2)}) async-start(bf16[32,656,128]{2,1,0:T(8,128)(2,1)} %bitcast.22), calls=%async_computation.1 | async-start | bytes 10747904 | tf_op jit(solution)/shard_map/all_to_all | solution.py:453
  181.1 7.1 %collective-permute-start.9 = (bf16[16,64,128]{2,1,0:T(8,128)(2,1)S(1)}, bf16[16,64,128]{2,1,0:T(8,128)(2,1)S(1)}, u32[]{:S(2)}, u32[]{:S(2)}) collective-permute-start(bf16[16,64,128]{2,1,0:T(8,128)(2,1)S(1)} %bitcast.21), channel_id=1, source_target_pairs={{0,56},{8,0},{16,8},{24,16},{32,24},{40,32},{48,40},{56,48},{1,57}... | collective-permute-start | bytes 786440 | tf_op jit(solution)/shard_map/ppermute | solution.py:443
  181.2 9.9 %collective-permute-start.2 = (bf16[16,64,128]{2,1,0:T(8,128)(2,1)S(1)}, bf16[16,64,128]{2,1,0:T(8,128)(2,1)S(1)}, u32[]{:S(2)}, u32[]{:S(2)}) collective-permute-start(bf16[16,64,128]{2,1,0:T(8,128)(2,1)S(1)} %bitcast.20), channel_id=1, source_target_pairs={{0,8},{8,16},{16,24},{24,32},{32,40},{40,48},{48,56},{56,0},{1,9},... | collective-permute-start | bytes 786440 | tf_op jit(solution)/shard_map/ppermute | solution.py:443
  186.5 8.6 %collective-permute-start.7 = (bf16[16,64,128]{2,1,0:T(8,128)(2,1)S(1)}, bf16[16,64,128]{2,1,0:T(8,128)(2,1)S(1)}, u32[]{:S(2)}, u32[]{:S(2)}) collective-permute-start(bf16[16,64,128]{2,1,0:T(8,128)(2,1)S(1)} %slice_bitcast_fusion), channel_id=1, source_target_pairs={{0,56},{8,0},{16,8},{24,16},{32,24},{40,32},{48,40},{56,48},{1,57}... | collective-permute-start | bytes 786440 | tf_op jit(solution)/shard_map/ppermute | solution.py:443
  187.9 8.5 %collective-permute-start.5 = (bf16[16,64,128]{2,1,0:T(8,128)(2,1)S(1)}, bf16[16,64,128]{2,1,0:T(8,128)(2,1)S(1)}, u32[]{:S(2)}, u32[]{:S(2)}) collective-permute-start(bf16[16,64,128]{2,1,0:T(8,128)(2,1)S(1)} %slice_bitcast_fusion.1), channel_id=1, source_target_pairs={{0,8},{8,16},{16,24},{24,32},{32,40},{40,48},{48,56},{56,0},{1,9},... | collective-permute-start | bytes 786440 | tf_op jit(solution)/shard_map/ppermute | solution.py:443
  188.2 10.4 %collective-permute-start.10 = (bf16[16,64,128]{2,1,0:T(8,128)(2,1)S(1)}, bf16[16,64,128]{2,1,0:T(8,128)(2,1)S(1)}, u32[]{:S(2)}, u32[]{:S(2)}) collective-permute-start(bf16[16,64,128]{2,1,0:T(8,128)(2,1)S(1)} %join.10), channel_id=1, source_target_pairs={{0,56},{8,0},{16,8},{24,16},{32,24},{40,32},{48,40},{56,48},{1,57}... | collective-permute-start | bytes 786440 | tf_op jit(solution)/shard_map/ppermute | solution.py:443
  191.1 9.9 %collective-permute-start.3 = (bf16[16,64,128]{2,1,0:T(8,128)(2,1)S(1)}, bf16[16,64,128]{2,1,0:T(8,128)(2,1)S(1)}, u32[]{:S(2)}, u32[]{:S(2)}) collective-permute-start(bf16[16,64,128]{2,1,0:T(8,128)(2,1)S(1)} %join.6), channel_id=1, source_target_pairs={{0,8},{8,16},{16,24},{24,32},{32,40},{40,48},{48,56},{56,0},{1,9},... | collective-permute-start | bytes 786440 | tf_op jit(solution)/shard_map/ppermute | solution.py:443
  195.2 13.7 %collective-permute-start.8 = (bf16[16,64,128]{2,1,0:T(8,128)(2,1)S(1)}, bf16[16,64,128]{2,1,0:T(8,128)(2,1)S(1)}, u32[]{:S(2)}, u32[]{:S(2)}) collective-permute-start(bf16[16,64,128]{2,1,0:T(8,128)(2,1)S(1)} %join.9), channel_id=1, source_target_pairs={{0,48},{8,56},{16,0},{24,8},{32,16},{40,24},{48,32},{56,40},{1,49}... | collective-permute-start | bytes 786440 | tf_op jit(solution)/shard_map/ppermute | solution.py:443
  196.5 12.3 %collective-permute-start.6 = (bf16[16,64,128]{2,1,0:T(8,128)(2,1)S(1)}, bf16[16,64,128]{2,1,0:T(8,128)(2,1)S(1)}, u32[]{:S(2)}, u32[]{:S(2)}) collective-permute-start(bf16[16,64,128]{2,1,0:T(8,128)(2,1)S(1)} %join.8), channel_id=1, source_target_pairs={{0,16},{8,24},{16,32},{24,40},{32,48},{40,56},{48,0},{56,8},{1,17}... | collective-permute-start | bytes 786440 | tf_op jit(solution)/shard_map/ppermute | solution.py:443
  198.7 22.6 %collective-permute-start.11 = (bf16[16,64,128]{2,1,0:T(8,128)(2,1)S(1)}, bf16[16,64,128]{2,1,0:T(8,128)(2,1)S(1)}, u32[]{:S(2)}, u32[]{:S(2)}) collective-permute-start(bf16[16,64,128]{2,1,0:T(8,128)(2,1)S(1)} %join.11), channel_id=1, source_target_pairs={{0,48},{8,56},{16,0},{24,8},{32,16},{40,24},{48,32},{56,40},{1,49}... | collective-permute-start | bytes 786440 | tf_op jit(solution)/shard_map/ppermute | solution.py:443
  201.0 20.3 %collective-permute-start.4 = (bf16[16,64,128]{2,1,0:T(8,128)(2,1)S(1)}, bf16[16,64,128]{2,1,0:T(8,128)(2,1)S(1)}, u32[]{:S(2)}, u32[]{:S(2)}) collective-permute-start(bf16[16,64,128]{2,1,0:T(8,128)(2,1)S(1)} %join.7), channel_id=1, source_target_pairs={{0,16},{8,24},{16,32},{24,40},{32,48},{40,56},{48,0},{56,8},{1,17}... | collective-permute-start | bytes 786440 | tf_op jit(solution)/shard_map/ppermute | solution.py:443
  221.6 8.5 %collective-permute-start.12 = (bf16[4,128,128]{2,1,0:T(8,128)(2,1)S(1)}, bf16[4,128,128]{2,1,0:T(8,128)(2,1)S(1)}, u32[]{:S(2)}, u32[]{:S(2)}) collective-permute-start(bf16[4,128,128]{2,1,0:T(8,128)(2,1)S(1)} %get-tuple-element.32), channel_id=1, source_target_pairs={{0,1},{1,2},{2,3},{3,0},{4,5},{5,6},{6,7},{7,4},{8,9},{9,10},{10,1... | collective-permute-start | bytes 393224 | tf_op jit(solution)/shard_map/ppermute | solution.py:443
  227.3 6.2 %collective-permute-start.13 = (bf16[4,128,128]{2,1,0:T(8,128)(2,1)S(1)}, bf16[4,128,128]{2,1,0:T(8,128)(2,1)S(1)}, u32[]{:S(2)}, u32[]{:S(2)}) collective-permute-start(bf16[4,128,128]{2,1,0:T(8,128)(2,1)S(1)} %get-tuple-element.33), channel_id=1, source_target_pairs={{0,2},{1,3},{2,0},{3,1},{4,6},{5,7},{6,4},{7,5},{8,10},{9,11},{10,... | collective-permute-start | bytes 393224 | tf_op jit(solution)/shard_map/ppermute | solution.py:443
  227.3 6.5 %collective-permute-start.14 = (bf16[4,128,128]{2,1,0:T(8,128)(2,1)S(1)}, bf16[4,128,128]{2,1,0:T(8,128)(2,1)S(1)}, u32[]{:S(2)}, u32[]{:S(2)}) collective-permute-start(bf16[4,128,128]{2,1,0:T(8,128)(2,1)S(1)} %get-tuple-element.34), channel_id=1, source_target_pairs={{0,3},{1,0},{2,1},{3,2},{4,7},{5,4},{6,5},{7,6},{8,11},{9,8},{10,9... | collective-permute-start | bytes 393224 | tf_op jit(solution)/shard_map/ppermute | solution.py:443
